TPU v7x, 8 devices: a whole 2x2x1 slice. The times are simulated.
8 devices in a mesh: dp: 1 (over z), tp: 8 (over y, x, core).
Axes of the slice: x: 2, y: 2, z: 1, core: 2. Of those that a mesh axis runs over, the one named last changes fastest.
Arguments:
- x_in: bfloat16 [1, 2048, 2560], P('dp', 'tp')
- x_mid: bfloat16 [1, 2048, 2560], P('dp', 'tp')
- d_out: bfloat16 [1, 2048, 2560], P('dp', 'tp')
- q_saved: bfloat16 [1, 2048, 32, 80], P('dp', None, 'tp')
- k_saved: bfloat16 [1, 2048, 32, 80], P('dp', None, 'tp')
- v_saved: bfloat16 [1, 2048, 32, 80], P('dp', None, 'tp')
- z_saved: bfloat16 [1, 2048, 10240], P('dp', None, 'tp')
- ln1_gain: float32 [2560], replicated
- ln1_bias: float32 [2560], replicated
- ln2_gain: float32 [2560], replicated
- ln2_bias: float32 [2560], replicated
- w_qkv: bfloat16 [3, 2560, 32, 80], P(None, None, 'tp')
- w_proj: bfloat16 [32, 80, 2560], P('tp')
- w_fc1: bfloat16 [2560, 10240], P(None, 'tp')
- w_fc2: bfloat16 [10240, 2560], P('tp')
Outputs:
- output 1: bfloat16 [1, 2048, 2560], P('dp', 'tp')
- output 2: float32 [3, 2560, 32, 80], P('dp', None, 'tp')
- output 3: float32 [3, 32, 80], P('dp', 'tp')
- output 4: float32 [32, 80, 2560], P(('dp', 'tp'))
- output 5: float32 [2560, 10240], P('dp', 'tp')
- output 6: float32 [10240], P(('dp', 'tp'))
- output 7: float32 [10240, 2560], P(('dp', 'tp'))
- output 8: float32 [6, 2560], P('dp')
All inputs are finite; a program needn't handle non-finite values.
Results may differ from a plain program's by a relative error of at most 0.0110037.
Values are sent between devices in bfloat16 or wider.
A program may use at most 1 GiB of HBM per device.

v0:
```python
import jax
import jax.numpy as jnp
from jax import lax
from jax.sharding import PartitionSpec as P

LN_EPS = 1e-5
GELU_COEF = 0.044715
GELU_SCALE = 0.7978845608028654


def layer_norm_fwd(token_rows, norm_gain, norm_bias):
    rows_f32 = token_rows.astype(jnp.float32)
    centered = rows_f32 - jnp.mean(rows_f32, axis=-1, keepdims=True)
    inv_std = lax.rsqrt(jnp.mean(centered * centered, axis=-1, keepdims=True) + LN_EPS)
    x_hat = centered * inv_std
    return x_hat, inv_std, (x_hat * norm_gain + norm_bias).astype(jnp.bfloat16)


def layer_norm_bwd(grad_norm, x_hat, inv_std, norm_gain):
    grad_hat = grad_norm * norm_gain
    centered_grad = grad_hat - jnp.mean(grad_hat, axis=-1, keepdims=True)
    return inv_std * (centered_grad - x_hat * jnp.mean(grad_hat * x_hat, axis=-1, keepdims=True))


def gelu_parts(pre_act):
    tanh_val = jnp.tanh(GELU_SCALE * (pre_act + GELU_COEF * pre_act * pre_act * pre_act))
    act_value = 0.5 * pre_act * (1.0 + tanh_val)
    act_slope = 0.5 * (1.0 + tanh_val) + 0.5 * pre_act * (1.0 - tanh_val * tanh_val) * GELU_SCALE * (1.0 + 3.0 * GELU_COEF * pre_act * pre_act)
    return act_value, act_slope


def attention_grads(q_heads, k_heads, v_heads, grad_ctx):
    seq_len = q_heads.shape[1]
    score_scale = q_heads.shape[-1] ** -0.5
    scores = jnp.einsum('bqhe,bkhe->bhqk', q_heads, k_heads, preferred_element_type=jnp.float32) * score_scale
    row_ids = lax.broadcasted_iota(jnp.int32, (seq_len, seq_len), 0)
    col_ids = lax.broadcasted_iota(jnp.int32, (seq_len, seq_len), 1)
    scores = jnp.where(row_ids >= col_ids, scores, -1e30)
    attn_probs = jax.nn.softmax(scores, axis=-1)
    probs_low = attn_probs.astype(jnp.bfloat16)
    context = jnp.einsum('bhqk,bkhe->bqhe', probs_low, v_heads, preferred_element_type=jnp.float32).astype(jnp.bfloat16)
    grad_probs = jnp.einsum('bqhe,bkhe->bhqk', grad_ctx, v_heads, preferred_element_type=jnp.float32)
    grad_scores = (attn_probs * (grad_probs - jnp.sum(grad_probs * attn_probs, axis=-1, keepdims=True)) * score_scale).astype(jnp.bfloat16)
    grad_q = jnp.einsum('bhqk,bkhe->bqhe', grad_scores, k_heads, preferred_element_type=jnp.float32).astype(jnp.bfloat16)
    grad_k = jnp.einsum('bhqk,bqhe->bkhe', grad_scores, q_heads, preferred_element_type=jnp.float32).astype(jnp.bfloat16)
    grad_v = jnp.einsum('bhqk,bqhe->bkhe', probs_low, grad_ctx, preferred_element_type=jnp.float32).astype(jnp.bfloat16)
    return context, grad_q, grad_k, grad_v


def solution(mesh):
    def local_backward(x_in, x_mid, d_out, q_saved, k_saved, v_saved, z_saved, ln1_gain, ln1_bias, ln2_gain, ln2_bias, w_qkv, w_proj, w_fc1, w_fc2):
        norm2_hat, norm2_rstd, h2_local = layer_norm_fwd(x_mid, ln2_gain, ln2_bias)
        h2_full = lax.all_gather(h2_local, 'tp', axis=1, tiled=True)
        dout_full = lax.all_gather(d_out, 'tp', axis=1, tiled=True)
        act_value, act_slope = gelu_parts(z_saved.astype(jnp.float32))
        grad_wfc2 = jnp.einsum('bsf,bsd->fd', act_value.astype(jnp.bfloat16), dout_full, preferred_element_type=jnp.float32)
        grad_pre = (jnp.einsum('bsd,fd->bsf', dout_full, w_fc2, preferred_element_type=jnp.float32) * act_slope).astype(jnp.bfloat16)
        grad_wfc1 = jnp.einsum('bsd,bsf->df', h2_full, grad_pre, preferred_element_type=jnp.float32)
        grad_bfc1 = jnp.sum(grad_pre, axis=(0, 1), dtype=jnp.float32)
        h2_partial = jnp.einsum('bsf,df->bsd', grad_pre, w_fc1, preferred_element_type=jnp.float32).astype(jnp.bfloat16)
        grad_h2 = lax.psum_scatter(h2_partial, 'tp', scatter_dimension=1, tiled=True).astype(jnp.float32)
        grad_mid = (d_out.astype(jnp.float32) + layer_norm_bwd(grad_h2, norm2_hat, norm2_rstd, ln2_gain)).astype(jnp.bfloat16)
        mid_full = lax.all_gather(grad_mid, 'tp', axis=1, tiled=True)
        norm1_hat, norm1_rstd, h1_local = layer_norm_fwd(x_in, ln1_gain, ln1_bias)
        h1_full = lax.all_gather(h1_local, 'tp', axis=1, tiled=True)
        grad_ctx = jnp.einsum('bsd,hed->bshe', mid_full, w_proj, preferred_element_type=jnp.float32).astype(jnp.bfloat16)
        context, grad_q, grad_k, grad_v = attention_grads(q_saved, k_saved, v_saved, grad_ctx)
        grad_wproj = jnp.einsum('bshe,bsd->hed', context, mid_full, preferred_element_type=jnp.float32)
        qkv_grads = jnp.stack([grad_q, grad_k, grad_v])
        grad_wqkv = jnp.einsum('bsd,ibshe->idhe', h1_full, qkv_grads, preferred_element_type=jnp.float32)
        grad_bqkv = jnp.sum(qkv_grads, axis=(1, 2), dtype=jnp.float32)
        h1_partial = jnp.einsum('ibshe,idhe->bsd', qkv_grads, w_qkv, preferred_element_type=jnp.float32).astype(jnp.bfloat16)
        grad_h1 = lax.psum_scatter(h1_partial, 'tp', scatter_dimension=1, tiled=True).astype(jnp.float32)
        grad_x = (grad_mid.astype(jnp.float32) + layer_norm_bwd(grad_h1, norm1_hat, norm1_rstd, ln1_gain)).astype(jnp.bfloat16)
        vec_partial = jnp.stack([
            jnp.sum(grad_h1 * norm1_hat, axis=(0, 1)),
            jnp.sum(grad_h1, axis=(0, 1)),
            jnp.sum(grad_h2 * norm2_hat, axis=(0, 1)),
            jnp.sum(grad_h2, axis=(0, 1)),
            jnp.sum(grad_mid, axis=(0, 1), dtype=jnp.float32),
            jnp.sum(d_out, axis=(0, 1), dtype=jnp.float32),
        ])
        grad_vecs = lax.psum(vec_partial, 'tp')
        return grad_x, grad_wqkv, grad_bqkv, grad_wproj, grad_wfc1, grad_bfc1, grad_wfc2, grad_vecs

    tok_spec = P('dp', 'tp', None)
    head_spec = P('dp', None, 'tp', None)
    in_specs = (tok_spec, tok_spec, tok_spec, head_spec, head_spec, head_spec, P('dp', None, 'tp'),
                P(None), P(None), P(None), P(None),
                P(None, None, 'tp', None), P('tp', None, None), P(None, 'tp'), P('tp', None))
    out_specs = (tok_spec, P('dp', None, 'tp', None), P('dp', 'tp', None), P(('dp', 'tp'), None, None),
                 P('dp', 'tp'), P(('dp', 'tp')), P(('dp', 'tp'), None), P('dp', None))
    return jax.shard_map(local_backward, mesh=mesh, in_specs=in_specs, out_specs=out_specs, check_vma=False)
```

profile of v0, /device:TPU:0, one launch (start us, length us, event | category | flops | bytes accessed | tf_op | source)
XLA Modules:
  0.0 721.9 jit_solution(1896685962784071859)
XLA Ops:
  7.2 0.0 copy-start
  7.2 0.0 all-gather.5.cloned.1.call-start
  7.2 0.7 all-gather.5.cloned.1.call-update
  7.9 0.0 reduce-scatter.3.cloned.1.call-start
  8.0 62.1 %all-gather.5.cloned.1.call-done = bf16[1,2048,2560]{2,1,0:T(8,128)(2,1)} async-done(((bf16[1,256,2560]{2,1,0:T(8,128)(2,1)}), bf16[1,2048,2560]{2,1,0:T(8,128)(2,1)}) %all-gather.5.cloned.1.call-update) | async-done | bytes 10485776 | tf_op jit(solution)/shard_map/all_gather | solution.py:54
  70.1 24.1 %convert_reduce_fusion = (f32[1280]{0:T(1024)}, bf16[1,2048,1280]{2,1,0:T(8,128)(2,1)S(1)}) fusion(bf16[1,2048,1280]{2,1,0:T(8,128)(2,1)} %param.21, bf16[1280,2560]{1,0:T(8,128)(2,1)} %param.29, bf16[1,2048,2560]{2,1,0:T(8,128)(2,1)} %all-gather.5.cloned.1.call-done), kind=kOutput, calls=%fused_computation.51 | convolution fusion | flops 13479443456 | bytes 27530240 | tf_op jit(solution)/shard_map/bsd,fd->bsf/dot_general | solution.py:57
  94.2 2.4 copy-done.21
  96.5 18.7 %fusion.44 = bf16[1,2048,2560]{2,1,0:T(8,128)(2,1)} fusion(bf16[2560,1280]{1,0:T(8,128)(2,1)} %param.28, bf16[1,2048,1280]{2,1,0:T(8,128)(2,1)S(1)} %get-tuple-element.24), kind=kOutput, calls=%fused_computation.52 | convolution fusion | flops 13427015680 | bytes 22282240 | tf_op jit(solution)/shard_map/bsf,df->bsd/dot_general | solution.py:60
  115.3 0.0 reduce-scatter.3.cloned.1.call-update
  115.3 0.0 all-gather.7.cloned.1.call-start
  115.3 1.2 copy-done.2
  116.6 0.3 convert_reduce_fusion.6
  116.8 0.5 fusion.99
  117.3 70.5 %reduce-scatter.3.cloned.1.call-done = bf16[1,256,2560]{2,1,0:T(8,128)(2,1)} async-done(((bf16[1,2048,2560]{2,1,0:T(8,128)(2,1)}), bf16[1,256,2560]{2,1,0:T(8,128)(2,1)}) %reduce-scatter.3.cloned.1.call-update) | async-done | bytes 1310736 | tf_op jit(solution)/shard_map/reduce_scatter | solution.py:61
  187.9 4.3 fusion.104
  192.2 3.6 convert_reduce_fusion.5
  195.8 0.0 all-gather.7.cloned.1.call-update
  195.8 0.5 reduce-scatter.5.cloned.1.call-start
  196.3 4.1 iota_compare_fusion
  200.5 36.2 %fusion.150 = (f32[4,2048]{1,0:T(4,128)S(1)}, f32[4,2048,2048]{1,2,0:T(8,128)}) fusion(pred[2048,2048]{0,1:T(8,128)(4,1)} %iota_compare_fusion, bf16[1,2048,4,80]{1,3,2,0:T(8,128)(2,1)} %param.19, bf16[1,2048,4,80]{1,3,2,0:T(8,128)(2,1)S(1)} %copy-done.20), kind=kOutput, calls=%fused_computation.149 | convolution fusion | flops 2751465472 | bytes 73957376 | tf_op jit(solution)/shard_map/sub | solution.py:39
  236.7 16.7 %all-gather.7.cloned.1.call-done = bf16[1,2048,2560]{2,1,0:T(8,128)(2,1)} async-done(((bf16[1,256,2560]{2,1,0:T(8,128)(2,1)}), bf16[1,2048,2560]{2,1,0:T(8,128)(2,1)}) %all-gather.7.cloned.1.call-update) | async-done | bytes 10485776 | tf_op jit(solution)/shard_map/all_gather | solution.py:63
  253.4 7.7 %fusion.81 = bf16[2048,4,80]{0,2,1:T(8,128)(2,1)S(1)} fusion(bf16[4,80,2560]{2,1,0:T(8,128)(2,1)S(1)} %copy-done, bf16[1,2048,2560]{2,1,0:T(8,128)(2,1)} %all-gather.7.cloned.1.call-done), kind=kOutput, calls=%fused_computation.97 | convolution fusion | flops 3356098560 | bytes 13434880 | tf_op jit(solution)/shard_map/bsd,hed->bshe/dot_general | solution.py:66
  261.0 23.1 %fusion.123 = f32[4,2048,2048]{1,2,0:T(8,128)} fusion(bf16[2048,4,80]{0,2,1:T(8,128)(2,1)S(1)} %fusion.81, bf16[1,2048,4,80]{1,3,2,0:T(8,128)(2,1)S(1)} %copy-done.7), kind=kOutput, calls=%fused_computation.122 | convolution fusion | flops 2684354560 | bytes 69730304 | tf_op jit(solution)/shard_map/bqhe,bkhe->bhqk/dot_general | solution.py:42
  284.2 24.5 %fusion.117 = bf16[1,1,2048,4,80]{2,4,3,1,0:T(8,128)(2,1)} fusion(bf16[2048,4,80]{0,2,1:T(8,128)(2,1)S(1)} %fusion.81, f32[4,2048,2048]{1,2,0:T(8,128)} %get-tuple-element.22, f32[4,2048]{1,0:T(4,128)S(1)} %get-tuple-element.21), kind=kOutput, calls=%fused_computation.119 | convolution fusion | flops 2718564352 | bytes 69763072 | tf_op jit(solution)/shard_map/bhqk,bqhe->bkhe/dot_general | solution.py:46
  308.6 82.3 %fusion.106 = bf16[1,1,2048,4,80]{2,4,3,1,0:T(8,128)(2,1)S(1)} fusion(f32[4,2048,2048]{1,2,0:T(8,128)} %fusion.123, bf16[1,2048,4,80]{1,3,2,0:T(8,128)(2,1)} %param.18, f32[4,2048,2048]{1,2,0:T(8,128)} %get-tuple-element.22, f32[4,2048]{1,0:T(4,128)S(1)} %get-tuple-element.21), kind=kOutput, calls=%fused_computation.116 | convolution fusion | flops 2802460672 | bytes 136871936 | tf_op jit(solution)/shard_map/bhqk,bqhe->bkhe/dot_general | solution.py:45
  391.0 83.2 %fusion.109 = bf16[1,1,2048,4,80]{2,4,3,1,0:T(8,128)(2,1)} fusion(f32[4,2048,2048]{1,2,0:T(8,128)} %fusion.123, bf16[1,2048,4,80]{1,3,2,0:T(8,128)(2,1)} %param.19, f32[4,2048,2048]{1,2,0:T(8,128)} %get-tuple-element.22, f32[4,2048]{1,0:T(4,128)S(1)} %get-tuple-element.21), kind=kOutput, calls=%fused_computation.117 | convolution fusion | flops 2802460672 | bytes 136871936 | tf_op jit(solution)/shard_map/bhqk,bkhe->bqhe/dot_general | solution.py:44
  474.1 15.8 %fusion.45 = bf16[1,2048,2560]{2,1,0:T(8,128)(2,1)} fusion(bf16[3,2560,4,80]{1,3,2,0:T(8,128)(2,1)} %param.26, bf16[1,1,2048,4,80]{2,4,3,1,0:T(8,128)(2,1)S(1)} %copy-done.8, bf16[1,1,2048,4,80]{2,4,3,1,0:T(8,128)(2,1)S(1)} %fusion.106, bf16[1,1,2048,4,80]{2,4,3,1,0:T(8,128)(2,1)} %fusion.109), kind=kOutput, calls=%fused_computation.53 | convolution fusion | flops 10075504640 | bytes 19333120 | tf_op jit(solution)/shard_map/ibshe,idhe->bsd/dot_general | solution.py:72
  489.9 0.0 reduce-scatter.5.cloned.1.call-update
  489.9 0.0 copy-start.13
  490.0 0.0 copy-start.19
  490.0 0.0 all-gather.11.cloned.1.call-start
  490.0 0.5 all-gather.11.cloned.1.call-update
  490.6 0.0 all-gather.9.cloned.1.call-start
  490.6 0.6 copy-done.3
  491.2 0.3 convert_reduce_fusion.4
  491.5 0.5 fusion.94
  492.0 70.5 %reduce-scatter.5.cloned.1.call-done = bf16[1,256,2560]{2,1,0:T(8,128)(2,1)} async-done(((bf16[1,2048,2560]{2,1,0:T(8,128)(2,1)}), bf16[1,256,2560]{2,1,0:T(8,128)(2,1)}) %reduce-scatter.5.cloned.1.call-update) | async-done | bytes 1310736 | tf_op jit(solution)/shard_map/reduce_scatter | solution.py:73
  562.5 3.9 fusion.105
  566.4 0.0 all-gather.9.cloned.1.call-update
  566.5 24.8 %fusion.38 = f32[1280,2560]{1,0:T(8,128)} fusion(bf16[1,2048,2560]{2,1,0:T(8,128)(2,1)} %all-gather.5.cloned.1.call-done, bf16[1,2048,1280]{2,1,0:T(8,128)(2,1)} %param.21), kind=kOutput, calls=%fused_computation.47 | convolution fusion | flops 13447987200 | bytes 28835840 | tf_op jit(solution)/shard_map/bsf,bsd->fd/dot_general | solution.py:56
  591.4 1.3 convert_reduce_fusion.1
  592.7 29.5 %all-gather.11.cloned.1.call-done = bf16[1,2048,2560]{2,1,0:T(8,128)(2,1)} async-done(((bf16[1,256,2560]{2,1,0:T(8,128)(2,1)}), bf16[1,2048,2560]{2,1,0:T(8,128)(2,1)}) %all-gather.11.cloned.1.call-update) | async-done | bytes 10485776 | tf_op jit(solution)/shard_map/all_gather | solution.py:53
  622.2 19.8 %fusion.32 = f32[2560,1280]{1,0:T(8,128)} fusion(bf16[1,2048,2560]{2,1,0:T(8,128)(2,1)} %all-gather.11.cloned.1.call-done, bf16[1,2048,1280]{2,1,0:T(8,128)(2,1)} %copy-done.21), kind=kOutput, calls=%fused_computation.41 | convolution fusion | flops 13421772800 | bytes 28835840 | tf_op jit(solution)/shard_map/bsd,bsf->df/dot_general | solution.py:58
  642.0 29.0 %fusion.34 = f32[4,80,2560]{2,1,0:T(8,128)} fusion(bf16[1,2048,2560]{2,1,0:T(8,128)(2,1)} %all-gather.7.cloned.1.call-done, bf16[1,2048,4,80]{1,3,2,0:T(8,128)(2,1)} %param.20, f32[4,2048,2048]{1,2,0:T(8,128)} %get-tuple-element.22, f32[4,2048]{1,0:T(4,128)S(1)} %get-tuple-element.21), kind=kOutput, calls=%fused_computation.43 | convolution fusion | flops 6074007552 | bytes 82214912 | tf_op jit(solution)/shard_map/bshe,bsd->hed/dot_general | solution.py:68
  671.0 0.1 stack.43
  671.1 23.5 %psum.7 = f32[6,2560]{1,0:T(8,128)} all-reduce(f32[6,2560]{1,0:T(8,128)S(1)} %stack.43), channel_id=1, replica_groups=mesh['dp'=1,'tp'=8] {'tp'}, use_global_device_ids=true, to_apply=%region_21.22 | all-reduce | flops 15360 | bytes 122880 | tf_op jit(solution)/shard_map/psum | solution.py:83
  694.6 3.6 fusion.101
  698.1 16.5 %fusion.48 = f32[3,2560,4,80]{1,3,2,0:T(8,128)} fusion(bf16[1,2048,2560]{2,1,0:T(8,128)(2,1)} %all-gather.9.cloned.1.call-done, bf16[1,1,2048,4,80]{2,4,3,1,0:T(8,128)(2,1)} %fusion.117, bf16[1,1,2048,4,80]{2,4,3,1,0:T(8,128)(2,1)} %copy-done.9, bf16[1,1,2048,4,80]{2,4,3,1,0:T(8,128)(2,1)} %fusion.109), kind=kOutput, calls=%fused_computation.56 | convolution fusion | flops 10070261760 | bytes 24248320 | tf_op jit(solution)/shard_map/bsd,ibshe->idhe/dot_general | solution.py:70
  (52 shorter events, 0.2 us)
Async XLA Ops:
  7.2 246.2 %copy-start = (bf16[4,80,2560]{2,1,0:T(8,128)(2,1)S(1)}, bf16[4,80,2560]{2,1,0:T(8,128)(2,1)}, u32[]{:S(2)}) copy-start(bf16[4,80,2560]{2,1,0:T(8,128)(2,1)} %param.27) | copy-start | bytes 4915204
  7.2 62.9 %all-gather.5.cloned.1.call-start = ((), (), s32[]{:S(2)}) async-start(), calls=%async_computation.2 | async-start | bytes 11796480 | tf_op jit(solution)/shard_map/all_gather | solution.py:54
  7.9 180.0 %reduce-scatter.3.cloned.1.call-start = ((), (), s32[]{:S(2)}) async-start(), calls=%async_computation.3 | async-start | bytes 11796480 | tf_op jit(solution)/shard_map/reduce_scatter | solution.py:61
  94.2 2.4 copy-start.21
  115.2 1.3 copy-start.2
  115.3 72.6 %copy-start.12 = (f32[2560]{0:T(1024)S(1)}, f32[2560]{0:T(1024)}, u32[]{:S(2)}) copy-start(f32[2560]{0:T(1024)} %param.24) | copy-start | bytes 30724
  115.3 72.6 %copy-start.18 = (f32[2560]{0:T(1024)S(1)}, f32[2560]{0:T(1024)}, u32[]{:S(2)}) copy-start(f32[2560]{0:T(1024)} %param.25) | copy-start | bytes 30724
  115.3 138.1 %all-gather.7.cloned.1.call-start = ((), (), s32[]{:S(2)}) async-start(), calls=%async_computation.4 | async-start | bytes 11796480 | tf_op jit(solution)/shard_map/all_gather | solution.py:63
  187.9 4.3 copy-start.5
  187.9 4.3 copy-start.6
  195.8 4.7 copy-start.20
  195.8 366.7 %reduce-scatter.5.cloned.1.call-start = ((), (), s32[]{:S(2)}) async-start(), calls=%async_computation.5 | async-start | bytes 11796480 | tf_op jit(solution)/shard_map/reduce_scatter | solution.py:73
  253.4 7.7 %copy-start.7 = (bf16[1,2048,4,80]{1,3,2,0:T(8,128)(2,1)S(1)}, bf16[1,2048,4,80]{1,3,2,0:T(8,128)(2,1)}, u32[]{:S(2)}) copy-start(bf16[1,2048,4,80]{1,3,2,0:T(8,128)(2,1)} %param.20) | copy-start | bytes 3932164
  390.9 83.2 %copy-start.9 = (bf16[1,1,2048,4,80]{2,4,3,1,0:T(8,128)(2,1)}, bf16[1,1,2048,4,80]{2,4,3,1,0:T(8,128)(2,1)S(1)}, u32[]{:S(2)}) copy-start(bf16[1,1,2048,4,80]{2,4,3,1,0:T(8,128)(2,1)S(1)} %fusion.106) | copy-start | bytes 3932164
  390.9 83.2 %copy-start.8 = (bf16[1,1,2048,4,80]{2,4,3,1,0:T(8,128)(2,1)S(1)}, bf16[1,1,2048,4,80]{2,4,3,1,0:T(8,128)(2,1)}, u32[]{:S(2)}) copy-start(bf16[1,1,2048,4,80]{2,4,3,1,0:T(8,128)(2,1)} %fusion.117) | copy-start | bytes 3932164
  489.9 1.3 copy-start.3
  489.9 72.6 %copy-start.13 = (f32[2560]{0:T(1024)S(1)}, f32[2560]{0:T(1024)}, u32[]{:S(2)}) copy-start(f32[2560]{0:T(1024)} %param.22) | copy-start | bytes 30724
  490.0 72.6 %copy-start.19 = (f32[2560]{0:T(1024)S(1)}, f32[2560]{0:T(1024)}, u32[]{:S(2)}) copy-start(f32[2560]{0:T(1024)} %param.23) | copy-start | bytes 30724
  490.0 132.2 %all-gather.11.cloned.1.call-start = ((), (), s32[]{:S(2)}) async-start(), calls=%async_computation.7 | async-start | bytes 11796480 | tf_op jit(solution)/shard_map/all_gather | solution.py:53
  490.6 207.6 %all-gather.9.cloned.1.call-start = ((), (), s32[]{:S(2)}) async-start(), calls=%async_computation.6 | async-start | bytes 11796480 | tf_op jit(solution)/shard_map/all_gather | solution.py:65
  566.4 24.8 %copy-start.15 = (f32[2560]{0:T(1024)S(1)}, f32[2560]{0:T(1024)}, u32[]{:S(2)}) copy-start(f32[2560]{0:T(1024)} %get-tuple-element.8) | copy-start | bytes 30724
  566.5 24.9 %copy-start.14 = (f32[2560]{0:T(1024)S(1)}, f32[2560]{0:T(1024)}, u32[]{:S(2)}) copy-start(f32[2560]{0:T(1024)} %get-tuple-element.14) | copy-start | bytes 30724
  566.5 24.9 %copy-start.17 = (f32[2560]{0:T(1024)S(1)}, f32[2560]{0:T(1024)}, u32[]{:S(2)}) copy-start(f32[2560]{0:T(1024)} %get-tuple-element.16) | copy-start | bytes 30724
  566.5 24.9 %copy-start.16 = (f32[2560]{0:T(1024)S(1)}, f32[2560]{0:T(1024)}, u32[]{:S(2)}) copy-start(f32[2560]{0:T(1024)} %get-tuple-element.20) | copy-start | bytes 30724
  566.5 24.9 %copy-start.10 = (bf16[1,1,2048,4,80]{2,4,3,1,0:T(8,128)(2,1)S(1)}, bf16[1,1,2048,4,80]{2,4,3,1,0:T(8,128)(2,1)}, u32[]{:S(2)}) copy-start(bf16[1,1,2048,4,80]{2,4,3,1,0:T(8,128)(2,1)} %copy-done.9) | copy-start | bytes 3932164
  566.5 24.9 %copy-start.11 = (bf16[1,1,2048,4,80]{2,4,3,1,0:T(8,128)(2,1)S(1)}, bf16[1,1,2048,4,80]{2,4,3,1,0:T(8,128)(2,1)}, u32[]{:S(2)}) copy-start(bf16[1,1,2048,4,80]{2,4,3,1,0:T(8,128)(2,1)} %fusion.109) | copy-start | bytes 3932164
  642.0 52.6 %copy-start.4 = (bf16[1,256,2560]{2,1,0:T(8,128)(2,1)S(1)}, bf16[1,256,2560]{2,1,0:T(8,128)(2,1)}, u32[]{:S(2)}) copy-start(bf16[1,256,2560]{2,1,0:T(8,128)(2,1)} %get-tuple-element.17) | copy-start | bytes 3932164
  698.1 16.5 %copy-start.1 = (bf16[4,80,2560]{2,1,0:T(8,128)(2,1)S(1)}, bf16[4,80,2560]{2,1,0:T(8,128)(2,1)}, u32[]{:S(2)}) copy-start(bf16[4,80,2560]{2,1,0:T(8,128)(2,1)} %param.27) | copy-start | bytes 4915204
Sparse Core Ops, SparseCore 0:
  9.8 60.2 all-gather.4
  115.4 72.4 reduce-scatter.2
  195.9 57.3 all-gather.6
  490.1 72.4 reduce-scatter.4
  564.8 57.3 all-gather.10
  623.8 57.9 all-gather.8
where the time goes:
time: 730 us; the launch traced here: 722 us
  matrix products  406 us (56%)
  waiting for transfers between devices  251 us (34%)
  blocking collectives  23.5 us (3%)
  other arithmetic  22.3 us (3%)
  between operations  14.8 us (2%)
    dot_general x1, matrix products, attention_grads(): jnp.einsum('bhqk,bkhe->bqhe', grad_scores, k_heads, preferred_element_typ...  83.2 us
    dot_general x1, matrix products, attention_grads(): jnp.einsum('bhqk,bqhe->bkhe', grad_scores, q_heads, preferred_element_typ...  82.3 us
    reduce_scatter x1, waiting for transfers between devices, local_backward(): lax.psum_scatter(h2_partial, 'tp', scatter_dimension=1, tiled=True)  70.5 us
    reduce_scatter x1, waiting for transfers between devices, local_backward(): lax.psum_scatter(h1_partial, 'tp', scatter_dimension=1, tiled=True)  70.5 us
    all_gather x1, waiting for transfers between devices, local_backward(): dout_full = lax.all_gather(d_out, 'tp', axis=1, tiled=True)  62.1 us
    sub x1, matrix products, attention_grads(): attn_probs = jax.nn.softmax(scores, axis=-1)  36.2 us
    all_gather x1, waiting for transfers between devices, local_backward(): h2_full = lax.all_gather(h2_local, 'tp', axis=1, tiled=True)  29.5 us
    dot_general x1, matrix products, local_backward(): jnp.einsum('bshe,bsd->hed', context, mid_full, preferred_element_type=jnp...  29 us
  transfers between devices with their start and end apart: 6, of which 5 were waited for; matrix products, arithmetic and copies ran while one was open for 17% of the time, Pallas kernels for 0%

commit v1 on v0

v1 whole, which is shorter than its diff:
```python
import jax
import jax.numpy as jnp
from jax import lax
from jax.experimental import pallas as pl
from jax.experimental.pallas import tpu as pltpu
from jax.sharding import PartitionSpec as P

LN_EPS = 1e-5
GELU_COEF = 0.044715
GELU_SCALE = 0.7978845608028654
LOG2E = 1.4426950408889634
BLK = 512
F32 = jnp.float32
BF16 = jnp.bfloat16


def layer_norm_fwd(token_rows, norm_gain, norm_bias):
    rows_f32 = token_rows.astype(F32)
    centered = rows_f32 - jnp.mean(rows_f32, axis=-1, keepdims=True)
    inv_std = lax.rsqrt(jnp.mean(centered * centered, axis=-1, keepdims=True) + LN_EPS)
    x_hat = centered * inv_std
    return x_hat, inv_std, (x_hat * norm_gain + norm_bias).astype(BF16)


def layer_norm_bwd(grad_norm, x_hat, inv_std, norm_gain):
    grad_hat = grad_norm * norm_gain
    centered_grad = grad_hat - jnp.mean(grad_hat, axis=-1, keepdims=True)
    return inv_std * (centered_grad - x_hat * jnp.mean(grad_hat * x_hat, axis=-1, keepdims=True))


def gelu_parts(pre_act):
    tanh_val = jnp.tanh(GELU_SCALE * (pre_act + GELU_COEF * pre_act * pre_act * pre_act))
    act_value = 0.5 * pre_act * (1.0 + tanh_val)
    act_slope = 0.5 * (1.0 + tanh_val) + 0.5 * pre_act * (1.0 - tanh_val * tanh_val) * GELU_SCALE * (1.0 + 3.0 * GELU_COEF * pre_act * pre_act)
    return act_value, act_slope


def dot(a, b):
    return jnp.dot(a, b, preferred_element_type=F32)


def causal_fill(scores, fill):
    key_ids = lax.broadcasted_iota(jnp.int32, scores.shape, 0)
    query_ids = lax.broadcasted_iota(jnp.int32, scores.shape, 1)
    return jnp.where(query_ids >= key_ids, scores, fill)


def attn_fwd_kernel(q_ref, k_ref, v_ref, ctx_ref, wide_ref, max_ref, inv_ref, k_rows, strip):
    qi = pl.program_id(1)
    exp_scale = q_ref.shape[1] ** -0.5 * LOG2E

    @pl.when(qi == 0)
    def _():
        k_rows[...] = k_ref[0].T

    q_blk = q_ref[0]

    def scores(ki):
        rows = k_rows[pl.ds(pl.multiple_of(ki * BLK, BLK), BLK), :]
        return dot(rows, q_blk)

    def score_step(ki, run_max):
        blk = scores(ki)
        strip[pl.ds(pl.multiple_of(ki * BLK, BLK), BLK), :] = blk
        return jnp.maximum(run_max, jnp.max(blk, axis=0, keepdims=True))

    diag = causal_fill(scores(qi), -1e30)
    strip[pl.ds(pl.multiple_of(qi * BLK, BLK), BLK), :] = diag
    row_max = lax.fori_loop(0, qi, score_step, jnp.max(diag, axis=0, keepdims=True))

    def exp_step(ki, run_sum):
        at = pl.ds(pl.multiple_of(ki * BLK, BLK), BLK)
        probs = jnp.exp2((strip[at, :] - row_max) * exp_scale)
        strip[at, :] = probs
        return run_sum + jnp.sum(probs, axis=0, keepdims=True)

    row_inv = 1.0 / lax.fori_loop(0, qi + 1, exp_step, jnp.zeros_like(row_max))

    def ctx_step(ki, carry):
        high, low = carry
        off = pl.multiple_of(ki * BLK, BLK)
        probs = strip[pl.ds(off, BLK), :] * row_inv
        probs_low = probs.astype(BF16)
        rest = (probs - probs_low.astype(F32)).astype(BF16)
        v_blk = v_ref[0, :, pl.ds(off, BLK)]
        return high + dot(v_blk, probs_low), low + dot(v_blk, rest)

    zero = jnp.zeros((q_ref.shape[1], BLK), F32)
    high, low = lax.fori_loop(0, qi + 1, ctx_step, (zero, zero))
    ctx_ref[0] = high.astype(BF16)
    wide_ref[0] = high + low
    max_ref[0] = row_max
    inv_ref[0] = row_inv


def attn_fwd(q_t, k_t, v_t):
    heads, dim, seq = q_t.shape
    whole = pl.BlockSpec((1, dim, seq), lambda h, i: (h, 0, 0))
    part = pl.BlockSpec((1, dim, BLK), lambda h, i: (h, 0, i))
    row = pl.BlockSpec((1, 1, BLK), lambda h, i: (h, 0, i))
    shape = jax.ShapeDtypeStruct
    return pl.pallas_call(
        attn_fwd_kernel,
        grid=(heads, seq // BLK),
        in_specs=[part, whole, whole],
        out_specs=[part, part, row, row],
        out_shape=[shape((heads, dim, seq), BF16), shape((heads, dim, seq), F32),
                   shape((heads, 1, seq), F32), shape((heads, 1, seq), F32)],
        scratch_shapes=[pltpu.VMEM((seq, dim), BF16), pltpu.VMEM((seq, BLK), F32)],
        cost_estimate=pl.CostEstimate(flops=20_000_000_000, bytes_accessed=12_000_000, transcendentals=10_000_000),
        name="attn_fwd",
    )(q_t, k_t, v_t)


def attn_bwd_kernel(qi_tab, ki_tab, q_ref, k_ref, v_ref, do_ref, wide_ref, max_ref, inv_ref, out_ref,
                    k_rows, v_rows, q_rows, do_rows, delta, dq_acc, dk_acc, dv_acc):
    step = pl.program_id(1)
    scale = q_ref.shape[1] ** -0.5
    exp_scale = scale * LOG2E

    @pl.when(step == 0)
    def _():
        k_rows[...] = k_ref[0].T
        v_rows[...] = v_ref[0].T
        q_rows[...] = q_ref[0].T
        do_rows[...] = do_ref[0].T
        delta[...] = jnp.sum(do_ref[0].astype(F32) * wide_ref[0], axis=0, keepdims=True)
        dq_acc[...] = jnp.zeros_like(dq_acc)
        dk_acc[...] = jnp.zeros_like(dk_acc)
        dv_acc[...] = jnp.zeros_like(dv_acc)

    qi, ki = qi_tab[step], ki_tab[step]
    q_at = pl.ds(pl.multiple_of(qi * BLK, BLK), BLK)
    k_at = pl.ds(pl.multiple_of(ki * BLK, BLK), BLK)

    def block(on_diag):
        scores = dot(k_rows[k_at, :], q_ref[0, :, q_at])
        if on_diag:
            scores = causal_fill(scores, -1e30)
        probs = jnp.exp2((scores - max_ref[0, :, q_at]) * exp_scale) * inv_ref[0, :, q_at]
        grad_probs = dot(v_rows[k_at, :], do_ref[0, :, q_at])
        dv_acc[k_at, :] += dot(probs.astype(BF16), do_rows[q_at, :])
        grad_scores = (probs * (grad_probs - delta[:, q_at]) * scale).astype(BF16)
        dk_acc[k_at, :] += dot(grad_scores, q_rows[q_at, :])
        dq_acc[:, q_at] += dot(k_ref[0, :, k_at], grad_scores)

    @pl.when(qi == ki)
    def _():
        block(True)

    @pl.when(qi != ki)
    def _():
        block(False)

    @pl.when(step == pl.num_programs(1) - 1)
    def _():
        out_ref[0, 0] = dq_acc[...].astype(BF16)
        out_ref[1, 0] = dk_acc[...].T.astype(BF16)
        out_ref[2, 0] = dv_acc[...].T.astype(BF16)


def attn_bwd(q_t, k_t, v_t, do_t, wide, row_max, row_inv):
    heads, dim, seq = q_t.shape
    n_blk = seq // BLK
    pairs = [(qi, ki) for ki in range(n_blk) for qi in range(ki, n_blk)]
    qi_tab = jnp.array([p[0] for p in pairs], jnp.int32)
    ki_tab = jnp.array([p[1] for p in pairs], jnp.int32)
    whole = pl.BlockSpec((1, dim, seq), lambda h, s, *_: (h, 0, 0))
    row = pl.BlockSpec((1, 1, seq), lambda h, s, *_: (h, 0, 0))
    rows = pltpu.VMEM((seq, dim), BF16)
    return pl.pallas_call(
        attn_bwd_kernel,
        grid_spec=pltpu.PrefetchScalarGridSpec(
            num_scalar_prefetch=2,
            grid=(heads, len(pairs)),
            in_specs=[whole] * 5 + [row] * 2,
            out_specs=[pl.BlockSpec((3, 1, dim, seq), lambda h, s, *_: (0, h, 0, 0))],
            scratch_shapes=[rows] * 4 + [pltpu.VMEM((1, seq), F32), pltpu.VMEM((dim, seq), F32),
                                         pltpu.VMEM((seq, dim), F32), pltpu.VMEM((seq, dim), F32)],
        ),
        out_shape=[jax.ShapeDtypeStruct((3, heads, dim, seq), BF16)],
        cost_estimate=pl.CostEstimate(flops=40_000_000_000, bytes_accessed=16_000_000, transcendentals=10_000_000),
        name="attn_bwd",
    )(qi_tab, ki_tab, q_t, k_t, v_t, do_t, wide, row_max, row_inv)[0]


def after(value, *others):
    return lax.optimization_barrier((value,) + others)[0]


def solution(mesh):
    def local_backward(x_in, x_mid, d_out, q_saved, k_saved, v_saved, z_saved, ln1_gain, ln1_bias, ln2_gain, ln2_bias, w_qkv, w_proj, w_fc1, w_fc2):
        x_in, x_mid, d_out, z_saved = x_in[0], x_mid[0], d_out[0], z_saved[0]
        heads, dim = q_saved.shape[2:]
        seq, model = z_saved.shape[0], x_in.shape[1]
        gather = lambda v: lax.all_gather(v, 'tp', axis=0, tiled=True)
        scatter = lambda v: lax.psum_scatter(v, 'tp', scatter_dimension=0, tiled=True).astype(F32)

        dout_full = gather(d_out)
        q_t, k_t, v_t = (v[0].transpose(1, 2, 0) for v in (q_saved, k_saved, v_saved))
        ctx_t, wide_t, row_max, row_inv = attn_fwd(q_t, k_t, v_t)
        norm2_hat, norm2_rstd, h2_local = layer_norm_fwd(x_mid, ln2_gain, ln2_bias)
        norm1_hat, norm1_rstd, h1_local = layer_norm_fwd(x_in, ln1_gain, ln1_bias)

        act_value, act_slope = gelu_parts(z_saved.astype(F32))
        grad_pre = (jnp.einsum('sd,fd->sf', dout_full, w_fc2, preferred_element_type=F32) * act_slope).astype(BF16)
        h2_partial = jnp.einsum('sf,df->sd', grad_pre, w_fc1, preferred_element_type=F32).astype(BF16)
        grad_h2 = scatter(h2_partial)
        grad_wfc2 = jnp.einsum('sf,sd->fd', act_value.astype(BF16), dout_full, preferred_element_type=F32)
        grad_bfc1 = jnp.sum(grad_pre, axis=0, dtype=F32)
        grad_mid = (d_out.astype(F32) + layer_norm_bwd(grad_h2, norm2_hat, norm2_rstd, ln2_gain)).astype(BF16)
        mid_full = gather(grad_mid)

        h1_full = gather(after(h1_local, mid_full))
        do_t = jnp.einsum('hed,sd->hes', w_proj, mid_full, preferred_element_type=F32).astype(BF16)
        qkv_t = attn_bwd(q_t, k_t, v_t, do_t, wide_t, row_max, row_inv)
        grad_wproj = jnp.einsum('hes,sd->hed', ctx_t, mid_full, preferred_element_type=F32)
        qkv_rows = qkv_t.reshape(3 * heads * dim, seq)
        w_rows = w_qkv.transpose(0, 2, 3, 1).reshape(3 * heads * dim, model)
        h1_partial = jnp.einsum('fs,fd->sd', qkv_rows, w_rows, preferred_element_type=F32).astype(BF16)
        grad_h1 = scatter(h1_partial)
        grad_wqkv = jnp.einsum('fs,sd->fd', qkv_rows, h1_full, preferred_element_type=F32)
        grad_wqkv = grad_wqkv.reshape(3, heads, dim, model).transpose(0, 3, 1, 2)
        grad_bqkv = jnp.sum(qkv_t, axis=3, dtype=F32)
        h2_full = gather(after(h2_local, h1_partial))
        grad_wfc1 = jnp.einsum('sd,sf->df', h2_full, grad_pre, preferred_element_type=F32)
        grad_x = (grad_mid.astype(F32) + layer_norm_bwd(grad_h1, norm1_hat, norm1_rstd, ln1_gain)).astype(BF16)
        vec_partial = jnp.stack([
            jnp.sum(grad_h1 * norm1_hat, axis=0),
            jnp.sum(grad_h1, axis=0),
            jnp.sum(grad_h2 * norm2_hat, axis=0),
            jnp.sum(grad_h2, axis=0),
            jnp.sum(grad_mid, axis=0, dtype=F32),
            jnp.sum(d_out, axis=0, dtype=F32),
        ])
        grad_vecs = lax.psum(vec_partial, 'tp')
        return grad_x[None], grad_wqkv, grad_bqkv, grad_wproj, grad_wfc1, grad_bfc1, grad_wfc2, grad_vecs

    tok_spec = P('dp', 'tp', None)
    head_spec = P('dp', None, 'tp', None)
    in_specs = (tok_spec, tok_spec, tok_spec, head_spec, head_spec, head_spec, P('dp', None, 'tp'),
                P(None), P(None), P(None), P(None),
                P(None, None, 'tp', None), P('tp', None, None), P(None, 'tp'), P('tp', None))
    out_specs = (tok_spec, P('dp', None, 'tp', None), P('dp', 'tp', None), P(('dp', 'tp'), None, None),
                 P('dp', 'tp'), P(('dp', 'tp')), P(('dp', 'tp'), None), P('dp', None))
    return jax.shard_map(local_backward, mesh=mesh, in_specs=in_specs, out_specs=out_specs, check_vma=False)
```

time: 730 us -> 545 us (0.75)
  matrix products: 406 us -> 134 us
  Pallas kernels: 0 us -> 79 us
  waiting for transfers between devices: 251 us -> 263 us
    dot_general x12 -> x8, matrix products: 369 us -> 134 us  [the longest x1 24.6 us: local_backward(): jnp.einsum('sf,sd->fd', act_value.astype(BF16), dout_full, preferred_elem...]
    pallas_call x0 -> x2, Pallas kernels: none -> 79 us  [the longest x1 42.8 us: attn_bwd(): pl.pallas_call(attn_bwd_kernel, grid_spec=pltpu.PrefetchScalarGridSpec(nu...]
    sub x1 -> x0, matrix products: 36.2 us -> none  [attention_grads(): attn_probs = jax.nn.softmax(scores, axis=-1)]
    all_gather x4, waiting for transfers between devices: 108 us -> 120 us  [local_backward(): gather = lambda v: lax.all_gather(v, 'tp', axis=0, tiled=True)]
  transfers between devices with their start and end apart: 6 -> 6, of which waited for: 5 -> 5; matrix products, arithmetic and copies ran while one was open for 17% -> 11% of each run, Pallas kernels for 0% -> 7%
where the time goes in v1:
time: 545 us; the launch traced here: 537 us
  waiting for transfers between devices  263 us (48%)
  matrix products  134 us (25%)
  Pallas kernels  79 us (14%)
  blocking collectives  24.3 us (4%)
  other arithmetic  17.1 us (3%)
  between operations  14.7 us (3%)
    reduce_scatter x2, waiting for transfers between devices, local_backward(): lax.psum_scatter(v, 'tp', scatter_dimension=0, tiled=True).astype(F32)  141 us
    all_gather x4, waiting for transfers between devices, local_backward(): gather = lambda v: lax.all_gather(v, 'tp', axis=0, tiled=True)  120 us
    pallas_call x1, Pallas kernels, attn_bwd(): pl.pallas_call(attn_bwd_kernel, grid_spec=pltpu.PrefetchScalarGridSpec(nu...  42.8 us
    pallas_call x1, Pallas kernels, attn_fwd(): pl.pallas_call(attn_fwd_kernel, grid=(heads, seq // BLK), in_specs=[part,...  36.3 us
    dot_general x1, matrix products, local_backward(): jnp.einsum('sf,sd->fd', act_value.astype(BF16), dout_full, preferred_elem...  24.6 us
    psum x1, blocking collectives, local_backward(): grad_vecs = lax.psum(vec_partial, 'tp')  24.3 us
    dot_general x1, matrix products, local_backward(): jnp.einsum('sd,fd->sf', dout_full, w_fc2, preferred_element_type=F32)  24.1 us
    dot_general x1, matrix products, local_backward(): jnp.einsum('sd,sf->df', h2_full, grad_pre, preferred_element_type=F32)  19.5 us
  transfers between devices with their start and end apart: 6, of which 5 were waited for; matrix products, arithmetic and copies ran while one was open for 11% of the time, Pallas kernels for 7%

profile of v1, /device:TPU:0, one launch (start us, length us, event | category | flops | bytes accessed | tf_op | source)
XLA Modules:
  0.0 536.7 jit_solution(15170539019080178816)
XLA Ops:
  7.2 0.0 copy-start
  7.2 0.0 all-gather.12.cloned.1.call-start
  7.2 0.7 all-gather.12.cloned.1.call-update
  7.9 0.0 reduce-scatter.3.cloned.1.call-start
  8.0 62.1 %all-gather.12.cloned.1.call-done = bf16[1,2048,2560]{2,1,0:T(8,128)(2,1)} async-done(((bf16[1,256,2560]{2,1,0:T(8,128)(2,1)}), bf16[1,2048,2560]{2,1,0:T(8,128)(2,1)}) %all-gather.12.cloned.1.call-update) | async-done | bytes 10485776 | tf_op jit(solution)/shard_map/all_gather | solution.py:196
  70.1 24.1 %convert_reduce_fusion = (f32[1280]{0:T(1024)}, bf16[2048,1280]{1,0:T(8,128)(2,1)S(1)}) fusion(bf16[1,2048,1280]{2,1,0:T(8,128)(2,1)} %param.23, bf16[1280,2560]{1,0:T(8,128)(2,1)} %param.31, bf16[1,2048,2560]{2,1,0:T(8,128)(2,1)} %all-gather.12.cloned.1.call-done), kind=kOutput, calls=%fused_computation.30 | convolution fusion | flops 13479443456 | bytes 27530240 | tf_op jit(solution)/shard_map/sd,fd->sf/dot_general | solution.py:206
  94.2 2.4 copy-done.14
  96.5 18.7 %convolution_convert_fusion = bf16[2048,2560]{1,0:T(8,128)(2,1)} fusion(bf16[2048,1280]{1,0:T(8,128)(2,1)S(1)} %get-tuple-element.33, bf16[2560,1280]{1,0:T(8,128)(2,1)} %param.30), kind=kOutput, calls=%fused_computation.10 | convolution fusion | flops 13427015680 | bytes 22282240 | tf_op jit(solution)/shard_map/sf,df->sd/dot_general | solution.py:207
  115.2 0.0 reduce-scatter.3.cloned.1.call-update
  115.3 0.0 copy-start.10
  115.3 0.0 copy-start.11
  115.3 0.0 all-gather.6.cloned.1.call-start
  115.3 1.2 copy-done.3
  116.6 0.3 convert_reduce_fusion.7
  116.8 0.5 fusion.53
  117.3 70.5 %reduce-scatter.3.cloned.1.call-done = bf16[256,2560]{1,0:T(8,128)(2,1)} async-done(((bf16[2048,2560]{1,0:T(8,128)(2,1)}), bf16[256,2560]{1,0:T(8,128)(2,1)}) %reduce-scatter.3.cloned.1.call-update) | async-done | bytes 1310736 | tf_op jit(solution)/shard_map/reduce_scatter | solution.py:197
  187.9 4.1 fusion.67
  191.9 2.6 convert_reduce_fusion.6
  194.6 0.0 all-gather.6.cloned.1.call-update
  194.6 0.2 reduce-scatter.5.cloned.1.call-start
  194.8 36.3 %attn_fwd.1 = (bf16[4,80,2048]{2,1,0:T(8,128)(2,1)}, f32[4,80,2048]{2,1,0:T(8,128)}, f32[4,1,2048]{2,1,0:T(1,128)}, f32[4,1,2048]{2,1,0:T(1,128)}) custom-call(bf16[4,80,2048]{2,1,0:T(8,128)(2,1)} %bitcast.139, bf16[4,80,2048]{2,1,0:T(8,128)(2,1)} %bitcast.141, bf16[4,80,2048]{2,1,0:T(8,128)(2,1)} %bitcast.143), custom_call_target="tpu_custom_call" | custom-call | flops 20000000000 | bytes 12000000 | tf_op jit(solution)/shard_map/attn_fwd/pallas_call | solution.py:102
  231.1 21.0 %all-gather.6.cloned.1.call-done = bf16[2048,2560]{1,0:T(8,128)(2,1)} async-done(((bf16[256,2560]{1,0:T(8,128)(2,1)}), bf16[2048,2560]{1,0:T(8,128)(2,1)}) %all-gather.6.cloned.1.call-update) | async-done | bytes 10485776 | tf_op jit(solution)/shard_map/all_gather | solution.py:196
  252.2 8.6 %fusion.69.do_ref = bf16[4,80,2048]{2,1,0:T(8,128)(2,1)} fusion(bf16[4,80,2560]{2,1,0:T(8,128)(2,1)S(1)} %copy-done, bf16[2048,2560]{1,0:T(8,128)(2,1)} %all-gather.6.cloned.1.call-done), kind=kOutput, calls=%fused_computation.87 | convolution fusion | flops 3356098560 | bytes 13434880 | tf_op jit(solution)/shard_map/hed,sd->hes/dot_general | solution.py:215
  260.8 42.8 %attn_bwd.1 = bf16[3,4,80,2048]{3,2,1,0:T(8,128)(2,1)} custom-call(s32[10]{0:T(128)} %constant.28.clone.qi_tab, s32[10]{0:T(128)} %constant.29.clone.ki_tab, bf16[4,80,2048]{2,1,0:T(8,128)(2,1)} %bitcast.140, bf16[4,80,2048]{2,1,0:T(8,128)(2,1)} %bitcast.142, bf16[4,80,2048]{2,1,0:T(8,128)(2,1)} %bitcast.144, bf16[4,80,2048]{2,1,0:T(8,128)(2,1)} %fusion.69.do_ref, ...), custom_call_target="tpu_custom_call" | custom-call | flops 40000000000 | bytes 16000000 | tf_op jit(solution)/shard_map/attn_bwd/pallas_call | solution.py:171
  303.5 16.6 %bitcast_convert_fusion = bf16[2048,2560]{1,0:T(8,128)(2,1)} fusion(bf16[3,4,80,2048]{3,2,1,0:T(8,128)(2,1)} %attn_bwd.1, bf16[3,2560,4,80]{1,3,2,0:T(8,128)(2,1)} %param.28), kind=kOutput, calls=%fused_computation.7 | convolution fusion | flops 10071572480 | bytes 19333120 | tf_op jit(solution)/shard_map/fs,fd->sd/dot_general | solution.py:220
  320.2 0.0 reduce-scatter.5.cloned.1.call-update
  320.2 0.0 copy-start.9
  320.2 0.0 copy-start.12
  320.2 0.0 all-gather.10.cloned.1.call-start
  320.2 0.5 all-gather.10.cloned.1.call-update
  320.8 0.3 all-gather.8.cloned.1.call-start
  321.1 0.4 copy-done.2
  321.5 0.3 convert_reduce_fusion.5
  321.7 0.5 fusion.64
  322.2 70.5 %reduce-scatter.5.cloned.1.call-done = bf16[256,2560]{1,0:T(8,128)(2,1)} async-done(((bf16[2048,2560]{1,0:T(8,128)(2,1)}), bf16[256,2560]{1,0:T(8,128)(2,1)}) %reduce-scatter.5.cloned.1.call-update) | async-done | bytes 1310736 | tf_op jit(solution)/shard_map/reduce_scatter | solution.py:197
  392.8 3.9 fusion.68
  396.7 0.0 all-gather.8.cloned.1.call-update
  396.7 0.2 convert_reduce_fusion.4
  397.0 24.6 %fusion.17 = f32[1280,2560]{1,0:T(8,128)} fusion(bf16[1,2048,2560]{2,1,0:T(8,128)(2,1)} %all-gather.12.cloned.1.call-done, bf16[1,2048,1280]{2,1,0:T(8,128)(2,1)} %param.23), kind=kOutput, calls=%fused_computation.26 | convolution fusion | flops 13447987200 | bytes 28835840 | tf_op jit(solution)/shard_map/sf,sd->fd/dot_general | solution.py:209
  421.6 1.2 convert_reduce_fusion.1
  422.9 0.0 copy-done.13
  422.9 5.3 fusion.13
  428.2 0.1 stack.27
  428.3 24.3 %psum.7 = f32[6,2560]{1,0:T(8,128)} all-reduce(f32[6,2560]{1,0:T(8,128)S(1)} %stack.27), channel_id=1, replica_groups=mesh['dp'=1,'tp'=8] {'tp'}, use_global_device_ids=true, to_apply=%region_18.0 | all-reduce | flops 15360 | bytes 122880 | tf_op jit(solution)/shard_map/psum | solution.py:236
  452.6 3.6 fusion.72
  456.2 19.5 %fusion.78 = f32[2560,1280]{1,0:T(8,128)} fusion(bf16[2048,2560]{1,0:T(8,128)(2,1)} %all-gather.10.cloned.1.call-done, bf16[2048,1280]{1,0:T(8,128)(2,1)} %copy-done.14), kind=kOutput, calls=%fused_computation.101 | convolution fusion | flops 13421772800 | bytes 28835840 | tf_op jit(solution)/shard_map/sd,sf->df/dot_general | solution.py:226
  475.7 37.2 %all-gather.8.cloned.1.call-done = bf16[2048,2560]{1,0:T(8,128)(2,1)} async-done(((bf16[256,2560]{1,0:T(8,128)(2,1)}), bf16[2048,2560]{1,0:T(8,128)(2,1)}) %all-gather.8.cloned.1.call-update) | async-done | bytes 10485776 | tf_op jit(solution)/shard_map/all_gather | solution.py:196
  512.9 16.5 %fusion.23 = f32[3,2560,4,80]{1,3,2,0:T(8,128)} fusion(bf16[3,4,80,2048]{3,2,1,0:T(8,128)(2,1)} %attn_bwd.1, bf16[2048,2560]{1,0:T(8,128)(2,1)} %all-gather.8.cloned.1.call-done), kind=kOutput, calls=%fused_computation.32 | convolution fusion | flops 10066329600 | bytes 24248320 | tf_op jit(solution)/shard_map/fs,sd->fd/dot_general | solution.py:222
  (42 shorter events, 0.2 us)
Async XLA Ops:
  7.2 245.0 %copy-start = (bf16[4,80,2560]{2,1,0:T(8,128)(2,1)S(1)}, bf16[4,80,2560]{2,1,0:T(8,128)(2,1)}, u32[]{:S(2)}) copy-start(bf16[4,80,2560]{2,1,0:T(8,128)(2,1)} %param.29) | copy-start | bytes 4915204
  7.2 62.9 %all-gather.12.cloned.1.call-start = ((), (), s32[]{:S(2)}) async-start(), calls=%async_computation.7 | async-start | bytes 11796480 | tf_op jit(solution)/shard_map/all_gather | solution.py:196
  7.9 179.9 %reduce-scatter.3.cloned.1.call-start = ((), (), s32[]{:S(2)}) async-start(), calls=%async_computation.2 | async-start | bytes 11796480 | tf_op jit(solution)/shard_map/reduce_scatter | solution.py:197
  94.2 2.4 copy-start.14
  115.2 1.3 copy-start.3
  115.3 72.6 %copy-start.10 = (f32[2560]{0:T(1024)S(1)}, f32[2560]{0:T(1024)}, u32[]{:S(2)}) copy-start(f32[2560]{0:T(1024)} %param.26) | copy-start | bytes 30724
  115.3 72.6 %copy-start.11 = (f32[2560]{0:T(1024)S(1)}, f32[2560]{0:T(1024)}, u32[]{:S(2)}) copy-start(f32[2560]{0:T(1024)} %param.27) | copy-start | bytes 30724
  115.3 136.9 %all-gather.6.cloned.1.call-start = ((), (), s32[]{:S(2)}) async-start(), calls=%async_computation.3 | async-start | bytes 11796480 | tf_op jit(solution)/shard_map/all_gather | solution.py:196
  187.9 4.1 copy-start.5
  187.9 4.1 copy-start.7
  194.6 198.2 %reduce-scatter.5.cloned.1.call-start = ((), (), s32[]{:S(2)}) async-start(), calls=%async_computation.4 | async-start | bytes 11796480 | tf_op jit(solution)/shard_map/reduce_scatter | solution.py:197
  320.2 1.3 copy-start.2
  320.2 72.6 %copy-start.9 = (f32[2560]{0:T(1024)S(1)}, f32[2560]{0:T(1024)}, u32[]{:S(2)}) copy-start(f32[2560]{0:T(1024)} %param.24) | copy-start | bytes 30724
  320.2 72.6 %copy-start.12 = (f32[2560]{0:T(1024)S(1)}, f32[2560]{0:T(1024)}, u32[]{:S(2)}) copy-start(f32[2560]{0:T(1024)} %param.25) | copy-start | bytes 30724
  320.2 136.0 %all-gather.10.cloned.1.call-start = ((), (), s32[]{:S(2)}) async-start(), calls=%async_computation.6 | async-start | bytes 11796480 | tf_op jit(solution)/shard_map/all_gather | solution.py:196
  320.8 192.1 %all-gather.8.cloned.1.call-start = ((), (), s32[]{:S(2)}) async-start(), calls=%async_computation.5 | async-start | bytes 11796480 | tf_op jit(solution)/shard_map/all_gather | solution.py:196
  322.2 74.4 %copy-start.6 = (bf16[1,256,2560]{2,1,0:T(8,128)(2,1)S(1)}, bf16[1,256,2560]{2,1,0:T(8,128)(2,1)}, u32[]{:S(2)}) copy-start(bf16[1,256,2560]{2,1,0:T(8,128)(2,1)} %param.19) | copy-start | bytes 3932164
  396.9 25.9 %slice-start = ((s8[10485760]{0:T(1024)(128)(4,1)}), s8[4194304]{0:T(1024)(128)(4,1)S(1)}, s32[]{:S(2)}) async-start(s8[10485760]{0:T(1024)(128)(4,1)} %bitcast.137), calls=%async_computation.8 | async-start | bytes 8388608
  396.9 24.7 %copy-start.8 = (bf16[3,4,80,2048]{3,2,1,0:T(8,128)(2,1)S(1)}, bf16[3,4,80,2048]{3,2,1,0:T(8,128)(2,1)}, u32[]{:S(2)}) copy-start(bf16[3,4,80,2048]{3,2,1,0:T(8,128)(2,1)} %attn_bwd.1) | copy-start | bytes 11796484
  396.9 25.9 %slice-start.1 = ((s8[10485760]{0:T(1024)(128)(4,1)}), s8[4194304]{0:T(1024)(128)(4,1)S(1)}, s32[]{:S(2)}) async-start(s8[10485760]{0:T(1024)(128)(4,1)} %bitcast.137), calls=%async_computation.9 | async-start | bytes 8388608
  397.0 25.9 %slice-start.2 = ((s8[10485760]{0:T(1024)(128)(4,1)}), s8[2097152]{0:T(1024)(128)(4,1)S(1)}, s32[]{:S(2)}) async-start(s8[10485760]{0:T(1024)(128)(4,1)} %bitcast.137), calls=%async_computation.10 | async-start | bytes 4194304
  421.6 1.3 copy-start.13
  422.9 29.7 %copy-start.4 = (bf16[256,2560]{1,0:T(8,128)(2,1)S(1)}, bf16[256,2560]{1,0:T(8,128)(2,1)}, u32[]{:S(2)}) copy-start(bf16[256,2560]{1,0:T(8,128)(2,1)} %get-tuple-element.29) | copy-start | bytes 3932164
  512.9 16.5 %copy-start.1 = (bf16[4,80,2560]{2,1,0:T(8,128)(2,1)S(1)}, bf16[4,80,2560]{2,1,0:T(8,128)(2,1)}, u32[]{:S(2)}) copy-start(bf16[4,80,2560]{2,1,0:T(8,128)(2,1)} %param.29) | copy-start | bytes 4915204
Sparse Core Ops, SparseCore 0:
  9.8 60.2 all-gather.11
  115.4 72.4 reduce-scatter.2
  194.7 57.3 all-gather.5
  320.3 72.4 reduce-scatter.4
  395.0 58.7 all-gather.9
  455.5 57.3 all-gather.7

commit v2 on v0

v2 whole, which is shorter than its diff:
```python
import jax
import jax.numpy as jnp
from jax import lax
from jax.experimental import pallas as pl
from jax.experimental.pallas import tpu as pltpu
from jax.sharding import PartitionSpec as P

LN_EPS = 1e-5
GELU_COEF = 0.044715
GELU_SCALE = 0.7978845608028654
LOG2E = 1.4426950408889634
BLK = 512
F32 = jnp.float32
BF16 = jnp.bfloat16


def layer_norm_fwd(token_rows, norm_gain, norm_bias):
    rows_f32 = token_rows.astype(F32)
    centered = rows_f32 - jnp.mean(rows_f32, axis=-1, keepdims=True)
    inv_std = lax.rsqrt(jnp.mean(centered * centered, axis=-1, keepdims=True) + LN_EPS)
    x_hat = centered * inv_std
    return x_hat, inv_std, (x_hat * norm_gain + norm_bias).astype(BF16)


def layer_norm_bwd(grad_norm, x_hat, inv_std, norm_gain):
    grad_hat = grad_norm * norm_gain
    centered_grad = grad_hat - jnp.mean(grad_hat, axis=-1, keepdims=True)
    return inv_std * (centered_grad - x_hat * jnp.mean(grad_hat * x_hat, axis=-1, keepdims=True))


def gelu_parts(pre_act):
    tanh_val = jnp.tanh(GELU_SCALE * (pre_act + GELU_COEF * pre_act * pre_act * pre_act))
    act_value = 0.5 * pre_act * (1.0 + tanh_val)
    act_slope = 0.5 * (1.0 + tanh_val) + 0.5 * pre_act * (1.0 - tanh_val * tanh_val) * GELU_SCALE * (1.0 + 3.0 * GELU_COEF * pre_act * pre_act)
    return act_value, act_slope


def dot(a, b):
    return jnp.dot(a, b, preferred_element_type=F32)


def causal_fill(scores, fill):
    key_ids = lax.broadcasted_iota(jnp.int32, scores.shape, 0)
    query_ids = lax.broadcasted_iota(jnp.int32, scores.shape, 1)
    return jnp.where(query_ids >= key_ids, scores, fill)


class Place:
    def __init__(self):
        self.group = lax.axis_index('dp')
        self.me = lax.axis_index('tp')
        self.core = self.me % 2
        self.dx = 2 - 4 * ((self.me // 2) % 2)
        self.dy = 4 - 8 * (self.me // 4)
        self.dc = 1 - 2 * self.core
        self.peer = {'X': self.me + self.dx, 'Y': self.me + self.dy, 'C': self.me + self.dc}
        self.block = {'O': self.me, 'X': self.me + self.dx, 'Y': self.me + self.dy, 'D': self.me + self.dx + self.dy}
        self.pair = {key: val // 2 for key, val in self.block.items()}

    def barrier(self):
        sem = pltpu.get_barrier_semaphore()
        for key in 'XYC':
            pl.semaphore_signal(sem, inc=1, device_id=(self.group, self.peer[key]), device_id_type=pl.DeviceIdType.MESH)
        pl.semaphore_wait(sem, 3)


class Links:
    def __init__(self, place, send_sem, recv_sem):
        self.place, self.send_sem, self.recv_sem = place, send_sem, recv_sem
        self.copies = {}

    def send(self, name, src, dst, to):
        at = len(self.copies)
        copy = pltpu.make_async_remote_copy(
            src_ref=src, dst_ref=dst, send_sem=self.send_sem.at[at], recv_sem=self.recv_sem.at[at],
            device_id=(self.place.group, self.place.peer[to]), device_id_type=pl.DeviceIdType.MESH)
        copy.start()
        self.copies[name] = copy

    def wait(self, *names):
        for name in names:
            self.copies[name].wait_recv()

    def finish(self):
        for copy in self.copies.values():
            copy.wait_send()


class Gather:
    COPIES = 10

    def __init__(self, place, own, full, send_sem, recv_sem):
        self.place, self.own, self.full = place, own, full
        self.links = Links(place, send_sem, recv_sem)
        half = own.shape[0] // 2
        self.first, self.second = pl.ds(0, half), pl.ds(half, half)

    def start(self):
        me, full, own, send = self.place.me, self.full, self.own, self.links.send
        send('Xa', own.at[self.first], full.at[me, self.first], 'X')
        send('Yb', own.at[self.second], full.at[me, self.second], 'Y')
        send('Xb', own.at[self.second], full.at[me, self.second], 'X')
        send('Ya', own.at[self.first], full.at[me, self.first], 'Y')
        send('CO', own, full.at[me], 'C')

    def relay(self):
        links, full, block = self.links, self.full, self.place.block
        links.wait('Xa')
        links.send('Da', full.at[block['X'], self.first], full.at[block['X'], self.first], 'Y')
        links.wait('Yb')
        links.send('Db', full.at[block['Y'], self.second], full.at[block['Y'], self.second], 'X')

    def forward(self, key):
        first, second = ('Xb', None) if key == 'X' else ('Ya', None) if key == 'Y' else ('Da', 'Db')
        self.links.wait(first)
        if second:
            self.links.wait(second)
        slot = self.full.at[self.place.block[key]]
        self.links.send('C' + key, slot, slot, 'C')


class Scatter:
    COPIES = 10

    def __init__(self, place, part, crecv, diag_recv, last_recv, send_sem, recv_sem):
        self.place, self.part, self.crecv = place, part, crecv
        self.diag_recv, self.last_recv = diag_recv, last_recv
        self.links = Links(place, send_sem, recv_sem)
        half = part.shape[1] // 2
        self.half = {'a': pl.ds(0, half), 'b': pl.ds(half, half)}

    def add_rows(self, slot, start, count, other, other_start):
        step = 64

        def body(i, carry):
            here = pl.ds(pl.multiple_of(start + i * step, step), step)
            there = pl.ds(pl.multiple_of(other_start + i * step, step), step)
            total = self.part[slot, here, :].astype(F32) + other[there, :].astype(F32)
            self.part[slot, here, :] = total.astype(BF16)
            return carry

        lax.fori_loop(0, count // step, body, 0)

    def swap(self, key):
        at = 'OXYD'.index(key)
        self.links.send('C' + key, self.part.at[self.place.block[key] + self.place.dc], self.crecv.at[at], 'C')

    def add_pair(self, key):
        self.links.wait('C' + key)
        at = 'OXYD'.index(key)
        self.add_rows(self.place.block[key], 0, self.part.shape[1], self.crecv.at[at], 0)

    def send_half(self, key, half):
        at = self.half[half]
        src = self.part.at[self.place.block[key], at]
        self.links.send(key + half, src, self.last_recv.at['XY'.index(key), at], key)

    def send_diag(self):
        for i, (key, half) in enumerate((('X', 'a'), ('Y', 'b'))):
            src = self.part.at[self.place.block['D'], self.half[half]]
            self.links.send('D' + half, src, self.diag_recv.at[i], key)

    def add_diag(self):
        rows = self.part.shape[1] // 2
        self.links.wait('Da')
        self.add_rows(self.place.block['Y'], 0, rows, self.diag_recv.at[0], 0)
        self.links.wait('Db')
        self.add_rows(self.place.block['X'], rows, rows, self.diag_recv.at[1], 0)
        self.send_half('Y', 'a')
        self.send_half('X', 'b')

    def wait_last(self):
        self.links.wait('Xa', 'Xb', 'Ya', 'Yb', 'CO')

    def run(self, first_half, second_half):
        second_half('D')
        self.swap('D')
        first_half('X')
        self.add_pair('D')
        self.send_diag()
        second_half('X')
        self.swap('X')
        first_half('Y')
        self.add_pair('X')
        self.send_half('X', 'a')
        second_half('Y')
        self.swap('Y')
        first_half('O')
        self.add_pair('Y')
        self.send_half('Y', 'b')
        second_half('O')
        self.swap('O')
        self.add_diag()
        self.wait_last()

    def total(self, at):
        me = self.place.me
        return (self.part[me, at, :].astype(F32) + self.crecv[0, at, :].astype(F32)
                + self.last_recv[0, at, :].astype(F32) + self.last_recv[1, at, :].astype(F32))


def gelu_slope(pre_act):
    tanh_val = jnp.tanh(GELU_SCALE * (pre_act + GELU_COEF * pre_act * pre_act * pre_act))
    return 0.5 * (1.0 + tanh_val) + 0.5 * pre_act * (1.0 - tanh_val * tanh_val) * GELU_SCALE * (1.0 + 3.0 * GELU_COEF * pre_act * pre_act)


def layer_norm_hat(rows_f32):
    centered = rows_f32 - jnp.mean(rows_f32, axis=-1, keepdims=True)
    inv_std = lax.rsqrt(jnp.mean(centered * centered, axis=-1, keepdims=True) + LN_EPS)
    return centered * inv_std, inv_std


LN_ROWS = 32
TILE = 1280
VMEM = pl.BlockSpec(memory_space=pltpu.VMEM)
HBM = pl.BlockSpec(memory_space=pl.ANY)
DMA = pltpu.SemaphoreType.DMA
shape = jax.ShapeDtypeStruct


def tile_at(i, size):
    return pl.ds(pl.multiple_of(i * size, size), size)


def loop(count, body, start=0):
    def step(i, carry):
        body(i)
        return carry

    lax.fori_loop(start, count, step, 0)


def comm_call(kernel, name, ident, flops, args, in_specs, out_shape, out_specs, scratch):
    return pl.pallas_call(
        kernel, in_specs=in_specs, out_specs=out_specs, out_shape=out_shape, scratch_shapes=scratch, name=name,
        compiler_params=pltpu.CompilerParams(collective_id=ident, has_side_effects=True, vmem_limit_bytes=66_000_000),
        cost_estimate=pl.CostEstimate(flops=flops, bytes_accessed=40_000_000, transcendentals=3_000_000),
    )(*args)


def fwd_kernel(dout_ref, q_ref, k_ref, v_ref, dfull, ctx_ref, wide_ref, max_ref, inv_ref, k_rows, strip, own_sem, *comm_sems):
    place = Place()
    place.barrier()
    gather = Gather(place, dout_ref, dfull, *comm_sems)
    gather.start()
    own_copy = pltpu.make_async_copy(dout_ref, dfull.at[place.me], own_sem)
    own_copy.start()
    heads, dim, seq = q_ref.shape
    exp_scale = dim ** -0.5 * LOG2E

    def head(h):
        k_rows[...] = k_ref[h].T

        def query_block(qi):
            q_at = tile_at(qi, BLK)
            q_blk = q_ref[h, :, q_at]

            def score_step(ki, run_max):
                at = tile_at(ki, BLK)
                blk = dot(k_rows[at, :], q_blk)
                strip[at, :] = blk
                return jnp.maximum(run_max, jnp.max(blk, axis=0, keepdims=True))

            diag = causal_fill(dot(k_rows[q_at, :], q_blk), -1e30)
            strip[q_at, :] = diag
            row_max = lax.fori_loop(0, qi, score_step, jnp.max(diag, axis=0, keepdims=True))

            def exp_step(ki, run_sum):
                at = tile_at(ki, BLK)
                probs = jnp.exp2((strip[at, :] - row_max) * exp_scale)
                strip[at, :] = probs
                return run_sum + jnp.sum(probs, axis=0, keepdims=True)

            row_inv = 1.0 / lax.fori_loop(0, qi + 1, exp_step, jnp.zeros_like(row_max))

            def ctx_step(ki, carry):
                high, low = carry
                at = tile_at(ki, BLK)
                probs = strip[at, :] * row_inv
                probs_low = probs.astype(BF16)
                rest = (probs - probs_low.astype(F32)).astype(BF16)
                v_blk = v_ref[h, :, at]
                return high + dot(v_blk, probs_low), low + dot(v_blk, rest)

            zero = jnp.zeros((dim, BLK), F32)
            high, low = lax.fori_loop(0, qi + 1, ctx_step, (zero, zero))
            ctx_ref[h, :, q_at] = high.astype(BF16)
            wide_ref[h, :, q_at] = high + low
            max_ref[h, :, q_at] = row_max
            inv_ref[h, :, q_at] = row_inv

        loop(seq // BLK, query_block)

    for h in range(heads):
        head(h)
        if h == 1:
            gather.relay()
        if h == 2:
            gather.forward('X')
            gather.forward('Y')
    gather.forward('D')
    gather.links.wait('CO', 'CX', 'CY', 'CD')
    own_copy.wait()
    gather.links.finish()


def fwd_call(d_out, q_t, k_t, v_t):
    heads, dim, seq = q_t.shape
    rows, model = d_out.shape
    return comm_call(
        fwd_kernel, "attn_fwd", 0, 40_000_000_000, (d_out, q_t, k_t, v_t), [VMEM] * 4,
        [shape((seq // rows, rows, model), BF16), shape((heads, dim, seq), BF16), shape((heads, dim, seq), F32),
         shape((heads, 1, seq), F32), shape((heads, 1, seq), F32)],
        [HBM] + [VMEM] * 4,
        [pltpu.VMEM((seq, dim), BF16), pltpu.VMEM((seq, BLK), F32), DMA(())] + [DMA((10,))] * 2)


def dot_t(a, b):
    return lax.dot_general(a, b, (((1,), (1,)), ((), ())), preferred_element_type=F32)


def mlp_kernel(dfull, dout_ref, mid_ref, gain_ref, z_ref, w2_ref, w1_ref,
               dx1_ref, dz_ref, gb1_ref, vec_ref,
               w2v, w1v, zv, dzv, ybuf, part, crecv, diag_recv, last_recv,
               load_sem, y_sem, dz_sem, *comm_sems):
    place = Place()
    place.barrier()
    rows, model = dout_ref.shape
    hidden = w2v.shape[0]
    scatter = Scatter(place, part, crecv, diag_recv, last_recv, *comm_sems)

    def load_pair(key):
        copy = pltpu.make_async_copy(dfull.at[pl.ds(2 * place.pair[key], 2)], ybuf.at['DXYO'.index(key) % 2],
                                     y_sem.at['DXYO'.index(key)])
        copy.start()
        return copy

    pairs = {'D': load_pair('D')}
    loads = [pltpu.make_async_copy(src, dst, load_sem.at[i])
             for i, (src, dst) in enumerate(((w2_ref, w2v), (z_ref, zv), (w1_ref, w1v)))]
    for copy in loads:
        copy.start()
    pairs['X'] = load_pair('X')
    gb1_ref[...] = jnp.zeros_like(gb1_ref)
    vec_ref[...] = jnp.zeros_like(vec_ref)
    dz_copies = []

    def grad_act(key):
        slot = 'DXYO'.index(key) % 2
        at = tile_at(place.pair[key], 2 * rows)
        pairs[key].wait()

        def body(n):
            cols = tile_at(n, TILE)
            acc = dot_t(ybuf[slot].reshape(2 * rows, model), w2v[cols, :])
            grad = (acc * gelu_slope(zv[at, cols].astype(F32))).astype(BF16)
            dzv[at, cols] = grad
            gb1_ref[:, cols] += jnp.sum(grad.astype(F32), axis=0, keepdims=True)

        loop(hidden // TILE, body)
        following = {'D': 'Y', 'X': 'O'}.get(key)
        if following:
            pairs[following] = load_pair(following)
        copy = pltpu.make_async_copy(dzv.at[at], dz_ref.at[at], dz_sem.at['DXYO'.index(key)])
        copy.start()
        dz_copies.append(copy)

    def grad_norm(key):
        at = tile_at(place.pair[key], 2 * rows)
        slot = 2 * place.pair[key]

        def body(n):
            cols = tile_at(n, TILE)
            acc = dot_t(dzv[at, :], w1v[cols, :]).astype(BF16)
            part[slot, :, cols] = acc[:rows]
            part[slot + 1, :, cols] = acc[rows:]

        loop(model // TILE, body)

    loads[0].wait()
    loads[1].wait()
    grad_act('D')
    loads[2].wait()
    scatter.run(grad_act, grad_norm)

    gain = gain_ref[...]

    def norm_rows(i):
        at = tile_at(i, LN_ROWS)
        grad = scatter.total(at)
        x_hat, inv_std = layer_norm_hat(mid_ref[at, :].astype(F32))
        dout_rows = dout_ref[at, :].astype(F32)
        mid = (dout_rows + layer_norm_bwd(grad, x_hat, inv_std, gain)).astype(BF16)
        dx1_ref[at, :] = mid
        for row, val in enumerate((grad * x_hat, grad, mid.astype(F32), dout_rows)):
            vec_ref[row:row + 1, :] += jnp.sum(val, axis=0, keepdims=True)

    loop(rows // LN_ROWS, norm_rows)
    for copy in dz_copies:
        copy.wait()
    scatter.links.finish()


def scatter_scratch(rows, model):
    return [pltpu.VMEM((8, rows, model), BF16), pltpu.VMEM((4, rows, model), BF16),
            pltpu.VMEM((2, rows // 2, model), BF16), pltpu.VMEM((2, rows, model), BF16)]


def mlp_call(dfull, d_out, x_mid, ln2_gain, z_saved, w2, w1):
    rows, model = d_out.shape
    seq, hidden = z_saved.shape
    return comm_call(
        mlp_kernel, "mlp_grads", 1, 60_000_000_000, (dfull, d_out, x_mid, ln2_gain[None], z_saved, w2, w1),
        [HBM] + [VMEM] * 3 + [HBM] * 3,
        [shape((rows, model), BF16), shape((seq, hidden), BF16), shape((1, hidden), F32), shape((8, model), F32)],
        [VMEM, HBM, VMEM, VMEM],
        [pltpu.VMEM((hidden, model), BF16), pltpu.VMEM((model, hidden), BF16),
         pltpu.VMEM((seq, hidden), BF16), pltpu.VMEM((seq, hidden), BF16), pltpu.VMEM((2, 2, rows, model), BF16)]
        + scatter_scratch(rows, model) + [DMA((3,)), DMA((4,)), DMA((4,))] + [DMA((10,))] * 2)


def ctx_kernel(dx1_ref, wo_ref, mfull, do_ref, mbuf, own_sem, m_sem, *comm_sems):
    place = Place()
    place.barrier()
    rows, model = dx1_ref.shape
    gather = Gather(place, dx1_ref, mfull, *comm_sems)
    gather.start()
    own_copy = pltpu.make_async_copy(dx1_ref, mfull.at[place.me], own_sem)
    own_copy.start()

    def grad_ctx(key):
        copy = pltpu.make_async_copy(mfull.at[pl.ds(2 * place.pair[key], 2)], mbuf, m_sem.at['OXYD'.index(key)])
        copy.start()
        copy.wait()
        do_ref[:, tile_at(place.pair[key], 2 * rows)] = dot_t(wo_ref[...], mbuf[...].reshape(2 * rows, model)).astype(BF16)

    gather.links.wait('CO')
    own_copy.wait()
    grad_ctx('O')
    gather.relay()
    gather.forward('X')
    gather.forward('Y')
    gather.links.wait('CX')
    grad_ctx('X')
    gather.links.wait('CY')
    grad_ctx('Y')
    gather.forward('D')
    gather.links.wait('CD')
    grad_ctx('D')
    gather.links.finish()


def ctx_call(dx1, w_rows, seq):
    rows, model = dx1.shape
    feats = w_rows.shape[0]
    return comm_call(
        ctx_kernel, "ctx_grads", 2, 8_000_000_000, (dx1, w_rows), [VMEM] * 2,
        [shape((seq // rows, rows, model), BF16), shape((feats, seq), BF16)], [HBM, VMEM],
        [pltpu.VMEM((2, rows, model), BF16), DMA(()), DMA((4,))] + [DMA((10,))] * 2)


def bwd_kernel(h1_ref, h2_ref, q_ref, k_ref, v_ref, do_ref, wide_ref, max_ref, inv_ref,
               h1full, h2full, out_ref,
               k_rows, v_rows, q_rows, do_rows, delta, dq_acc, dk_acc, dv_acc, own_sem, *comm_sems):
    place = Place()
    place.barrier()
    gather1 = Gather(place, h1_ref, h1full, *comm_sems[0:2])
    gather2 = Gather(place, h2_ref, h2full, *comm_sems[2:4])
    gather1.start()
    own_copies = [pltpu.make_async_copy(src, dst.at[place.me], own_sem.at[i])
                  for i, (src, dst) in enumerate(((h1_ref, h1full), (h2_ref, h2full)))]
    for copy in own_copies:
        copy.start()
    heads, dim, seq = q_ref.shape
    blocks = seq // BLK
    scale = dim ** -0.5
    exp_scale = scale * LOG2E

    def head(h):
        k_rows[...] = k_ref[h].T
        v_rows[...] = v_ref[h].T
        q_rows[...] = q_ref[h].T
        do_rows[...] = do_ref[h].T
        delta[...] = jnp.sum(do_ref[h].astype(F32) * wide_ref[h], axis=0, keepdims=True)
        dq_acc[...] = jnp.zeros_like(dq_acc)
        dk_acc[...] = jnp.zeros_like(dk_acc)
        dv_acc[...] = jnp.zeros_like(dv_acc)

        def block(qi, ki, on_diag):
            q_at, k_at = tile_at(qi, BLK), tile_at(ki, BLK)
            scores = dot(k_rows[k_at, :], q_ref[h, :, q_at])
            if on_diag:
                scores = causal_fill(scores, -1e30)
            probs = jnp.exp2((scores - max_ref[h, :, q_at]) * exp_scale) * inv_ref[h, :, q_at]
            grad_probs = dot(v_rows[k_at, :], do_ref[h, :, q_at])
            dv_acc[k_at, :] += dot(probs.astype(BF16), do_rows[q_at, :])
            grad_scores = (probs * (grad_probs - delta[:, q_at]) * scale).astype(BF16)
            dk_acc[k_at, :] += dot(grad_scores, q_rows[q_at, :])
            dq_acc[:, q_at] += dot(k_ref[h, :, k_at], grad_scores)

        loop(blocks, lambda i: block(i, i, True))
        loop(blocks, lambda ki: loop(blocks, lambda qi: block(qi, ki, False), ki + 1))
        out_ref[0, h] = dq_acc[...].astype(BF16)
        out_ref[1, h] = dk_acc[...].T.astype(BF16)
        out_ref[2, h] = dv_acc[...].T.astype(BF16)

    for h in range(heads):
        head(h)
        if h == 0:
            gather1.relay()
            gather2.start()
        if h == 2:
            gather1.forward('X')
            gather1.forward('Y')
    gather1.forward('D')
    gather2.relay()
    gather2.forward('X')
    gather2.forward('Y')
    gather2.forward('D')
    for gather in (gather1, gather2):
        gather.links.wait('CO', 'CX', 'CY', 'CD')
        gather.links.finish()
    for copy in own_copies:
        copy.wait()


def bwd_call(h1, h2, q_t, k_t, v_t, do_t, wide, row_max, row_inv):
    heads, dim, seq = q_t.shape
    rows, model = h1.shape
    full = shape((seq // rows, rows, model), BF16)
    turned = pltpu.VMEM((seq, dim), BF16)
    return comm_call(
        bwd_kernel, "attn_bwd", 3, 60_000_000_000, (h1, h2, q_t, k_t, v_t, do_t, wide, row_max, row_inv), [VMEM] * 9,
        [full, full, shape((3, heads, dim, seq), BF16)], [HBM, HBM, VMEM],
        [turned] * 4 + [pltpu.VMEM((1, seq), F32), pltpu.VMEM((dim, seq), F32), pltpu.VMEM((seq, dim), F32),
                        pltpu.VMEM((seq, dim), F32), DMA((2,))] + [DMA((10,))] * 4)


def qkv_kernel(qkv_ref, w_ref, dx1_ref, x_ref, gain_ref, vec_ref, dx_ref, vsum_ref,
               turned, part, crecv, diag_recv, last_recv, vsend, vrecv, vsem, *comm_sems):
    place = Place()
    place.barrier()
    rows, model = dx1_ref.shape
    scatter = Scatter(place, part, crecv, diag_recv, last_recv, *comm_sems)

    def turn(key):
        turned[...] = qkv_ref[:, tile_at(place.pair[key], 2 * rows)].T

    def grad_norm(key):
        slot = 2 * place.pair[key]

        def body(n):
            cols = tile_at(n, TILE)
            acc = dot(turned[...], w_ref[:, cols]).astype(BF16)
            part[slot, :, cols] = acc[:rows]
            part[slot + 1, :, cols] = acc[rows:]

        loop(model // TILE, body)

    turn('D')
    scatter.run(turn, grad_norm)
    gain = gain_ref[...]
    vsum_ref[...] = vec_ref[...]

    def norm_rows(i):
        at = tile_at(i, LN_ROWS)
        grad = scatter.total(at)
        x_hat, inv_std = layer_norm_hat(x_ref[at, :].astype(F32))
        dx_ref[at, :] = (dx1_ref[at, :].astype(F32) + layer_norm_bwd(grad, x_hat, inv_std, gain)).astype(BF16)
        vsum_ref[4:5, :] += jnp.sum(grad * x_hat, axis=0, keepdims=True)
        vsum_ref[5:6, :] += jnp.sum(grad, axis=0, keepdims=True)

    loop(rows // LN_ROWS, norm_rows)
    for i, key in enumerate('CXY'):
        vsend[i] = vsum_ref[...]
        copy = pltpu.make_async_remote_copy(
            src_ref=vsend.at[i], dst_ref=vrecv.at[i], send_sem=vsem.at[i], recv_sem=vsem.at[3 + i],
            device_id=(place.group, place.peer[key]), device_id_type=pl.DeviceIdType.MESH)
        copy.start()
        copy.wait()
        vsum_ref[...] += vrecv[i]
    scatter.links.finish()


def qkv_call(qkv_rows, w_rows, dx1, x_in, ln1_gain, vec):
    rows, model = dx1.shape
    feats = qkv_rows.shape[0]
    return comm_call(
        qkv_kernel, "qkv_grads", 4, 20_000_000_000, (qkv_rows, w_rows, dx1, x_in, ln1_gain[None], vec), [VMEM] * 6,
        [shape((rows, model), BF16), shape((8, model), F32)], [VMEM] * 2,
        [pltpu.VMEM((2 * rows, feats), BF16)] + scatter_scratch(rows, model)
        + [pltpu.VMEM((3, 8, model), F32), pltpu.VMEM((3, 8, model), F32), DMA((6,))] + [DMA((10,))] * 2)


def solution(mesh):
    def local_backward(x_in, x_mid, d_out, q_saved, k_saved, v_saved, z_saved, ln1_gain, ln1_bias, ln2_gain, ln2_bias, w_qkv, w_proj, w_fc1, w_fc2):
        x_in, x_mid, d_out, z_saved = x_in[0], x_mid[0], d_out[0], z_saved[0]
        heads, dim = q_saved.shape[2:]
        seq, model = z_saved.shape[0], x_in.shape[1]
        q_t, k_t, v_t = (v[0].transpose(1, 2, 0) for v in (q_saved, k_saved, v_saved))
        _, _, h2_local = layer_norm_fwd(x_mid, ln2_gain, ln2_bias)
        _, _, h1_local = layer_norm_fwd(x_in, ln1_gain, ln1_bias)
        dfull, ctx_t, wide_t, row_max, row_inv = fwd_call(d_out, q_t, k_t, v_t)
        dx1, grad_pre, grad_bfc1, vec = mlp_call(dfull, d_out, x_mid, ln2_gain, z_saved, w_fc2, w_fc1)
        mfull, do_t = ctx_call(dx1, w_proj.reshape(heads * dim, model), seq)
        h1_full, h2_full, qkv_t = bwd_call(h1_local, h2_local, q_t, k_t, v_t, do_t.reshape(heads, dim, seq), wide_t, row_max, row_inv)
        dout_full, mid_full, h1_full, h2_full = (v.reshape(seq, model) for v in (dfull, mfull, h1_full, h2_full))
        qkv_rows = qkv_t.reshape(3 * heads * dim, seq)
        w_rows = w_qkv.transpose(0, 2, 3, 1).reshape(3 * heads * dim, model)
        grad_x, vec_sum = qkv_call(qkv_rows, w_rows, dx1, x_in, ln1_gain, vec)
        act_value, _ = gelu_parts(z_saved.astype(F32))
        grad_wfc2 = jnp.einsum('sf,sd->fd', act_value.astype(BF16), dout_full, preferred_element_type=F32)
        grad_wproj = jnp.einsum('hes,sd->hed', ctx_t, mid_full, preferred_element_type=F32)
        grad_wqkv = jnp.einsum('fs,sd->fd', qkv_rows, h1_full, preferred_element_type=F32)
        grad_wqkv = grad_wqkv.reshape(3, heads, dim, model).transpose(0, 3, 1, 2)
        grad_bqkv = jnp.sum(qkv_t, axis=3, dtype=F32)
        grad_wfc1 = jnp.einsum('sd,sf->df', h2_full, grad_pre, preferred_element_type=F32)
        grad_vecs = jnp.concatenate([vec_sum[4:6], vec_sum[:4]])
        return grad_x[None], grad_wqkv, grad_bqkv, grad_wproj, grad_wfc1, grad_bfc1[0], grad_wfc2, grad_vecs

    tok_spec = P('dp', 'tp', None)
    head_spec = P('dp', None, 'tp', None)
    in_specs = (tok_spec, tok_spec, tok_spec, head_spec, head_spec, head_spec, P('dp', None, 'tp'),
                P(None), P(None), P(None), P(None),
                P(None, None, 'tp', None), P('tp', None, None), P(None, 'tp'), P('tp', None))
    out_specs = (tok_spec, P('dp', None, 'tp', None), P('dp', 'tp', None), P(('dp', 'tp'), None, None),
                 P('dp', 'tp'), P(('dp', 'tp')), P(('dp', 'tp'), None), P('dp', None))
    return jax.shard_map(local_backward, mesh=mesh, in_specs=in_specs, out_specs=out_specs, check_vma=False)
```

time: 730 us -> 443 us (0.61)
  Pallas kernels: 0 us -> 349 us
  matrix products: 406 us -> 71 us
  waiting for transfers between devices: 251 us -> 0 us
  blocking collectives: 23.5 us -> 0 us
  between operations: 14.8 us -> 1.23 us
  other arithmetic: 22.3 us -> 10.2 us
    pallas_call x0 -> x5, Pallas kernels: none -> 349 us  [comm_call(): pl.pallas_call(kernel, in_specs=in_specs, out_specs=out_specs, out_shape=...]
    dot_general x12 -> x4, matrix products: 369 us -> 71 us  [the longest x1 24.8 us: local_backward(): jnp.einsum('sf,sd->fd', act_value.astype(BF16), dout_full, preferred_elem...]
    reduce_scatter x2 -> x0, waiting for transfers between devices: 141 us -> none  [the longest x1 70.5 us: local_backward(): lax.psum_scatter(h2_partial, 'tp', scatter_dimension=1, tiled=True)]
    all_gather x4 -> x0, waiting for transfers between devices: 108 us -> none  [the longest x1 62.1 us: local_backward(): dout_full = lax.all_gather(d_out, 'tp', axis=1, tiled=True)]
    sub x1 -> x0, matrix products: 36.2 us -> none  [attention_grads(): attn_probs = jax.nn.softmax(scores, axis=-1)]
    psum x1 -> x0, blocking collectives: 23.5 us -> none  [local_backward(): grad_vecs = lax.psum(vec_partial, 'tp')]
    reduce_sum x4 -> x1, other arithmetic: 13.1 us -> 1.21 us  [local_backward(): grad_bqkv = jnp.sum(qkv_t, axis=3, dtype=F32)]
  transfers between devices with their start and end apart: 6 -> 0, of which waited for: 5 -> 0; matrix products, arithmetic and copies ran while one was open for 17% -> 0% of each run, Pallas kernels for 0% -> 0%
where the time goes in v2:
time: 443 us; the launch traced here: 434 us
  Pallas kernels  349 us (79%)
  matrix products  71 us (16%)
  other arithmetic  10.2 us (2%)
    pallas_call x5, Pallas kernels, comm_call(): pl.pallas_call(kernel, in_specs=in_specs, out_specs=out_specs, out_shape=...  349 us
    dot_general x1, matrix products, local_backward(): jnp.einsum('sf,sd->fd', act_value.astype(BF16), dout_full, preferred_elem...  24.8 us
    dot_general x1, matrix products, local_backward(): jnp.einsum('sd,sf->df', h2_full, grad_pre, preferred_element_type=F32)  20 us
    dot_general x1, matrix products, local_backward(): jnp.einsum('fs,sd->fd', qkv_rows, h1_full, preferred_element_type=F32)  16.6 us
    dot_general x1, matrix products, local_backward(): jnp.einsum('hes,sd->hed', ctx_t, mid_full, preferred_element_type=F32)  9.64 us

profile of v2, /device:TPU:0, one launch (start us, length us, event | category | flops | bytes accessed | tf_op | source)
XLA Modules:
  0.0 434.1 jit_solution(11592865836287226351)
XLA Ops:
  0.6 0.0 copy-start
  0.6 0.0 copy-start.1
  0.7 0.0 copy-start.4
  0.7 0.0 copy-start.5
  0.7 0.0 copy-start.7
  0.7 0.0 copy-start.8
  0.7 1.7 convert_reduce_fusion.2
  2.4 1.8 fusion.20
  4.2 0.0 copy-done
  4.2 0.3 convert_reduce_fusion.1
  4.5 0.5 fusion.16
  5.0 0.0 copy-done.5
  5.0 0.6 broadcast_in_dim.7.gain_ref
  5.6 0.0 copy-done.4
  5.6 0.6 broadcast_in_dim.6.gain_ref
  6.2 0.0 copy-done.1
  6.2 0.0 copy-done.7
  6.2 0.0 copy-done.8
  6.2 2.7 fusion.19
  8.9 54.7 %attn_fwd.1 = (bf16[8,256,2560]{2,1,0:T(8,128)(2,1)}, bf16[4,80,2048]{2,1,0:T(8,128)(2,1)}, f32[4,80,2048]{2,1,0:T(8,128)}, f32[4,1,2048]{2,1,0:T(1,128)}, f32[4,1,2048]{2,1,0:T(1,128)}) custom-call(bf16[256,2560]{1,0:T(8,128)(2,1)} %bitcast.55, bf16[4,80,2048]{2,1,0:T(8,128)(2,1)} %bitcast.57, bf16[4,80,2048]{2,1,0:T(8,128)(2,1)} %bitcast.59, ...), custom_call_target="tpu_custom_call" | custom-call | flops 40000000000 | bytes 40000000 | tf_op jit(solution)/shard_map/attn_fwd/pallas_call | solution.py:234
  63.6 75.8 %mlp_grads.1 = (bf16[256,2560]{1,0:T(8,128)(2,1)}, bf16[2048,1280]{1,0:T(8,128)(2,1)}, f32[1,1280]{1,0:T(1,128)}, f32[8,2560]{1,0:T(8,128)}) custom-call(bf16[8,256,2560]{2,1,0:T(8,128)(2,1)} %get-tuple-element.24.dfull, bf16[256,2560]{1,0:T(8,128)(2,1)} %bitcast.56, bf16[256,2560]{1,0:T(8,128)(2,1)} %bitcast.48, f32[1,2560]{1,0:T(1,128)} %broadcast_in_dim.6.gain_ref, ...), custom_call_target="tpu_custom_call" | custom-call | flops 60000002048 | bytes 40000000 | tf_op jit(solution)/shard_map/mlp_grads/pallas_call | solution.py:234
  139.5 1.3 reduce
  140.8 51.8 %ctx_grads.1 = (bf16[8,256,2560]{2,1,0:T(8,128)(2,1)}, bf16[320,2048]{1,0:T(8,128)(2,1)}) custom-call(bf16[256,2560]{1,0:T(8,128)(2,1)} %get-tuple-element.25.dx1_ref, bf16[320,2560]{1,0:T(8,128)(2,1)} %bitcast.54), custom_call_target="tpu_custom_call" | custom-call | flops 8000000000 | bytes 40000000 | tf_op jit(solution)/shard_map/ctx_grads/pallas_call | solution.py:234
  192.6 9.6 %fusion.28 = f32[4,80,2560]{2,1,0:T(8,128)} fusion(bf16[4,80,2048]{2,1,0:T(8,128)(2,1)} %get-tuple-element.34, bf16[2048,2560,1]{1,0,2:T(8,128)(2,1)} %bitcast.66), kind=kOutput, calls=%fused_computation.43 | convolution fusion | flops 3355443200 | bytes 15073280 | tf_op jit(solution)/shard_map/hes,sd->hed/dot_general | solution.py:613
  202.2 24.8 %fusion.6 = f32[1280,2560]{1,0:T(8,128)} fusion(bf16[2048,2560]{1,0:T(8,128)(2,1)} %bitcast.63, bf16[1,2048,1280]{2,1,0:T(8,128)(2,1)} %param.21), kind=kOutput, calls=%fused_computation.13 | convolution fusion | flops 13447987200 | bytes 28835840 | tf_op jit(solution)/shard_map/sf,sd->fd/dot_general | solution.py:612
  227.1 97.5 %attn_bwd.1 = (bf16[8,256,2560]{2,1,0:T(8,128)(2,1)}, bf16[8,256,2560]{2,1,0:T(8,128)(2,1)}, bf16[3,4,80,2048]{3,2,1,0:T(8,128)(2,1)}) custom-call(bf16[256,2560]{1,0:T(8,128)(2,1)} %get-tuple-element.41.h1_ref, bf16[256,2560]{1,0:T(8,128)(2,1)} %get-tuple-element.40.h2_ref, bf16[4,80,2048]{2,1,0:T(8,128)(2,1)} %bitcast.58, bf16[4,80,2048]{2,1,0:T(8,128)(2,1)} %bitcast.60, ...), custom_call_target="tpu_custom_call" | custom-call | flops 60000002048 | bytes 40000000 | tf_op jit(solution)/shard_map/attn_bwd/pallas_call | solution.py:234
  324.6 69.5 %qkv_grads.1 = (bf16[256,2560]{1,0:T(8,128)(2,1)}, f32[8,2560]{1,0:T(8,128)}) custom-call(bf16[960,2048]{1,0:T(8,128)(2,1)} %bitcast.50, bf16[960,2560]{1,0:T(8,128)(2,1)} %bitcast.53, bf16[256,2560]{1,0:T(8,128)(2,1)} %get-tuple-element.25.dx1_ref, bf16[256,2560]{1,0:T(8,128)(2,1)} %bitcast.49, f32[1,2560]{1,0:T(1,128)} %broadcast_in_dim.7.gain_ref, ...), custom_call_target="tpu_custom_call" | custom-call | flops 20000000000 | bytes 40000000 | tf_op jit(solution)/shard_map/qkv_grads/pallas_call | solution.py:234
  394.1 0.0 copy-start.2
  394.1 0.0 copy-start.9
  394.2 16.6 %convolution_bitcast_fusion = f32[3,2560,4,80]{1,3,2,0:T(8,128)} fusion(bf16[3,4,80,2048]{3,2,1,0:T(8,128)(2,1)} %get-tuple-element.30, bf16[2048,2560,1,1]{1,0,3,2:T(8,128)(2,1)} %bitcast.65), kind=kOutput, calls=%fused_computation.11 | convolution fusion | flops 10066329600 | bytes 24248320 | tf_op jit(solution)/shard_map/fs,sd->fd/dot_general | solution.py:614
  410.7 0.0 copy-done.2
  410.7 1.2 convert_reduce_fusion
  411.9 0.0 copy-done.9
  411.9 0.0 copy-start.6
  411.9 0.0 copy-start.3
  411.9 20.0 %fusion.29 = f32[2560,1280]{1,0:T(8,128)} fusion(bf16[2048,2560]{1,0:T(8,128)(2,1)S(1)} %bitcast.64, bf16[2048,1280]{1,0:T(8,128)(2,1)} %get-tuple-element.37), kind=kOutput, calls=%fused_computation.44 | convolution fusion | flops 13421772800 | bytes 28835840 | tf_op jit(solution)/shard_map/sd,sf->df/dot_general | solution.py:617
  431.9 0.0 copy-done.6
  431.9 0.7 pad_maximum_fusion
  432.6 0.0 copy-done.3
  432.6 1.1 copy.25
  (6 shorter events, 0.0 us)
Async XLA Ops:
  0.6 3.6 copy-start
  0.6 5.6 %copy-start.1 = (bf16[1,256,2560]{2,1,0:T(8,128)(2,1)S(1)}, bf16[1,256,2560]{2,1,0:T(8,128)(2,1)}, u32[]{:S(2)}) copy-start(bf16[1,256,2560]{2,1,0:T(8,128)(2,1)} %param.15) | copy-start | bytes 3932164
  0.7 5.0 %copy-start.4 = (f32[2560]{0:T(1024)S(1)}, f32[2560]{0:T(1024)}, u32[]{:S(2)}) copy-start(f32[2560]{0:T(1024)} %param.24) | copy-start | bytes 30724
  0.7 4.3 %copy-start.5 = (f32[2560]{0:T(1024)S(1)}, f32[2560]{0:T(1024)}, u32[]{:S(2)}) copy-start(f32[2560]{0:T(1024)} %param.22) | copy-start | bytes 30724
  0.7 5.6 %copy-start.7 = (f32[2560]{0:T(1024)S(1)}, f32[2560]{0:T(1024)}, u32[]{:S(2)}) copy-start(f32[2560]{0:T(1024)} %param.25) | copy-start | bytes 30724
  0.7 5.6 %copy-start.8 = (f32[2560]{0:T(1024)S(1)}, f32[2560]{0:T(1024)}, u32[]{:S(2)}) copy-start(f32[2560]{0:T(1024)} %param.23) | copy-start | bytes 30724
  394.1 16.6 %copy-start.2 = (bf16[3,4,80,2048]{3,2,1,0:T(8,128)(2,1)S(1)}, bf16[3,4,80,2048]{3,2,1,0:T(8,128)(2,1)}, u32[]{:S(2)}) copy-start(bf16[3,4,80,2048]{3,2,1,0:T(8,128)(2,1)} %get-tuple-element.30) | copy-start | bytes 11796484
  394.1 17.8 %copy-start.9 = (bf16[8,256,2560]{2,1,0:T(8,128)(2,1)S(1)}, bf16[8,256,2560]{2,1,0:T(8,128)(2,1)}, u32[]{:S(2)}) copy-start(bf16[8,256,2560]{2,1,0:T(8,128)(2,1)} %get-tuple-element.36) | copy-start | bytes 31457284
  411.9 20.0 %copy-start.6 = (f32[8,2560]{1,0:T(8,128)S(1)}, f32[8,2560]{1,0:T(8,128)}, u32[]{:S(2)}) copy-start(f32[8,2560]{1,0:T(8,128)} %get-tuple-element.39) | copy-start | bytes 245764
  411.9 20.7 %copy-start.3 = (bf16[256,2560]{1,0:T(8,128)(2,1)S(1)}, bf16[256,2560]{1,0:T(8,128)(2,1)}, u32[]{:S(2)}) copy-start(bf16[256,2560]{1,0:T(8,128)(2,1)} %get-tuple-element.32) | copy-start | bytes 3932164

commit v3 on v2

--- a/solution.py
+++ b/solution.py
@@ -172,7 +172,7 @@
     def wait_last(self):
         self.links.wait('Xa', 'Xb', 'Ya', 'Yb', 'CO')
 
-    def run(self, first_half, second_half):
+    def run(self, first_half, second_half, early=None, late=None):
         second_half('D')
         self.swap('D')
         first_half('X')
@@ -190,7 +190,11 @@
         self.send_half('Y', 'b')
         second_half('O')
         self.swap('O')
+        if early:
+            early()
         self.add_diag()
+        if late:
+            late()
         self.wait_last()
 
     def total(self, at):
@@ -236,6 +240,36 @@
         compiler_params=pltpu.CompilerParams(collective_id=ident, has_side_effects=True, vmem_limit_bytes=66_000_000),
         cost_estimate=pl.CostEstimate(flops=flops, bytes_accessed=40_000_000, transcendentals=3_000_000),
     )(*args)
+
+
+class Tiles:
+    def __init__(self, buf, out, sem, rows=False):
+        self.buf, self.out, self.sem, self.rows = buf, out, sem, rows
+
+    def copy(self, n):
+        size = self.buf.shape[1 if self.rows else 2]
+        at = tile_at(n, size)
+        dst = self.out.at[at] if self.rows else self.out.at[:, at]
+        return pltpu.make_async_copy(self.buf.at[n % 2], dst, self.sem.at[n % 2])
+
+    def put(self, n, value):
+        @pl.when(n >= 2)
+        def _():
+            self.copy(n - 2).wait()
+
+        self.buf[n % 2] = value()
+        self.copy(n).start()
+
+    def finish(self, count):
+        self.copy(count - 2).wait()
+        self.copy(count - 1).wait()
+
+
+OUT_TILE = 512
+
+
+def flat_cols(ref, cols):
+    return ref[:, :, cols].reshape(ref.shape[0] * ref.shape[1], OUT_TILE)
 
 
 def fwd_kernel(dout_ref, q_ref, k_ref, v_ref, dfull, ctx_ref, wide_ref, max_ref, inv_ref, k_rows, strip, own_sem, *comm_sems):
@@ -419,7 +453,12 @@
         + scatter_scratch(rows, model) + [DMA((3,)), DMA((4,)), DMA((4,))] + [DMA((10,))] * 2)
 
 
-def ctx_kernel(dx1_ref, wo_ref, mfull, do_ref, mbuf, own_sem, m_sem, *comm_sems):
+def gelu(pre_act):
+    return 0.5 * pre_act * (1.0 + jnp.tanh(GELU_SCALE * (pre_act + GELU_COEF * pre_act * pre_act * pre_act)))
+
+
+def ctx_kernel(dx1_ref, wo_ref, z_ref, dfull, mfull, do_ref, dw2_ref,
+               mbuf, zv, ut, yv, obuf, own_sem, m_sem, load_sem, out_sem, *comm_sems):
     place = Place()
     place.barrier()
     rows, model = dx1_ref.shape
@@ -434,12 +473,31 @@
         copy.wait()
         do_ref[:, tile_at(place.pair[key], 2 * rows)] = dot_t(wo_ref[...], mbuf[...].reshape(2 * rows, model)).astype(BF16)
 
+    loads = [pltpu.make_async_copy(z_ref, zv, load_sem.at[0]), pltpu.make_async_copy(dfull, yv, load_sem.at[1])]
+    for copy in loads:
+        copy.start()
+    tiles = Tiles(obuf, dw2_ref, out_sem)
+    count = model // OUT_TILE
+
+    def turn(n):
+        cols = tile_at(n, 256)
+        ut[cols, :] = gelu(zv[:, cols].astype(F32)).astype(BF16).T
+
+    def weight_tile(n):
+        cols = tile_at(n, OUT_TILE)
+        tiles.put(n, lambda: dot(ut[...], flat_cols(yv, cols)))
+
+    loads[0].wait()
+    loop(ut.shape[0] // 256, turn)
     gather.links.wait('CO')
     own_copy.wait()
     grad_ctx('O')
     gather.relay()
+    loads[1].wait()
+    loop(count - 1, weight_tile)
     gather.forward('X')
     gather.forward('Y')
+    loop(count, weight_tile, count - 1)
     gather.links.wait('CX')
     grad_ctx('X')
     gather.links.wait('CY')
@@ -447,26 +505,31 @@
     gather.forward('D')
     gather.links.wait('CD')
     grad_ctx('D')
+    tiles.finish(count)
     gather.links.finish()
 
 
-def ctx_call(dx1, w_rows, seq):
+def ctx_call(dx1, w_rows, z_saved, dfull):
     rows, model = dx1.shape
     feats = w_rows.shape[0]
+    seq, hidden = z_saved.shape
     return comm_call(
-        ctx_kernel, "ctx_grads", 2, 8_000_000_000, (dx1, w_rows), [VMEM] * 2,
-        [shape((seq // rows, rows, model), BF16), shape((feats, seq), BF16)], [HBM, VMEM],
-        [pltpu.VMEM((2, rows, model), BF16), DMA(()), DMA((4,))] + [DMA((10,))] * 2)
-
-
-def bwd_kernel(h1_ref, h2_ref, q_ref, k_ref, v_ref, do_ref, wide_ref, max_ref, inv_ref,
-               h1full, h2full, out_ref,
-               k_rows, v_rows, q_rows, do_rows, delta, dq_acc, dk_acc, dv_acc, own_sem, *comm_sems):
+        ctx_kernel, "ctx_grads", 2, 30_000_000_000, (dx1, w_rows, z_saved, dfull), [VMEM] * 2 + [HBM] * 2,
+        [shape((seq // rows, rows, model), BF16), shape((feats, seq), BF16), shape((hidden, model), F32)], [HBM, VMEM, HBM],
+        [pltpu.VMEM((2, rows, model), BF16), pltpu.VMEM((seq, hidden), BF16), pltpu.VMEM((hidden, seq), BF16),
+         pltpu.VMEM((seq // rows, rows, model), BF16), pltpu.VMEM((2, hidden, OUT_TILE), F32),
+         DMA(()), DMA((4,)), DMA((2,)), DMA((2,))] + [DMA((10,))] * 2)
+
+
+def bwd_kernel(h1_ref, h2_ref, q_ref, k_ref, v_ref, do_ref, wide_ref, max_ref, inv_ref, ctx_ref, mfull, dz_ref,
+               h1full, h2full, out_ref, dwo_ref, dw1_ref,
+               k_rows, v_rows, q_rows, do_rows, delta, dq_acc, dk_acc, dv_acc, tok, dzv, obuf, wbuf,
+               own_sem, load_sem, out_sem, *comm_sems):
     place = Place()
     place.barrier()
     gather1 = Gather(place, h1_ref, h1full, *comm_sems[0:2])
     gather2 = Gather(place, h2_ref, h2full, *comm_sems[2:4])
-    gather1.start()
+    gather2.start()
     own_copies = [pltpu.make_async_copy(src, dst.at[place.me], own_sem.at[i])
                   for i, (src, dst) in enumerate(((h1_ref, h1full), (h2_ref, h2full)))]
     for copy in own_copies:
@@ -504,40 +567,72 @@
         out_ref[1, h] = dk_acc[...].T.astype(BF16)
         out_ref[2, h] = dv_acc[...].T.astype(BF16)
 
-    for h in range(heads):
-        head(h)
-        if h == 0:
-            gather1.relay()
-            gather2.start()
-        if h == 2:
-            gather1.forward('X')
-            gather1.forward('Y')
-    gather1.forward('D')
+    loads = [pltpu.make_async_copy(mfull, tok, load_sem.at[0]), pltpu.make_async_copy(dz_ref, dzv, load_sem.at[1])]
+    for copy in loads:
+        copy.start()
+    count = tok.shape[2] // OUT_TILE
+    tiles_o = Tiles(obuf, dwo_ref, out_sem.at[0])
+    tiles_1 = Tiles(wbuf, dw1_ref, out_sem.at[1], rows=True)
+
+    def proj_tile(n):
+        cols = tile_at(n, OUT_TILE)
+        tiles_o.put(n, lambda: dot(ctx_ref[...], flat_cols(tok, cols)))
+
+    def fc1_tile(n):
+        cols = tile_at(n, OUT_TILE)
+        tiles_1.put(n, lambda: dot(flat_cols(tok, cols).T, dzv[...]))
+
+    head(0)
+    loads[0].wait()
+    loop(count, proj_tile)
     gather2.relay()
+    gather1.start()
+    head(1)
+    head(2)
     gather2.forward('X')
     gather2.forward('Y')
+    head(3)
     gather2.forward('D')
-    for gather in (gather1, gather2):
-        gather.links.wait('CO', 'CX', 'CY', 'CD')
-        gather.links.finish()
-    for copy in own_copies:
-        copy.wait()
-
-
-def bwd_call(h1, h2, q_t, k_t, v_t, do_t, wide, row_max, row_inv):
+    own_copies[1].wait()
+    gather2.links.wait('CO', 'CX', 'CY', 'CD')
+    load = pltpu.make_async_copy(h2full, tok, load_sem.at[2])
+    load.start()
+    loads[1].wait()
+    load.wait()
+    loop(count - 2, fc1_tile)
+    gather1.relay()
+    loop(count, fc1_tile, count - 2)
+    gather1.forward('X')
+    gather1.forward('Y')
+    gather1.forward('D')
+    gather1.links.wait('CO', 'CX', 'CY', 'CD')
+    own_copies[0].wait()
+    tiles_o.finish(count)
+    tiles_1.finish(count)
+    gather1.links.finish()
+    gather2.links.finish()
+
+
+def bwd_call(h1, h2, q_t, k_t, v_t, do_t, wide, row_max, row_inv, ctx_rows, mfull, dz):
     heads, dim, seq = q_t.shape
     rows, model = h1.shape
     full = shape((seq // rows, rows, model), BF16)
     turned = pltpu.VMEM((seq, dim), BF16)
+    hidden = dz.shape[1]
+    feats = ctx_rows.shape[0]
     return comm_call(
-        bwd_kernel, "attn_bwd", 3, 60_000_000_000, (h1, h2, q_t, k_t, v_t, do_t, wide, row_max, row_inv), [VMEM] * 9,
-        [full, full, shape((3, heads, dim, seq), BF16)], [HBM, HBM, VMEM],
+        bwd_kernel, "attn_bwd", 3, 80_000_000_000,
+        (h1, h2, q_t, k_t, v_t, do_t, wide, row_max, row_inv, ctx_rows, mfull, dz), [VMEM] * 10 + [HBM] * 2,
+        [full, full, shape((3, heads, dim, seq), BF16), shape((feats, model), F32), shape((model, hidden), F32)],
+        [HBM, HBM, VMEM, HBM, HBM],
         [turned] * 4 + [pltpu.VMEM((1, seq), F32), pltpu.VMEM((dim, seq), F32), pltpu.VMEM((seq, dim), F32),
-                        pltpu.VMEM((seq, dim), F32), DMA((2,))] + [DMA((10,))] * 4)
-
-
-def qkv_kernel(qkv_ref, w_ref, dx1_ref, x_ref, gain_ref, vec_ref, dx_ref, vsum_ref,
-               turned, part, crecv, diag_recv, last_recv, vsend, vrecv, vsem, *comm_sems):
+                        pltpu.VMEM((seq, dim), F32), pltpu.VMEM((seq // rows, rows, model), BF16),
+                        pltpu.VMEM((seq, hidden), BF16), pltpu.VMEM((2, feats, OUT_TILE), F32),
+                        pltpu.VMEM((2, OUT_TILE, hidden), F32), DMA((2,)), DMA((3,)), DMA((2, 2))] + [DMA((10,))] * 4)
+
+
+def qkv_kernel(qkv_ref, w_ref, dx1_ref, x_ref, gain_ref, vec_ref, h1full, dx_ref, vsum_ref, dw_ref,
+               turned, part, crecv, diag_recv, last_recv, vsend, vrecv, tok, obuf, vsem, load_sem, out_sem, *comm_sems):
     place = Place()
     place.barrier()
     rows, model = dx1_ref.shape
@@ -557,8 +652,25 @@
 
         loop(model // TILE, body)
 
+    load = pltpu.make_async_copy(h1full, tok, load_sem)
+    load.start()
+    tiles = Tiles(obuf, dw_ref, out_sem)
+    count = model // OUT_TILE
+
+    def weight_tile(n):
+        cols = tile_at(n, OUT_TILE)
+        tiles.put(n, lambda: dot(qkv_ref[...], flat_cols(tok, cols)))
+
+    def early_tiles():
+        load.wait()
+        loop(count - 2, weight_tile)
+
+    def late_tiles():
+        loop(count, weight_tile, count - 2)
+
     turn('D')
-    scatter.run(turn, grad_norm)
+    scatter.run(turn, grad_norm, early_tiles, late_tiles)
+    tiles.finish(count)
     gain = gain_ref[...]
     vsum_ref[...] = vec_ref[...]
 
@@ -582,14 +694,15 @@
     scatter.links.finish()
 
 
-def qkv_call(qkv_rows, w_rows, dx1, x_in, ln1_gain, vec):
+def qkv_call(qkv_rows, w_rows, dx1, x_in, ln1_gain, vec, h1full):
     rows, model = dx1.shape
     feats = qkv_rows.shape[0]
     return comm_call(
-        qkv_kernel, "qkv_grads", 4, 20_000_000_000, (qkv_rows, w_rows, dx1, x_in, ln1_gain[None], vec), [VMEM] * 6,
-        [shape((rows, model), BF16), shape((8, model), F32)], [VMEM] * 2,
+        qkv_kernel, "qkv_grads", 4, 30_000_000_000, (qkv_rows, w_rows, dx1, x_in, ln1_gain[None], vec, h1full), [VMEM] * 6 + [HBM],
+        [shape((rows, model), BF16), shape((8, model), F32), shape((feats, model), F32)], [VMEM, VMEM, HBM],
         [pltpu.VMEM((2 * rows, feats), BF16)] + scatter_scratch(rows, model)
-        + [pltpu.VMEM((3, 8, model), F32), pltpu.VMEM((3, 8, model), F32), DMA((6,))] + [DMA((10,))] * 2)
+        + [pltpu.VMEM((3, 8, model), F32), pltpu.VMEM((3, 8, model), F32), pltpu.VMEM((8, rows, model), BF16),
+           pltpu.VMEM((2, feats, OUT_TILE), F32), DMA((6,)), DMA(()), DMA((2,))] + [DMA((10,))] * 2)
 
 
 def solution(mesh):
@@ -602,19 +715,16 @@
         _, _, h1_local = layer_norm_fwd(x_in, ln1_gain, ln1_bias)
         dfull, ctx_t, wide_t, row_max, row_inv = fwd_call(d_out, q_t, k_t, v_t)
         dx1, grad_pre, grad_bfc1, vec = mlp_call(dfull, d_out, x_mid, ln2_gain, z_saved, w_fc2, w_fc1)
-        mfull, do_t = ctx_call(dx1, w_proj.reshape(heads * dim, model), seq)
-        h1_full, h2_full, qkv_t = bwd_call(h1_local, h2_local, q_t, k_t, v_t, do_t.reshape(heads, dim, seq), wide_t, row_max, row_inv)
-        dout_full, mid_full, h1_full, h2_full = (v.reshape(seq, model) for v in (dfull, mfull, h1_full, h2_full))
+        mfull, do_t, grad_wfc2 = ctx_call(dx1, w_proj.reshape(heads * dim, model), z_saved, dfull)
+        h1_full, _, qkv_t, grad_wproj, grad_wfc1 = bwd_call(
+            h1_local, h2_local, q_t, k_t, v_t, do_t.reshape(heads, dim, seq), wide_t, row_max, row_inv,
+            ctx_t.reshape(heads * dim, seq), mfull, grad_pre)
         qkv_rows = qkv_t.reshape(3 * heads * dim, seq)
         w_rows = w_qkv.transpose(0, 2, 3, 1).reshape(3 * heads * dim, model)
-        grad_x, vec_sum = qkv_call(qkv_rows, w_rows, dx1, x_in, ln1_gain, vec)
-        act_value, _ = gelu_parts(z_saved.astype(F32))
-        grad_wfc2 = jnp.einsum('sf,sd->fd', act_value.astype(BF16), dout_full, preferred_element_type=F32)
-        grad_wproj = jnp.einsum('hes,sd->hed', ctx_t, mid_full, preferred_element_type=F32)
-        grad_wqkv = jnp.einsum('fs,sd->fd', qkv_rows, h1_full, preferred_element_type=F32)
+        grad_x, vec_sum, grad_wqkv = qkv_call(qkv_rows, w_rows, dx1, x_in, ln1_gain, vec, h1_full)
+        grad_wproj = grad_wproj.reshape(heads, dim, model)
         grad_wqkv = grad_wqkv.reshape(3, heads, dim, model).transpose(0, 3, 1, 2)
         grad_bqkv = jnp.sum(qkv_t, axis=3, dtype=F32)
-        grad_wfc1 = jnp.einsum('sd,sf->df', h2_full, grad_pre, preferred_element_type=F32)
         grad_vecs = jnp.concatenate([vec_sum[4:6], vec_sum[:4]])
         return grad_x[None], grad_wqkv, grad_bqkv, grad_wproj, grad_wfc1, grad_bfc1[0], grad_wfc2, grad_vecs
 

time: 443 us -> 406 us (0.916)
  matrix products: 71 us -> 0 us
  local copies, waits for them, and re-layouts: 2.33 us -> 35.6 us
    dot_general x4 -> x0, matrix products: 71 us -> none  [the longest x1 24.8 us: local_backward(): jnp.einsum('sf,sd->fd', act_value.astype(BF16), dout_full, preferred_elem...]
    unnamed x21 -> x23, local copies, waits for them, and re-layouts: 1.1 us -> 32.5 us
where the time goes in v3:
time: 406 us; the launch traced here: 399 us
  Pallas kernels  350 us (86%)
  local copies, waits for them, and re-layouts  35.6 us (9%)
  other arithmetic  11.6 us (3%)
    pallas_call x5, Pallas kernels, comm_call(): pl.pallas_call(kernel, in_specs=in_specs, out_specs=out_specs, out_shape=...  350 us
    unnamed x23, local copies, waits for them, and re-layouts  32.5 us

profile of v3, /device:TPU:0, one launch (start us, length us, event | category | flops | bytes accessed | tf_op | source)
XLA Modules:
  0.0 398.6 jit_solution(5350598210532946463)
XLA Ops:
  0.6 0.0 copy-start.4
  0.6 54.7 %attn_fwd.1 = (bf16[8,256,2560]{2,1,0:T(8,128)(2,1)}, bf16[4,80,2048]{2,1,0:T(8,128)(2,1)}, f32[4,80,2048]{2,1,0:T(8,128)}, f32[4,1,2048]{2,1,0:T(1,128)}, f32[4,1,2048]{2,1,0:T(1,128)}) custom-call(bf16[256,2560]{1,0:T(8,128)(2,1)} %bitcast.41, bf16[4,80,2048]{2,1,0:T(8,128)(2,1)} %bitcast.43, bf16[4,80,2048]{2,1,0:T(8,128)(2,1)} %bitcast.45, ...), custom_call_target="tpu_custom_call" | custom-call | flops 40000000000 | bytes 40000000 | tf_op jit(solution)/shard_map/attn_fwd/pallas_call | solution.py:238
  55.4 0.0 copy-done.4
  55.4 0.6 broadcast_in_dim.6.gain_ref
  56.0 76.1 %mlp_grads.1 = (bf16[256,2560]{1,0:T(8,128)(2,1)}, bf16[2048,1280]{1,0:T(8,128)(2,1)}, f32[1,1280]{1,0:T(1,128)}, f32[8,2560]{1,0:T(8,128)}) custom-call(bf16[8,256,2560]{2,1,0:T(8,128)(2,1)} %get-tuple-element.27.dfull, bf16[256,2560]{1,0:T(8,128)(2,1)} %bitcast.42, bf16[256,2560]{1,0:T(8,128)(2,1)} %bitcast.31, f32[1,2560]{1,0:T(1,128)} %broadcast_in_dim.6.gain_ref, ...), custom_call_target="tpu_custom_call" | custom-call | flops 60000002048 | bytes 40000000 | tf_op jit(solution)/shard_map/mlp_grads/pallas_call | solution.py:238
  132.0 51.9 %ctx_grads.1 = (bf16[8,256,2560]{2,1,0:T(8,128)(2,1)}, bf16[320,2048]{1,0:T(8,128)(2,1)}, f32[1280,2560]{1,0:T(8,128)}) custom-call(bf16[256,2560]{1,0:T(8,128)(2,1)} %get-tuple-element.28.dx1_ref, bf16[320,2560]{1,0:T(8,128)(2,1)} %bitcast.40, bf16[2048,1280]{1,0:T(8,128)(2,1)} %bitcast.38, bf16[8,256,2560]{2,1,0:T(8,128)(2,1)} %get-tuple-element.27.dfull), custom_call_target="tpu_custom_call" | custom-call | flops 30000001024 | bytes 40000000 | tf_op jit(solution)/shard_map/ctx_grads/pallas_call | solution.py:238
  184.0 0.0 copy-start.1
  184.0 0.0 copy-start
  184.0 0.0 copy-start.5
  184.0 0.0 copy-start.6
  184.0 0.0 copy-start.7
  184.0 1.7 convert_reduce_fusion.1
  185.8 1.8 fusion.4
  187.6 0.0 copy-done.1
  187.6 0.3 convert_reduce_fusion.2
  187.9 0.5 fusion.8
  188.4 0.0 copy-done
  188.4 0.0 copy-done.5
  188.4 0.0 copy-done.6
  188.4 0.0 copy-done.7
  188.4 2.7 fusion.7
  191.1 97.8 %attn_bwd.1 = (bf16[8,256,2560]{2,1,0:T(8,128)(2,1)}, bf16[8,256,2560]{2,1,0:T(8,128)(2,1)}, bf16[3,4,80,2048]{3,2,1,0:T(8,128)(2,1)}, f32[320,2560]{1,0:T(8,128)}, f32[2560,1280]{1,0:T(8,128)}) custom-call(bf16[256,2560]{1,0:T(8,128)(2,1)} %get-tuple-element.47.h1_ref, bf16[256,2560]{1,0:T(8,128)(2,1)} %get-tuple-element.46.h2_ref, ...), custom_call_target="tpu_custom_call" | custom-call | flops 80000000000 | bytes 40000000 | tf_op jit(solution)/shard_map/attn_bwd/pallas_call | solution.py:238
  288.9 0.6 broadcast_in_dim.7.gain_ref
  289.5 69.6 %qkv_grads.1 = (bf16[256,2560]{1,0:T(8,128)(2,1)}, f32[8,2560]{1,0:T(8,128)}, f32[960,2560]{1,0:T(8,128)}) custom-call(bf16[960,2048]{1,0:T(8,128)(2,1)} %bitcast.34, bf16[960,2560]{1,0:T(8,128)(2,1)} %bitcast.39, bf16[256,2560]{1,0:T(8,128)(2,1)} %get-tuple-element.28.dx1_ref, bf16[256,2560]{1,0:T(8,128)(2,1)} %bitcast.32, ...), custom_call_target="tpu_custom_call" | custom-call | flops 30000001024 | bytes 40000000 | tf_op jit(solution)/shard_map/qkv_grads/pallas_call | solution.py:238
  359.1 0.0 copy-start.8
  359.2 0.0 copy-start.3
  359.2 1.0 slice.7
  360.2 0.9 slice.6
  361.1 0.7 pad_maximum_fusion
  361.7 3.3 convert_reduce_fusion
  365.0 0.0 copy-done.8
  365.0 0.6 reduce
  365.7 0.0 copy-done.3
  365.7 1.1 copy.28
  366.7 0.0 copy-start.2
  366.7 8.5 %copy.29 = f32[3,2560,4,80]{1,3,2,0:T(8,128)} copy(f32[3,2560,4,80]{1,3,2,0:T(8,128)} %bitcast.33) | data formatting | bytes 19660800
  375.2 0.0 copy-done.2
  375.2 1.7 copy.30
  376.9 10.5 %copy.31 = f32[2560,1280]{1,0:T(8,128)} copy(f32[2560,1280]{1,0:T(8,128)} %get-tuple-element.60) | data formatting | bytes 26214400
  387.4 10.7 %copy.32 = f32[1280,2560]{1,0:T(8,128)} copy(f32[1280,2560]{1,0:T(8,128)} %get-tuple-element.62) | data formatting | bytes 26214400
  (4 shorter events, 0.0 us)
Async XLA Ops:
  0.6 54.7 %copy-start.4 = (f32[2560]{0:T(1024)S(1)}, f32[2560]{0:T(1024)}, u32[]{:S(2)}) copy-start(f32[2560]{0:T(1024)} %param.24) | copy-start | bytes 30724
  184.0 3.6 copy-start.1
  184.0 4.4 %copy-start = (bf16[1,256,2560]{2,1,0:T(8,128)(2,1)S(1)}, bf16[1,256,2560]{2,1,0:T(8,128)(2,1)}, u32[]{:S(2)}) copy-start(bf16[1,256,2560]{2,1,0:T(8,128)(2,1)} %param.16) | copy-start | bytes 3932164
  184.0 4.4 %copy-start.5 = (f32[2560]{0:T(1024)S(1)}, f32[2560]{0:T(1024)}, u32[]{:S(2)}) copy-start(f32[2560]{0:T(1024)} %param.22) | copy-start | bytes 30724
  184.0 4.4 %copy-start.6 = (f32[2560]{0:T(1024)S(1)}, f32[2560]{0:T(1024)}, u32[]{:S(2)}) copy-start(f32[2560]{0:T(1024)} %param.25) | copy-start | bytes 30724
  184.0 4.4 %copy-start.7 = (f32[2560]{0:T(1024)S(1)}, f32[2560]{0:T(1024)}, u32[]{:S(2)}) copy-start(f32[2560]{0:T(1024)} %param.23) | copy-start | bytes 30724
  359.1 5.9 %copy-start.8 = (f32[1,1280]{1,0:T(1,128)S(1)}, f32[1,1280]{1,0:T(1,128)}, u32[]{:S(2)}) copy-start(f32[1,1280]{1,0:T(1,128)} %get-tuple-element.43) | copy-start | bytes 15364
  359.2 6.5 %copy-start.3 = (bf16[256,2560]{1,0:T(8,128)(2,1)S(1)}, bf16[256,2560]{1,0:T(8,128)(2,1)}, u32[]{:S(2)}) copy-start(bf16[256,2560]{1,0:T(8,128)(2,1)} %get-tuple-element.39) | copy-start | bytes 3932164
  366.7 8.5 %copy-start.2 = (f32[320,2560]{1,0:T(8,128)S(1)}, f32[320,2560]{1,0:T(8,128)}, u32[]{:S(2)}) copy-start(f32[320,2560]{1,0:T(8,128)} %get-tuple-element.41) | copy-start | bytes 9830404

commit v4 on v3

v4 whole, which is shorter than its diff:
```python
import jax
import jax.numpy as jnp
from jax import lax
from jax.experimental import pallas as pl
from jax.experimental.pallas import tpu as pltpu
from jax.sharding import PartitionSpec as P

LN_EPS = 1e-5
GELU_COEF = 0.044715
GELU_SCALE = 0.7978845608028654
LOG2E = 1.4426950408889634
BLK = 512
F32 = jnp.float32
BF16 = jnp.bfloat16


def layer_norm_bwd(grad_norm, x_hat, inv_std, norm_gain):
    grad_hat = grad_norm * norm_gain
    centered_grad = grad_hat - jnp.mean(grad_hat, axis=-1, keepdims=True)
    return inv_std * (centered_grad - x_hat * jnp.mean(grad_hat * x_hat, axis=-1, keepdims=True))


def dot(a, b):
    return jnp.dot(a, b, preferred_element_type=F32)


def causal_fill(scores, fill):
    key_ids = lax.broadcasted_iota(jnp.int32, scores.shape, 0)
    query_ids = lax.broadcasted_iota(jnp.int32, scores.shape, 1)
    return jnp.where(query_ids >= key_ids, scores, fill)


class Place:
    def __init__(self):
        self.group = lax.axis_index('dp')
        self.me = lax.axis_index('tp')
        self.core = self.me % 2
        self.dx = 2 - 4 * ((self.me // 2) % 2)
        self.dy = 4 - 8 * (self.me // 4)
        self.dc = 1 - 2 * self.core
        self.peer = {'X': self.me + self.dx, 'Y': self.me + self.dy, 'C': self.me + self.dc}
        self.block = {'O': self.me, 'X': self.me + self.dx, 'Y': self.me + self.dy, 'D': self.me + self.dx + self.dy}
        self.other = {key: val + self.dc for key, val in self.block.items()}
        self.x, self.y = (self.me // 2) % 2, self.me // 4

    def pair_at(self, i):
        flip_x, flip_y = 1 - i // 2, 1 - i % 2
        return 2 * (self.y + flip_y * (1 - 2 * self.y)) + self.x + flip_x * (1 - 2 * self.x)

    def barrier(self):
        sem = pltpu.get_barrier_semaphore()
        for key in 'XYC':
            pl.semaphore_signal(sem, inc=1, device_id=(self.group, self.peer[key]), device_id_type=pl.DeviceIdType.MESH)
        pl.semaphore_wait(sem, 3)


class Links:
    def __init__(self, place, send_sem, recv_sem):
        self.place, self.send_sem, self.recv_sem = place, send_sem, recv_sem
        self.copies = {}

    def define(self, name, to, src, dst, *index):
        at = len(self.copies)

        def place_of(ref):
            ref, where = ref if isinstance(ref, tuple) else (ref, index)
            return ref.at[where] if where else ref

        def copy():
            return pltpu.make_async_remote_copy(
                src_ref=place_of(src), dst_ref=place_of(dst), send_sem=self.send_sem.at[at], recv_sem=self.recv_sem.at[at],
                device_id=(self.place.group, self.place.peer[to]), device_id_type=pl.DeviceIdType.MESH)

        self.copies[name] = copy

    def start(self, name):
        self.copies[name]().start()

    def send(self, name, *rest):
        self.define(name, *rest)
        self.start(name)

    def wait(self, *names):
        for name in names:
            self.copies[name]().wait_recv()

    def finish(self):
        for copy in self.copies.values():
            copy().wait_send()


class Gather:
    COPIES = 10

    def __init__(self, place, own, full, send_sem, recv_sem):
        self.place, self.own, self.full = place, own, full
        self.links = Links(place, send_sem, recv_sem)
        half = own.shape[0] // 2
        self.first, self.second = pl.ds(0, half), pl.ds(half, half)

    def start(self):
        me, full, own, send = self.place.me, self.full, self.own, self.links.send
        for name, half in (('Xa', self.first), ('Yb', self.second), ('Xb', self.second), ('Ya', self.first)):
            send(name, name[0], (own, (half,)), (full, (me, half)))
        send('CO', 'C', (own, ()), (full, (me,)))

    def relay(self):
        links, full, block = self.links, self.full, self.place.block
        links.wait('Xa')
        links.send('Da', 'Y', full, full, block['X'], self.first)
        links.wait('Yb')
        links.send('Db', 'X', full, full, block['Y'], self.second)

    def forward(self, key):
        first, second = ('Xb', None) if key == 'X' else ('Ya', None) if key == 'Y' else ('Da', 'Db')
        self.links.wait(first)
        if second:
            self.links.wait(second)
        self.links.send('C' + key, 'C', self.full, self.full, self.place.block[key])


class ThirdGather:
    COPIES = 5

    def __init__(self, place, full, send_sem, recv_sem):
        self.place, self.full = place, full
        self.links = Links(place, send_sem, recv_sem)
        half = full.shape[1] // 2
        self.first, self.second = pl.ds(0, half), pl.ds(half, half)

    def start(self, third, own):
        me, full = self.place.me, self.full
        near = {'X': self.first, 'Y': self.second} if third == 0 else {'X': self.second, 'Y': self.first}
        if third == 2:
            block = self.place.block
            near = {'Y': (block['X'], self.first), 'X': (block['Y'], self.second)}
        for key in 'XY':
            if third == 2:
                self.links.send('N' + key, key, full, full, *near[key])
            else:
                src = (full, (me, near[key])) if own is None else (own, (near[key],))
                self.links.send('N' + key, key, src, (full, (me, near[key])))
        if third == 0:
            self.links.send('CO', 'C', (own, ()), (full, (me,)))

    def forward(self, third):
        block = self.place.block
        for key in 'XY':
            self.links.wait('N' + key)
            half = self.first if (third == 0) == (key == 'X') else self.second
            slot = block[key]
            if third == 2:
                slot, half = block['D'], (self.second if key == 'X' else self.first)
            self.links.send('C' + key, 'C', self.full, self.full, slot, half)

    def wait_pair(self, third):
        self.links.wait('CX', 'CY', *(('CO',) if third == 0 else ()))


class Scatter:
    COPIES = 10

    def __init__(self, place, part, crecv, diag_recv, last_recv, send_sem, recv_sem):
        self.place, self.part, self.crecv = place, part, crecv
        self.diag_recv, self.last_recv = diag_recv, last_recv
        self.links = Links(place, send_sem, recv_sem)
        half = part.shape[1] // 2
        self.half = {'a': pl.ds(0, half), 'b': pl.ds(half, half)}
        for at, key in enumerate('OXYD'):
            self.links.define('C' + key, 'C', (part, (place.other[key],)), (crecv, (at,)))

    def add_rows(self, slot, start, count, other, other_start):
        step = 64

        def body(i, carry):
            here = pl.ds(pl.multiple_of(start + i * step, step), step)
            there = pl.ds(pl.multiple_of(other_start + i * step, step), step)
            total = self.part[slot, here, :].astype(F32) + other[there, :].astype(F32)
            self.part[slot, here, :] = total.astype(BF16)
            return carry

        lax.fori_loop(0, count // step, body, 0)

    def swap(self, key):
        self.links.start('C' + key)

    def add_pair(self, key):
        self.links.wait('C' + key)
        at = 'OXYD'.index(key)
        self.add_rows(self.place.block[key], 0, self.part.shape[1], self.crecv.at[at], 0)

    def send_half(self, key, half):
        at = self.half[half]
        self.links.send(key + half, key, (self.part, (self.place.block[key], at)), (self.last_recv, ('XY'.index(key), at)))

    def send_diag(self):
        for i, (key, half) in enumerate((('X', 'a'), ('Y', 'b'))):
            self.links.send('D' + half, key, (self.part, (self.place.block['D'], self.half[half])), (self.diag_recv, (i,)))

    def add_diag(self):
        rows = self.part.shape[1] // 2
        self.links.wait('Da')
        self.add_rows(self.place.block['Y'], 0, rows, self.diag_recv.at[0], 0)
        self.links.wait('Db')
        self.add_rows(self.place.block['X'], rows, rows, self.diag_recv.at[1], 0)
        self.send_half('Y', 'a')
        self.send_half('X', 'b')

    def wait_last(self):
        self.links.wait('Xa', 'Xb', 'Ya', 'Yb', 'CO')

    def between(self, i):
        @pl.when(i == 1)
        def _():
            self.add_pair('D')
            self.send_diag()

        @pl.when(i == 2)
        def _():
            self.add_pair('X')
            self.send_half('X', 'a')

        @pl.when(i == 3)
        def _():
            self.add_pair('Y')
            self.send_half('Y', 'b')

    def after(self, i):
        for at, key in enumerate('DXYO'):
            @pl.when(i == at)
            def _():
                self.swap(key)

    def total(self, at):
        me = self.place.me
        return (self.part[me, at, :].astype(F32) + self.crecv[0, at, :].astype(F32)
                + self.last_recv[0, at, :].astype(F32) + self.last_recv[1, at, :].astype(F32))


def gelu_slope(pre_act):
    tanh_val = jnp.tanh(GELU_SCALE * (pre_act + GELU_COEF * pre_act * pre_act * pre_act))
    return 0.5 * (1.0 + tanh_val) + 0.5 * pre_act * (1.0 - tanh_val * tanh_val) * GELU_SCALE * (1.0 + 3.0 * GELU_COEF * pre_act * pre_act)


def layer_norm_hat(rows_f32):
    centered = rows_f32 - jnp.mean(rows_f32, axis=-1, keepdims=True)
    inv_std = lax.rsqrt(jnp.mean(centered * centered, axis=-1, keepdims=True) + LN_EPS)
    return centered * inv_std, inv_std


LN_ROWS = 32
TILE = 1280
VMEM = pl.BlockSpec(memory_space=pltpu.VMEM)
HBM = pl.BlockSpec(memory_space=pl.ANY)
DMA = pltpu.SemaphoreType.DMA
shape = jax.ShapeDtypeStruct


def tile_at(i, size):
    return pl.ds(pl.multiple_of(i * size, size), size)


def loop(count, body, start=0):
    def step(i, carry):
        body(i)
        return carry

    lax.fori_loop(start, count, step, 0)


def comm_call(kernel, name, ident, flops, args, in_specs, out_shape, out_specs, scratch, aliases={}):
    return pl.pallas_call(
        kernel, in_specs=in_specs, out_specs=out_specs, out_shape=out_shape, scratch_shapes=scratch, name=name,
        input_output_aliases=aliases,
        compiler_params=pltpu.CompilerParams(collective_id=ident, has_side_effects=True, vmem_limit_bytes=66_000_000),
        cost_estimate=pl.CostEstimate(flops=flops, bytes_accessed=40_000_000, transcendentals=3_000_000),
    )(*args)


class Tiles:
    def __init__(self, buf, out, sem, rows=False):
        self.buf, self.out, self.sem, self.rows = buf, out, sem, rows

    def copy(self, n):
        size = self.buf.shape[1 if self.rows else 2]
        at = tile_at(n, size)
        dst = self.out.at[at] if self.rows else self.out.at[:, at]
        return pltpu.make_async_copy(self.buf.at[n % 2], dst, self.sem.at[n % 2])

    def put(self, n, value):
        @pl.when(n >= 2)
        def _():
            self.copy(n - 2).wait()

        self.buf[n % 2] = value()
        self.copy(n).start()

    def finish(self, count):
        self.copy(count - 2).wait()
        self.copy(count - 1).wait()


OUT_TILE = 512


def flat_cols(ref, cols):
    return ref[:, :, cols].reshape(ref.shape[0] * ref.shape[1], OUT_TILE)


def fwd_kernel(dout_ref, q_ref, k_ref, v_ref, x_ref, mid_ref, affine_ref,
               dfull, ctx_ref, wide_ref, max_ref, inv_ref, h1_ref, h2_ref, k_rows, strip, own_sem, *comm_sems):
    place = Place()
    place.barrier()
    gather = Gather(place, dout_ref, dfull, *comm_sems)
    gather.start()
    own_copy = pltpu.make_async_copy(dout_ref, dfull.at[place.me], own_sem)
    own_copy.start()
    heads, dim, seq = q_ref.shape
    exp_scale = dim ** -0.5 * LOG2E
    affine = affine_ref[...]

    def norm_rows(i):
        at = tile_at(i, LN_ROWS)
        for row, (src, dst) in enumerate(((x_ref, h1_ref), (mid_ref, h2_ref))):
            x_hat, _ = layer_norm_hat(src[at, :].astype(F32))
            dst[at, :] = (x_hat * affine[2 * row:2 * row + 1] + affine[2 * row + 1:2 * row + 2]).astype(BF16)

    loop(x_ref.shape[0] // LN_ROWS, norm_rows)

    def head(h):
        k_rows[...] = k_ref[h].T

        def query_block(qi):
            q_at = tile_at(qi, BLK)
            q_blk = q_ref[h, :, q_at]

            def score_step(ki, run_max):
                at = tile_at(ki, BLK)
                blk = dot(k_rows[at, :], q_blk)
                strip[at, :] = blk
                return jnp.maximum(run_max, jnp.max(blk, axis=0, keepdims=True))

            diag = causal_fill(dot(k_rows[q_at, :], q_blk), -1e30)
            strip[q_at, :] = diag
            row_max = lax.fori_loop(0, qi, score_step, jnp.max(diag, axis=0, keepdims=True))

            def exp_step(ki, run_sum):
                at = tile_at(ki, BLK)
                probs = jnp.exp2((strip[at, :] - row_max) * exp_scale)
                strip[at, :] = probs
                return run_sum + jnp.sum(probs, axis=0, keepdims=True)

            row_inv = 1.0 / lax.fori_loop(0, qi + 1, exp_step, jnp.zeros_like(row_max))

            def ctx_step(ki, carry):
                high, low = carry
                at = tile_at(ki, BLK)
                probs = strip[at, :] * row_inv
                probs_low = probs.astype(BF16)
                rest = (probs - probs_low.astype(F32)).astype(BF16)
                v_blk = v_ref[h, :, at]
                return high + dot(v_blk, probs_low), low + dot(v_blk, rest)

            zero = jnp.zeros((dim, BLK), F32)
            high, low = lax.fori_loop(0, qi + 1, ctx_step, (zero, zero))
            ctx_ref[h, :, q_at] = high.astype(BF16)
            wide_ref[h, :, q_at] = high + low
            max_ref[h, :, q_at] = row_max
            inv_ref[h, :, q_at] = row_inv

        loop(seq // BLK, query_block)

    def head_step(h):
        head(h)

        @pl.when(h == 1)
        def _():
            gather.relay()

        @pl.when(h == 2)
        def _():
            gather.forward('X')
            gather.forward('Y')

    loop(heads, head_step)
    gather.forward('D')
    gather.links.wait('CO', 'CX', 'CY', 'CD')
    own_copy.wait()
    gather.links.finish()


def fwd_call(d_out, q_t, k_t, v_t, x_in, x_mid, affine):
    heads, dim, seq = q_t.shape
    rows, model = d_out.shape
    return comm_call(
        fwd_kernel, "attn_fwd", 0, 40_000_000_000, (d_out, q_t, k_t, v_t, x_in, x_mid, affine), [VMEM] * 7,
        [shape((seq // rows, rows, model), BF16), shape((heads, dim, seq), BF16), shape((heads, dim, seq), F32),
         shape((heads, 1, seq), F32), shape((heads, 1, seq), F32), shape((rows, model), BF16), shape((rows, model), BF16)],
        [HBM] + [VMEM] * 6,
        [pltpu.VMEM((seq, dim), BF16), pltpu.VMEM((seq, BLK), F32), DMA(())] + [DMA((10,))] * 2)


def dot_t(a, b):
    return lax.dot_general(a, b, (((1,), (1,)), ((), ())), preferred_element_type=F32)


def mlp_kernel(dfull, dout_ref, mid_ref, affine_ref, h1_ref, z_ref, w2_ref, w1_ref,
               dx1_ref, dz_ref, gb1_ref, vec_ref, h1full,
               w2v, w1v, zv, dzv, ybuf, part, crecv, diag_recv, last_recv,
               load_sem, y_sem, dz_sem, own_sem, *comm_sems):
    place = Place()
    place.barrier()
    rows, model = dout_ref.shape
    hidden = w2v.shape[0]
    scatter = Scatter(place, part, crecv, diag_recv, last_recv, *comm_sems[0:2])
    gather = ThirdGather(place, h1full, *comm_sems[2:4])
    gather.start(0, h1_ref)
    own_copy = pltpu.make_async_copy(h1_ref, h1full.at[place.me], own_sem)

    def load_pair(i):
        return pltpu.make_async_copy(dfull.at[pl.ds(2 * place.pair_at(i), 2)], ybuf.at[i % 2], y_sem.at[i])

    def store_grad(i):
        at = tile_at(place.pair_at(i), 2 * rows)
        return pltpu.make_async_copy(dzv.at[at], dz_ref.at[at], dz_sem.at[i])

    load_pair(0).start()
    loads = [pltpu.make_async_copy(src, dst, load_sem.at[i])
             for i, (src, dst) in enumerate(((w2_ref, w2v), (z_ref, zv), (w1_ref, w1v)))]
    for copy in loads:
        copy.start()
    load_pair(1).start()
    own_copy.start()
    gb1_ref[...] = jnp.zeros_like(gb1_ref)
    vec_ref[...] = jnp.zeros_like(vec_ref)
    loads[0].wait()
    loads[1].wait()

    def pair_step(i):
        slot = i % 2
        pair = place.pair_at(i)
        at = tile_at(pair, 2 * rows)
        load_pair(i).wait()

        def grad_act(n):
            cols = tile_at(n, TILE)
            acc = dot_t(ybuf[slot].reshape(2 * rows, model), w2v[cols, :])
            grad = (acc * gelu_slope(zv[at, cols].astype(F32))).astype(BF16)
            dzv[at, cols] = grad
            gb1_ref[:, cols] += jnp.sum(grad.astype(F32), axis=0, keepdims=True)

        loop(hidden // TILE, grad_act)
        store_grad(i).start()

        @pl.when(i < 2)
        def _():
            load_pair(i + 2).start()

        @pl.when(i == 0)
        def _():
            loads[2].wait()

        @pl.when(i == 2)
        def _():
            gather.forward(0)

        scatter.between(i)

        def grad_norm(n):
            cols = tile_at(n, TILE)
            acc = dot_t(dzv[at, :], w1v[cols, :]).astype(BF16)
            part[2 * pair, :, cols] = acc[:rows]
            part[2 * pair + 1, :, cols] = acc[rows:]

        loop(model // TILE, grad_norm)
        scatter.after(i)

    loop(4, pair_step)
    scatter.add_diag()
    scatter.wait_last()

    gain = affine_ref[2:3, :]

    def norm_rows(i):
        at = tile_at(i, LN_ROWS)
        grad = scatter.total(at)
        x_hat, inv_std = layer_norm_hat(mid_ref[at, :].astype(F32))
        dout_rows = dout_ref[at, :].astype(F32)
        mid = (dout_rows + layer_norm_bwd(grad, x_hat, inv_std, gain)).astype(BF16)
        dx1_ref[at, :] = mid
        for row, val in enumerate((grad * x_hat, grad, mid.astype(F32), dout_rows)):
            vec_ref[row + 2:row + 3, :] += jnp.sum(val, axis=0, keepdims=True)

    loop(rows // LN_ROWS, norm_rows)
    for i in range(4):
        store_grad(i).wait()
    own_copy.wait()
    gather.wait_pair(0)
    gather.links.finish()
    scatter.links.finish()


def scatter_scratch(rows, model):
    return [pltpu.VMEM((8, rows, model), BF16), pltpu.VMEM((4, rows, model), BF16),
            pltpu.VMEM((2, rows // 2, model), BF16), pltpu.VMEM((2, rows, model), BF16)]


def mlp_call(dfull, d_out, x_mid, affine, h1, z_saved, w2, w1):
    rows, model = d_out.shape
    seq, hidden = z_saved.shape
    return comm_call(
        mlp_kernel, "mlp_grads", 1, 60_000_000_000, (dfull, d_out, x_mid, affine, h1, z_saved, w2, w1),
        [HBM] + [VMEM] * 3 + [HBM] * 4,
        [shape((rows, model), BF16), shape((seq, hidden), BF16), shape((1, hidden), F32), shape((8, model), F32),
         shape(dfull.shape, BF16)],
        [VMEM, HBM, VMEM, VMEM, HBM],
        [pltpu.VMEM((hidden, model), BF16), pltpu.VMEM((model, hidden), BF16),
         pltpu.VMEM((seq, hidden), BF16), pltpu.VMEM((seq, hidden), BF16), pltpu.VMEM((2, 2, rows, model), BF16)]
        + scatter_scratch(rows, model) + [DMA((3,)), DMA((4,)), DMA((4,)), DMA(())] + [DMA((10,))] * 2 + [DMA((5,))] * 2)


def gelu(pre_act):
    return 0.5 * pre_act * (1.0 + jnp.tanh(GELU_SCALE * (pre_act + GELU_COEF * pre_act * pre_act * pre_act)))


def ctx_kernel(dx1_ref, wo_ref, z_ref, dfull, mfull, do_ref, dw2_ref,
               mbuf, zv, ut, yv, obuf, own_sem, m_sem, load_sem, out_sem, *comm_sems):
    place = Place()
    place.barrier()
    rows, model = dx1_ref.shape
    gather = Gather(place, dx1_ref, mfull, *comm_sems)
    gather.start()
    own_copy = pltpu.make_async_copy(dx1_ref, mfull.at[place.me], own_sem)
    own_copy.start()

    loads = [pltpu.make_async_copy(z_ref, zv, load_sem.at[0]), pltpu.make_async_copy(dfull, yv, load_sem.at[1])]
    for copy in loads:
        copy.start()
    tiles = Tiles(obuf, dw2_ref, out_sem)
    count = model // OUT_TILE

    def turn(n):
        cols = tile_at(n, 256)
        ut[cols, :] = gelu(zv[:, cols].astype(F32)).astype(BF16).T

    def weight_tile(n):
        cols = tile_at(n, OUT_TILE)
        tiles.put(n, lambda: dot(ut[...], flat_cols(yv, cols)))

    loads[0].wait()
    loop(ut.shape[0] // 256, turn)
    gather.relay()
    loads[1].wait()
    loop(count, weight_tile)
    gather.forward('X')
    gather.forward('Y')
    own_copy.wait()
    gather.links.wait('CO')

    def grad_ctx(i):
        @pl.when(i == 1)
        def _():
            gather.links.wait('CY')

        @pl.when(i == 2)
        def _():
            gather.links.wait('CX')

        @pl.when(i == 3)
        def _():
            gather.forward('D')
            gather.links.wait('CD')

        pair = place.pair_at(3 - i)
        copy = pltpu.make_async_copy(mfull.at[pl.ds(2 * pair, 2)], mbuf, m_sem)
        copy.start()
        copy.wait()
        do_ref[:, tile_at(pair, 2 * rows)] = dot_t(wo_ref[...], mbuf[...].reshape(2 * rows, model)).astype(BF16)

    loop(4, grad_ctx)
    tiles.finish(count)
    gather.links.finish()


def ctx_call(dx1, w_rows, z_saved, dfull):
    rows, model = dx1.shape
    feats = w_rows.shape[0]
    seq, hidden = z_saved.shape
    return comm_call(
        ctx_kernel, "ctx_grads", 2, 30_000_000_000, (dx1, w_rows, z_saved, dfull), [VMEM] * 2 + [HBM] * 2,
        [shape((seq // rows, rows, model), BF16), shape((feats, seq), BF16), shape((hidden, model), F32)], [HBM, VMEM, HBM],
        [pltpu.VMEM((2, rows, model), BF16), pltpu.VMEM((seq, hidden), BF16), pltpu.VMEM((hidden, seq), BF16),
         pltpu.VMEM((seq // rows, rows, model), BF16), pltpu.VMEM((2, hidden, OUT_TILE), F32),
         DMA(()), DMA(()), DMA((2,)), DMA((2,))] + [DMA((10,))] * 2)


def bwd_kernel(h2_ref, q_ref, k_ref, v_ref, do_ref, wide_ref, max_ref, inv_ref, dz_ref, h1_in,
               h1full, h2full, out_ref, dw1_ref,
               k_rows, v_rows, q_rows, do_rows, delta, dq_acc, dk_acc, dv_acc, tok, dzv, wbuf,
               own_sem, load_sem, out_sem, *comm_sems):
    place = Place()
    place.barrier()
    gather1 = ThirdGather(place, h1full, *comm_sems[0:2])
    gather2 = Gather(place, h2_ref, h2full, *comm_sems[2:4])
    gather2.start()
    own_copy = pltpu.make_async_copy(h2_ref, h2full.at[place.me], own_sem)
    own_copy.start()
    heads, dim, seq = q_ref.shape
    blocks = seq // BLK
    scale = dim ** -0.5
    exp_scale = scale * LOG2E

    def head(h):
        k_rows[...] = k_ref[h].T
        v_rows[...] = v_ref[h].T
        q_rows[...] = q_ref[h].T
        do_rows[...] = do_ref[h].T
        delta[...] = jnp.sum(do_ref[h].astype(F32) * wide_ref[h], axis=0, keepdims=True)
        dq_acc[...] = jnp.zeros_like(dq_acc)
        dk_acc[...] = jnp.zeros_like(dk_acc)
        dv_acc[...] = jnp.zeros_like(dv_acc)

        def block(qi, ki, on_diag):
            q_at, k_at = tile_at(qi, BLK), tile_at(ki, BLK)
            scores = dot(k_rows[k_at, :], q_ref[h, :, q_at])
            if on_diag:
                scores = causal_fill(scores, -1e30)
            probs = jnp.exp2((scores - max_ref[h, :, q_at]) * exp_scale) * inv_ref[h, :, q_at]
            grad_probs = dot(v_rows[k_at, :], do_ref[h, :, q_at])
            dv_acc[k_at, :] += dot(probs.astype(BF16), do_rows[q_at, :])
            grad_scores = (probs * (grad_probs - delta[:, q_at]) * scale).astype(BF16)
            dk_acc[k_at, :] += dot(grad_scores, q_rows[q_at, :])
            dq_acc[:, q_at] += dot(k_ref[h, :, k_at], grad_scores)

        loop(blocks, lambda i: block(i, i, True))
        loop(blocks, lambda ki: loop(blocks, lambda qi: block(qi, ki, False), ki + 1))
        out_ref[0, h] = dq_acc[...].astype(BF16)
        out_ref[1, h] = dk_acc[...].T.astype(BF16)
        out_ref[2, h] = dv_acc[...].T.astype(BF16)

    load_grad = pltpu.make_async_copy(dz_ref, dzv, load_sem.at[0])
    load_grad.start()
    count = tok.shape[2] // OUT_TILE
    tiles = Tiles(wbuf, dw1_ref, out_sem, rows=True)

    def fc1_tile(n):
        cols = tile_at(n, OUT_TILE)
        tiles.put(n, lambda: dot(flat_cols(tok, cols).T, dzv[...]))

    def head_step(h):
        head(h)

        @pl.when(h == 1)
        def _():
            gather2.relay()
            gather1.start(1, None)

        @pl.when(h == 2)
        def _():
            gather2.forward('X')
            gather2.forward('Y')

    loop(heads, head_step)
    gather2.forward('D')
    own_copy.wait()
    gather2.links.wait('CO', 'CX', 'CY', 'CD')
    load = pltpu.make_async_copy(h2full, tok, load_sem.at[1])
    load.start()
    load_grad.wait()
    load.wait()
    loop(count, fc1_tile)
    gather1.forward(1)
    gather1.wait_pair(1)
    tiles.finish(count)
    gather1.links.finish()
    gather2.links.finish()


def bwd_call(h2, q_t, k_t, v_t, do_t, wide, row_max, row_inv, dz, h1full):
    heads, dim, seq = q_t.shape
    rows, model = h2.shape
    full = shape((seq // rows, rows, model), BF16)
    turned = pltpu.VMEM((seq, dim), BF16)
    hidden = dz.shape[1]
    return comm_call(
        bwd_kernel, "attn_bwd", 3, 80_000_000_000,
        (h2, q_t, k_t, v_t, do_t, wide, row_max, row_inv, dz, h1full), [VMEM] * 8 + [HBM] * 2,
        [full, full, shape((3, heads, dim, seq), BF16), shape((model, hidden), F32)], [HBM, HBM, VMEM, HBM],
        [turned] * 4 + [pltpu.VMEM((1, seq), F32), pltpu.VMEM((dim, seq), F32), pltpu.VMEM((seq, dim), F32),
                        pltpu.VMEM((seq, dim), F32), pltpu.VMEM((seq // rows, rows, model), BF16),
                        pltpu.VMEM((seq, hidden), BF16), pltpu.VMEM((2, OUT_TILE, hidden), F32),
                        DMA(()), DMA((2,)), DMA((2,))] + [DMA((5,))] * 2 + [DMA((10,))] * 2,
        aliases={9: 0})


def qkv_kernel(qkv_ref, w_ref, dx1_ref, x_ref, affine_ref, vec_ref, ctx_ref, mfull, h1_in,
               dx_ref, vsum_ref, bias_ref, dwo_ref, dw_ref, h1full,
               turned, part, crecv, diag_recv, last_recv, vacc, vsend, vrecv, last_send, last_got, tok, obuf, wbuf,
               vsem, load_sem, out_sem, *comm_sems):
    place = Place()
    place.barrier()
    rows, model = dx1_ref.shape
    scatter = Scatter(place, part, crecv, diag_recv, last_recv, *comm_sems[0:2])
    gather = ThirdGather(place, h1full, *comm_sems[2:4])
    gather.start(2, None)
    loads = [pltpu.make_async_copy(src, tok, load_sem.at[i]) for i, src in enumerate((mfull, h1full))]
    loads[0].start()
    tiles_o = Tiles(obuf, dwo_ref, out_sem.at[0])
    tiles = Tiles(wbuf, dw_ref, out_sem.at[1])
    count = model // OUT_TILE
    swaps = Links(place, vsem.at[0], vsem.at[1])

    def vec_step(i):
        if i > 0:
            swaps.wait('CXY'[i - 1])
            vacc[...] += vrecv[i - 1]
        if i < 3:
            vsend[i] = vacc[...]

    def vec_send(i):
        swaps.send('CXY'[i], 'CXY'[i], vsend, vrecv, i)

    vacc[...] = vec_ref[...]
    vec_step(0)

    def pair_step(i):
        pair = place.pair_at(i)
        turned[...] = qkv_ref[:, tile_at(pair, 2 * rows)].T

        @pl.when(i == 3)
        def _():
            gather.forward(2)

        for at in range(3):
            @pl.when(i == at)
            def _():
                vec_send(at)

        scatter.between(i)

        def grad_norm(n):
            cols = tile_at(n, TILE)
            acc = dot(turned[...], w_ref[:, cols]).astype(BF16)
            part[2 * pair, :, cols] = acc[:rows]
            part[2 * pair + 1, :, cols] = acc[rows:]

        loop(model // TILE, grad_norm)
        scatter.after(i)

        for at in range(3):
            @pl.when(i == at)
            def _():
                vec_step(at + 1)

    loop(4, pair_step)
    loads[0].wait()

    def proj_tile(n):
        cols = tile_at(n, OUT_TILE)
        tiles_o.put(n, lambda: dot(ctx_ref[...], flat_cols(tok, cols)))

    def qkv_tile(n):
        cols = tile_at(n, OUT_TILE)
        tiles.put(n, lambda: dot(qkv_ref[...], flat_cols(tok, cols)))

    loop(count, proj_tile)
    scatter.add_diag()
    gather.wait_pair(2)
    loads[1].start()
    ones = jnp.ones((8, qkv_ref.shape[1]), BF16)
    bias_ref[...] = dot_t(ones, qkv_ref[...])
    loads[1].wait()
    loop(count, qkv_tile)
    scatter.wait_last()
    gain = affine_ref[0:1, :]

    def norm_rows(i):
        at = tile_at(i, LN_ROWS)
        grad = scatter.total(at)
        x_hat, inv_std = layer_norm_hat(x_ref[at, :].astype(F32))
        dx_ref[at, :] = (dx1_ref[at, :].astype(F32) + layer_norm_bwd(grad, x_hat, inv_std, gain)).astype(BF16)
        vacc[0:1, :] += jnp.sum(grad * x_hat, axis=0, keepdims=True)
        vacc[1:2, :] += jnp.sum(grad, axis=0, keepdims=True)

    loop(rows // LN_ROWS, norm_rows)
    finals = Links(place, vsem.at[2], vsem.at[3])
    total = vacc[0:2, :]
    for i, key in enumerate('CXY'):
        last_send[i] = total
        finals.send(key, key, last_send, last_got, i)
        if i == 0:
            tiles_o.finish(count)
            tiles.finish(count)
        finals.wait(key)
        total = total + last_got[i]
    vsum_ref[0:2, :] = total
    vsum_ref[2:6, :] = vacc[2:6, :]
    for links in (swaps, finals, scatter.links, gather.links):
        links.finish()


def qkv_call(qkv_rows, w_rows, dx1, x_in, affine, vec, ctx_rows, mfull, h1full):
    rows, model = dx1.shape
    feats, seq = qkv_rows.shape
    proj = ctx_rows.shape[0]
    return comm_call(
        qkv_kernel, "qkv_grads", 4, 30_000_000_000,
        (qkv_rows, w_rows, dx1, x_in, affine, vec, ctx_rows, mfull, h1full), [VMEM] * 7 + [HBM] * 2,
        [shape((rows, model), BF16), shape((6, model), F32), shape((8, feats), F32), shape((proj, model), F32),
         shape((feats, model), F32), shape(h1full.shape, BF16)],
        [VMEM] * 3 + [HBM] * 3,
        [pltpu.VMEM((2 * rows, feats), BF16)] + scatter_scratch(rows, model)
        + [pltpu.VMEM((8, model), F32), pltpu.VMEM((3, 8, model), F32), pltpu.VMEM((3, 8, model), F32),
           pltpu.VMEM((3, 2, model), F32), pltpu.VMEM((3, 2, model), F32), pltpu.VMEM((8, rows, model), BF16),
           pltpu.VMEM((2, proj, OUT_TILE), F32), pltpu.VMEM((2, feats, OUT_TILE), F32),
           DMA((4, 3)), DMA((2,)), DMA((2, 2))] + [DMA((10,))] * 2 + [DMA((5,))] * 2,
        aliases={8: 5})


def solution(mesh):
    def local_backward(x_in, x_mid, d_out, q_saved, k_saved, v_saved, z_saved, ln1_gain, ln1_bias, ln2_gain, ln2_bias, w_qkv, w_proj, w_fc1, w_fc2):
        x_in, x_mid, d_out, z_saved = x_in[0], x_mid[0], d_out[0], z_saved[0]
        heads, dim = q_saved.shape[2:]
        seq, model = z_saved.shape[0], x_in.shape[1]
        q_t, k_t, v_t = (v[0].transpose(1, 2, 0) for v in (q_saved, k_saved, v_saved))
        affine = jnp.stack([ln1_gain, ln1_bias, ln2_gain, ln2_bias])
        dfull, ctx_t, wide_t, row_max, row_inv, h1_local, h2_local = fwd_call(d_out, q_t, k_t, v_t, x_in, x_mid, affine)
        dx1, grad_pre, grad_bfc1, vec, h1_full = mlp_call(dfull, d_out, x_mid, affine, h1_local, z_saved, w_fc2, w_fc1)
        mfull, do_t, grad_wfc2 = ctx_call(dx1, w_proj.reshape(heads * dim, model), z_saved, dfull)
        h1_full, _, qkv_t, grad_wfc1 = bwd_call(
            h2_local, q_t, k_t, v_t, do_t.reshape(heads, dim, seq), wide_t, row_max, row_inv, grad_pre, h1_full)
        qkv_rows = qkv_t.reshape(3 * heads * dim, seq)
        w_rows = w_qkv.transpose(0, 2, 3, 1).reshape(3 * heads * dim, model)
        grad_x, grad_vecs, bias_rows, grad_wproj, grad_wqkv, _ = qkv_call(
            qkv_rows, w_rows, dx1, x_in, affine, vec, ctx_t.reshape(heads * dim, seq), mfull, h1_full)
        grad_wproj = grad_wproj.reshape(heads, dim, model)
        grad_wqkv = grad_wqkv.reshape(3, heads, dim, model).transpose(0, 3, 1, 2)
        grad_bqkv = bias_rows[0].reshape(3, heads, dim)
        return grad_x[None], grad_wqkv, grad_bqkv, grad_wproj, grad_wfc1, grad_bfc1[0], grad_wfc2, grad_vecs

    tok_spec = P('dp', 'tp', None)
    head_spec = P('dp', None, 'tp', None)
    in_specs = (tok_spec, tok_spec, tok_spec, head_spec, head_spec, head_spec, P('dp', None, 'tp'),
                P(None), P(None), P(None), P(None),
                P(None, None, 'tp', None), P('tp', None, None), P(None, 'tp'), P('tp', None))
    out_specs = (tok_spec, P('dp', None, 'tp', None), P('dp', 'tp', None), P(('dp', 'tp'), None, None),
                 P('dp', 'tp'), P(('dp', 'tp')), P(('dp', 'tp'), None), P('dp', None))
    return jax.shard_map(local_backward, mesh=mesh, in_specs=in_specs, out_specs=out_specs, check_vma=False)
```

time: 406 us -> 380 us (0.936); the launches traced: 399 us -> 380 us
  Pallas kernels: 350 us -> 339 us
  other arithmetic: 11.6 us -> 1.28 us
    pallas_call x5, Pallas kernels: 350 us -> 339 us  [comm_call(): pl.pallas_call(kernel, in_specs=in_specs, out_specs=out_specs, out_shape=...]
    reduce_sum x5 -> x0, other arithmetic: 7.59 us -> none  [the longest x1 3.32 us: local_backward(): grad_bqkv = jnp.sum(qkv_t, axis=3, dtype=F32)]
    unnamed x23 -> x12, local copies, waits for them, and re-layouts: 32.5 us -> 34.6 us
where the time goes in v4:
time: 380 us
  Pallas kernels  339 us (89%)
  local copies, waits for them, and re-layouts  38.9 us (10%)
    pallas_call x5, Pallas kernels, comm_call(): pl.pallas_call(kernel, in_specs=in_specs, out_specs=out_specs, out_shape=...  339 us
    unnamed x12, local copies, waits for them, and re-layouts  34.6 us

profile of v4, /device:TPU:0, one launch (start us, length us, event | category | flops | bytes accessed | tf_op | source)
XLA Modules:
  0.0 379.5 jit_solution(4409986020767224642)
XLA Ops:
  0.6 0.7 stack.15
  1.4 0.7 stack.16
  2.1 0.7 stack.17
  2.8 0.7 stack.18
  3.5 0.7 pad_maximum_fusion.affine_ref
  4.2 56.2 %attn_fwd.1 = (bf16[8,256,2560]{2,1,0:T(8,128)(2,1)}, bf16[4,80,2048]{2,1,0:T(8,128)(2,1)}, f32[4,80,2048]{2,1,0:T(8,128)}, f32[4,1,2048]{2,1,0:T(1,128)}, f32[4...) custom-call(bf16[256,2560]{1,0:T(8,128)(2,1)} %bitcast.32, bf16[4,80,2048]{2,1,0:T(8,128)(2,1)} %bitcast.36, ...), custom_call_target="tpu_custom_call" | custom-call | flops 40000000000 | bytes 40000000 | tf_op jit(solution)/shard_map/attn_fwd/pallas_call | solution.py:272
  60.4 75.8 %mlp_grads.1 = (bf16[256,2560]{1,0:T(8,128)(2,1)}, bf16[2048,1280]{1,0:T(8,128)(2,1)}, f32[1,1280]{1,0:T(1,128)}, f32[8,2560]{1,0:T(8,128)}, bf16[8,256,2560]{2,1,0:T(8,128)(2,1)}) custom-call(bf16[8,256,2560]{2,1,0:T(8,128)(2,1)} %get-tuple-element.32.dfull, bf16[256,2560]{1,0:T(8,128)(2,1)} %bitcast.33, bf16[256,2560]{1,0:T(8,128)(2,1)} %bitcast.35, ...), custom_call_target="tpu_custom_call" | custom-call | flops 60000002048 | bytes 40000000 | tf_op jit(solution)/shard_map/mlp_grads/pallas_call | solution.py:272
  136.1 51.8 %ctx_grads.1 = (bf16[8,256,2560]{2,1,0:T(8,128)(2,1)}, bf16[320,2048]{1,0:T(8,128)(2,1)}, f32[1280,2560]{1,0:T(8,128)}) custom-call(bf16[256,2560]{1,0:T(8,128)(2,1)} %get-tuple-element.34.dx1_ref, bf16[320,2560]{1,0:T(8,128)(2,1)} %bitcast.31, bf16[2048,1280]{1,0:T(8,128)(2,1)} %bitcast.29, bf16[8,256,2560]{2,1,0:T(8,128)(2,1)} %get-tuple-element.32.dfull), custom_call_target="tpu_custom_call" | custom-call | flops 30000001024 | bytes 40000000 | tf_op jit(solution)/shard_map/ctx_grads/pallas_call | solution.py:272
  187.9 76.2 %attn_bwd.1 = (bf16[8,256,2560]{2,1,0:T(8,128)(2,1)}, bf16[8,256,2560]{2,1,0:T(8,128)(2,1)}, bf16[3,4,80,2048]{3,2,1,0:T(8,128)(2,1)}, f32[2560,1280]{1,0:T(8,128)}) custom-call(bf16[256,2560]{1,0:T(8,128)(2,1)} %get-tuple-element.31.h2_ref, bf16[4,80,2048]{2,1,0:T(8,128)(2,1)} %bitcast.37, ...), custom_call_target="tpu_custom_call", output_to_operand_aliasing={{0}: (9, {})} | custom-call | flops 80000000000 | bytes 40000000 | tf_op jit(solution)/shard_map/attn_bwd/pallas_call | solution.py:272
  264.2 0.0 copy-start.2
  264.2 78.7 %qkv_grads.1 = (bf16[256,2560]{1,0:T(8,128)(2,1)}, f32[6,2560]{1,0:T(8,128)}, f32[8,960]{1,0:T(8,128)}, f32[320,2560]{1,0:T(8,128)}, f32[960,2560]{1,0:T(8,128)}, /*index=5*/bf16[8,256,2560]{2,1,0:T(8,128)(2,1)}) custom-call(bf16[960,2048]{1,0:T(8,128)(2,1)} %bitcast.44, bf16[960,2560]{1,0:T(8,128)(2,1)} %bitcast.30, ...), custom_call_target="tpu_custom_call", output_to_operand_aliasing={{5}: (8, {})} | custom-call | flops 30000001024 | bytes 40000000 | tf_op jit(solution)/shard_map/qkv_grads/pallas_call | solution.py:272
  342.9 0.8 slice_reduce_fusion
  343.7 0.7 reshape_squeeze.3
  344.3 0.0 copy-done.2
  344.3 0.6 reduce.1
  344.9 2.5 copy.33
  347.4 0.0 copy-start
  347.4 8.5 %copy.34 = f32[3,2560,4,80]{1,3,2,0:T(8,128)} copy(f32[3,2560,4,80]{1,3,2,0:T(8,128)} %bitcast.25) | data formatting | bytes 19660800
  355.9 0.0 copy-done
  355.9 1.7 copy.35
  357.6 10.5 %copy.36 = f32[2560,1280]{1,0:T(8,128)} copy(f32[2560,1280]{1,0:T(8,128)} %get-tuple-element.66) | data formatting | bytes 26214400
  368.1 0.0 copy-start.1
  368.1 10.8 %copy.37 = f32[1280,2560]{1,0:T(8,128)} copy(f32[1280,2560]{1,0:T(8,128)} %get-tuple-element.68) | data formatting | bytes 26214400
  378.9 0.0 copy-done.1
  378.9 0.6 copy.38
Async XLA Ops:
  264.2 80.2 %copy-start.2 = (f32[1,1280]{1,0:T(1,128)S(1)}, f32[1,1280]{1,0:T(1,128)}, u32[]{:S(2)}) copy-start(f32[1,1280]{1,0:T(1,128)} %get-tuple-element.51) | copy-start | bytes 15364
  347.4 8.5 %copy-start = (f32[320,2560]{1,0:T(8,128)S(1)}, f32[320,2560]{1,0:T(8,128)}, u32[]{:S(2)}) copy-start(f32[320,2560]{1,0:T(8,128)} %get-tuple-element.49) | copy-start | bytes 9830404
  368.1 10.8 %copy-start.1 = (f32[6,2560]{1,0:T(8,128)S(1)}, f32[6,2560]{1,0:T(8,128)}, u32[]{:S(2)}) copy-start(f32[6,2560]{1,0:T(8,128)} %get-tuple-element.69) | copy-start | bytes 184324

commit v5 on v4

--- a/solution.py
+++ b/solution.py
@@ -39,6 +39,7 @@
         self.dy = 4 - 8 * (self.me // 4)
         self.dc = 1 - 2 * self.core
         self.peer = {'X': self.me + self.dx, 'Y': self.me + self.dy, 'C': self.me + self.dc}
+        self.peer.update({k: (self.me + k) % 8 for k in range(1, 8)})
         self.block = {'O': self.me, 'X': self.me + self.dx, 'Y': self.me + self.dy, 'D': self.me + self.dx + self.dy}
         self.other = {key: val + self.dc for key, val in self.block.items()}
         self.x, self.y = (self.me // 2) % 2, self.me // 4
@@ -47,11 +48,12 @@
         flip_x, flip_y = 1 - i // 2, 1 - i % 2
         return 2 * (self.y + flip_y * (1 - 2 * self.y)) + self.x + flip_x * (1 - 2 * self.x)
 
-    def barrier(self):
+    def barrier(self, everyone=False):
         sem = pltpu.get_barrier_semaphore()
-        for key in 'XYC':
+        keys = range(1, 8) if everyone else 'XYC'
+        for key in keys:
             pl.semaphore_signal(sem, inc=1, device_id=(self.group, self.peer[key]), device_id_type=pl.DeviceIdType.MESH)
-        pl.semaphore_wait(sem, 3)
+        pl.semaphore_wait(sem, len(keys))
 
 
 class Links:
@@ -198,16 +200,36 @@
             self.links.send('D' + half, key, (self.part, (self.place.block['D'], self.half[half])), (self.diag_recv, (i,)))
 
     def add_diag(self):
-        rows = self.part.shape[1] // 2
-        self.links.wait('Da')
-        self.add_rows(self.place.block['Y'], 0, rows, self.diag_recv.at[0], 0)
-        self.links.wait('Db')
-        self.add_rows(self.place.block['X'], rows, rows, self.diag_recv.at[1], 0)
-        self.send_half('Y', 'a')
-        self.send_half('X', 'b')
-
-    def wait_last(self):
-        self.links.wait('Xa', 'Xb', 'Ya', 'Yb', 'CO')
+        rows = self.part.shape[1] // 4
+        for i, (half, key, start) in enumerate((('a', 'Y', 0), ('b', 'X', 2 * rows))):
+            self.links.wait('D' + half)
+            for quarter in range(2):
+                off = quarter * rows
+                self.add_rows(self.place.block[key], start + off, rows, self.diag_recv.at[i], off)
+                at = pl.ds(start + off, rows)
+                self.links.send(key + half + str(quarter), key, (self.part, (self.place.block[key], at)),
+                                (self.last_recv, ('XY'.index(key), at)))
+
+    def wait_last(self, quarter):
+        if quarter == 0:
+            self.links.wait('Xa', 'Yb', 'CO')
+        self.links.wait('Ya' + str(quarter), 'Xb' + str(quarter))
+
+    def norm_loop(self, body):
+        rows = self.part.shape[1]
+        chunks = rows // LN_ROWS
+        quarter = chunks // 4
+
+        def step(i):
+            for part in range(2):
+                @pl.when(i == part * (chunks // 2))
+                def _():
+                    self.wait_last(part)
+
+            part, j = i // (2 * quarter), i % (2 * quarter)
+            body(tile_at((j // quarter) * 2 * quarter + part * quarter + j % quarter, LN_ROWS))
+
+        loop(chunks, step)
 
     def between(self, i):
         @pl.when(i == 1)
@@ -258,6 +280,13 @@
 
 def tile_at(i, size):
     return pl.ds(pl.multiple_of(i * size, size), size)
+
+
+def start_copies(sem, *pairs):
+    copies = [pltpu.make_async_copy(src, dst, sem.at[i]) for i, (src, dst) in enumerate(pairs)]
+    for copy in copies:
+        copy.start()
+    return copies
 
 
 def loop(count, body, start=0):
@@ -307,25 +336,31 @@
     return ref[:, :, cols].reshape(ref.shape[0] * ref.shape[1], OUT_TILE)
 
 
-def fwd_kernel(dout_ref, q_ref, k_ref, v_ref, x_ref, mid_ref, affine_ref,
-               dfull, ctx_ref, wide_ref, max_ref, inv_ref, h1_ref, h2_ref, k_rows, strip, own_sem, *comm_sems):
+def fwd_kernel(dout_ref, q_hbm, k_hbm, v_hbm, x_hbm, mid_hbm, gain1_ref, bias1_ref, gain2_ref, bias2_ref,
+               dfull, ctx_ref, wide_ref, max_ref, inv_ref, h1_ref, h2_ref,
+               k_rows, strip, q_ref, k_ref, v_ref, x_ref, mid_ref, own_sem, load_sem, *comm_sems):
     place = Place()
     place.barrier()
     gather = Gather(place, dout_ref, dfull, *comm_sems)
     gather.start()
+    loads = start_copies(load_sem, (x_hbm, x_ref), (mid_hbm, mid_ref), (k_hbm, k_ref), (q_hbm, q_ref), (v_hbm, v_ref))
     own_copy = pltpu.make_async_copy(dout_ref, dfull.at[place.me], own_sem)
     own_copy.start()
     heads, dim, seq = q_ref.shape
     exp_scale = dim ** -0.5 * LOG2E
-    affine = affine_ref[...]
+    loads[0].wait()
+    loads[1].wait()
+    affine = [ref[...].reshape(1, ref.shape[0]) for ref in (gain1_ref, bias1_ref, gain2_ref, bias2_ref)]
 
     def norm_rows(i):
         at = tile_at(i, LN_ROWS)
         for row, (src, dst) in enumerate(((x_ref, h1_ref), (mid_ref, h2_ref))):
             x_hat, _ = layer_norm_hat(src[at, :].astype(F32))
-            dst[at, :] = (x_hat * affine[2 * row:2 * row + 1] + affine[2 * row + 1:2 * row + 2]).astype(BF16)
+            dst[at, :] = (x_hat * affine[2 * row] + affine[2 * row + 1]).astype(BF16)
 
     loop(x_ref.shape[0] // LN_ROWS, norm_rows)
+    for copy in loads[2:]:
+        copy.wait()
 
     def head(h):
         k_rows[...] = k_ref[h].T
@@ -393,24 +428,26 @@
     heads, dim, seq = q_t.shape
     rows, model = d_out.shape
     return comm_call(
-        fwd_kernel, "attn_fwd", 0, 40_000_000_000, (d_out, q_t, k_t, v_t, x_in, x_mid, affine), [VMEM] * 7,
+        fwd_kernel, "attn_fwd", 0, 40_000_000_000, (d_out, q_t, k_t, v_t, x_in, x_mid, *affine),
+        [VMEM] + [HBM] * 5 + [VMEM] * 4,
         [shape((seq // rows, rows, model), BF16), shape((heads, dim, seq), BF16), shape((heads, dim, seq), F32),
          shape((heads, 1, seq), F32), shape((heads, 1, seq), F32), shape((rows, model), BF16), shape((rows, model), BF16)],
         [HBM] + [VMEM] * 6,
-        [pltpu.VMEM((seq, dim), BF16), pltpu.VMEM((seq, BLK), F32), DMA(())] + [DMA((10,))] * 2)
+        [pltpu.VMEM((seq, dim), BF16), pltpu.VMEM((seq, BLK), F32)] + [pltpu.VMEM(q_t.shape, BF16)] * 3
+        + [pltpu.VMEM((rows, model), BF16)] * 2 + [DMA(()), DMA((5,))] + [DMA((10,))] * 2)
 
 
 def dot_t(a, b):
     return lax.dot_general(a, b, (((1,), (1,)), ((), ())), preferred_element_type=F32)
 
 
-def mlp_kernel(dfull, dout_ref, mid_ref, affine_ref, h1_ref, z_ref, w2_ref, w1_ref,
+def mlp_kernel(dfull, dout_hbm, mid_hbm, gain_ref, h1_ref, z_ref, w2_ref, w1_ref,
                dx1_ref, dz_ref, gb1_ref, vec_ref, h1full,
-               w2v, w1v, zv, dzv, ybuf, part, crecv, diag_recv, last_recv,
-               load_sem, y_sem, dz_sem, own_sem, *comm_sems):
+               w2v, w1v, dzv, ybuf, part, crecv, diag_recv, last_recv, dout_ref, mid_ref,
+               load_sem, y_sem, z_sem, dz_sem, own_sem, *comm_sems):
     place = Place()
     place.barrier()
-    rows, model = dout_ref.shape
+    rows, model = dout_hbm.shape
     hidden = w2v.shape[0]
     scatter = Scatter(place, part, crecv, diag_recv, last_recv, *comm_sems[0:2])
     gather = ThirdGather(place, h1full, *comm_sems[2:4])
@@ -424,28 +461,32 @@
         at = tile_at(place.pair_at(i), 2 * rows)
         return pltpu.make_async_copy(dzv.at[at], dz_ref.at[at], dz_sem.at[i])
 
+    def load_pre(i):
+        at = tile_at(place.pair_at(i), 2 * rows)
+        return pltpu.make_async_copy(z_ref.at[at], dzv.at[at], z_sem.at[i])
+
     load_pair(0).start()
-    loads = [pltpu.make_async_copy(src, dst, load_sem.at[i])
-             for i, (src, dst) in enumerate(((w2_ref, w2v), (z_ref, zv), (w1_ref, w1v)))]
-    for copy in loads:
-        copy.start()
+    load_pre(0).start()
+    loads = start_copies(load_sem, (w2_ref, w2v), (w1_ref, w1v), (dout_hbm, dout_ref), (mid_hbm, mid_ref))
+    for i in range(1, 4):
+        load_pre(i).start()
     load_pair(1).start()
     own_copy.start()
     gb1_ref[...] = jnp.zeros_like(gb1_ref)
     vec_ref[...] = jnp.zeros_like(vec_ref)
     loads[0].wait()
-    loads[1].wait()
 
     def pair_step(i):
         slot = i % 2
         pair = place.pair_at(i)
         at = tile_at(pair, 2 * rows)
         load_pair(i).wait()
+        load_pre(i).wait()
 
         def grad_act(n):
             cols = tile_at(n, TILE)
             acc = dot_t(ybuf[slot].reshape(2 * rows, model), w2v[cols, :])
-            grad = (acc * gelu_slope(zv[at, cols].astype(F32))).astype(BF16)
+            grad = (acc * gelu_slope(dzv[at, cols].astype(F32))).astype(BF16)
             dzv[at, cols] = grad
             gb1_ref[:, cols] += jnp.sum(grad.astype(F32), axis=0, keepdims=True)
 
@@ -458,7 +499,7 @@
 
         @pl.when(i == 0)
         def _():
-            loads[2].wait()
+            loads[1].wait()
 
         @pl.when(i == 2)
         def _():
@@ -477,12 +518,12 @@
 
     loop(4, pair_step)
     scatter.add_diag()
-    scatter.wait_last()
-
-    gain = affine_ref[2:3, :]
-
-    def norm_rows(i):
-        at = tile_at(i, LN_ROWS)
+
+    gain = gain_ref[...].reshape(1, model)
+    loads[2].wait()
+    loads[3].wait()
+
+    def norm_rows(at):
         grad = scatter.total(at)
         x_hat, inv_std = layer_norm_hat(mid_ref[at, :].astype(F32))
         dout_rows = dout_ref[at, :].astype(F32)
@@ -491,7 +532,7 @@
         for row, val in enumerate((grad * x_hat, grad, mid.astype(F32), dout_rows)):
             vec_ref[row + 2:row + 3, :] += jnp.sum(val, axis=0, keepdims=True)
 
-    loop(rows // LN_ROWS, norm_rows)
+    scatter.norm_loop(norm_rows)
     for i in range(4):
         store_grad(i).wait()
     own_copy.wait()
@@ -505,18 +546,19 @@
             pltpu.VMEM((2, rows // 2, model), BF16), pltpu.VMEM((2, rows, model), BF16)]
 
 
-def mlp_call(dfull, d_out, x_mid, affine, h1, z_saved, w2, w1):
+def mlp_call(dfull, d_out, x_mid, gain, h1, z_saved, w2, w1):
     rows, model = d_out.shape
     seq, hidden = z_saved.shape
     return comm_call(
-        mlp_kernel, "mlp_grads", 1, 60_000_000_000, (dfull, d_out, x_mid, affine, h1, z_saved, w2, w1),
-        [HBM] + [VMEM] * 3 + [HBM] * 4,
+        mlp_kernel, "mlp_grads", 1, 60_000_000_000, (dfull, d_out, x_mid, gain, h1, z_saved, w2, w1),
+        [HBM] * 3 + [VMEM] + [HBM] * 4,
         [shape((rows, model), BF16), shape((seq, hidden), BF16), shape((1, hidden), F32), shape((8, model), F32),
          shape(dfull.shape, BF16)],
         [VMEM, HBM, VMEM, VMEM, HBM],
         [pltpu.VMEM((hidden, model), BF16), pltpu.VMEM((model, hidden), BF16),
-         pltpu.VMEM((seq, hidden), BF16), pltpu.VMEM((seq, hidden), BF16), pltpu.VMEM((2, 2, rows, model), BF16)]
-        + scatter_scratch(rows, model) + [DMA((3,)), DMA((4,)), DMA((4,)), DMA(())] + [DMA((10,))] * 2 + [DMA((5,))] * 2)
+         pltpu.VMEM((seq, hidden), BF16), pltpu.VMEM((2, 2, rows, model), BF16)]
+        + scatter_scratch(rows, model) + [pltpu.VMEM((rows, model), BF16)] * 2
+        + [DMA((4,))] * 4 + [DMA(())] + [DMA((12,))] * 2 + [DMA((5,))] * 2)
 
 
 def gelu(pre_act):
@@ -594,15 +636,16 @@
          DMA(()), DMA(()), DMA((2,)), DMA((2,))] + [DMA((10,))] * 2)
 
 
-def bwd_kernel(h2_ref, q_ref, k_ref, v_ref, do_ref, wide_ref, max_ref, inv_ref, dz_ref, h1_in,
+def bwd_kernel(h2_ref, q_hbm, k_hbm, v_hbm, do_hbm, wide_hbm, max_ref, inv_ref, dz_ref, h1_in,
                h1full, h2full, out_ref, dw1_ref,
                k_rows, v_rows, q_rows, do_rows, delta, dq_acc, dk_acc, dv_acc, tok, dzv, wbuf,
-               own_sem, load_sem, out_sem, *comm_sems):
+               q_ref, k_ref, v_ref, do_ref, wide_ref, own_sem, head_sem, load_sem, out_sem, *comm_sems):
     place = Place()
     place.barrier()
     gather1 = ThirdGather(place, h1full, *comm_sems[0:2])
     gather2 = Gather(place, h2_ref, h2full, *comm_sems[2:4])
     gather2.start()
+    loads = start_copies(head_sem, (k_hbm, k_ref), (v_hbm, v_ref), (q_hbm, q_ref), (do_hbm, do_ref), (wide_hbm, wide_ref))
     own_copy = pltpu.make_async_copy(h2_ref, h2full.at[place.me], own_sem)
     own_copy.start()
     heads, dim, seq = q_ref.shape
@@ -635,11 +678,17 @@
         loop(blocks, lambda i: block(i, i, True))
         loop(blocks, lambda ki: loop(blocks, lambda qi: block(qi, ki, False), ki + 1))
         out_ref[0, h] = dq_acc[...].astype(BF16)
-        out_ref[1, h] = dk_acc[...].T.astype(BF16)
-        out_ref[2, h] = dv_acc[...].T.astype(BF16)
-
-    load_grad = pltpu.make_async_copy(dz_ref, dzv, load_sem.at[0])
-    load_grad.start()
+        out_ref[1, h] = dk_acc[...].astype(BF16).T
+        out_ref[2, h] = dv_acc[...].astype(BF16).T
+
+    load_grad = pltpu.make_async_copy(dz_ref, dzv, load_sem.at[4])
+
+    def load_tok(i):
+        at = pl.ds(2 * place.pair_at(i), 2)
+        return pltpu.make_async_copy(h2full.at[at], tok.at[at], load_sem.at[i])
+
+    for copy in loads:
+        copy.wait()
     count = tok.shape[2] // OUT_TILE
     tiles = Tiles(wbuf, dw1_ref, out_sem, rows=True)
 
@@ -657,17 +706,23 @@
 
         @pl.when(h == 2)
         def _():
+            load_grad.start()
             gather2.forward('X')
             gather2.forward('Y')
+            own_copy.wait()
+            gather2.links.wait('CO')
+            load_tok(3).start()
 
     loop(heads, head_step)
     gather2.forward('D')
-    own_copy.wait()
-    gather2.links.wait('CO', 'CX', 'CY', 'CD')
-    load = pltpu.make_async_copy(h2full, tok, load_sem.at[1])
-    load.start()
+    gather2.links.wait('CX', 'CY')
+    load_tok(1).start()
+    load_tok(2).start()
     load_grad.wait()
-    load.wait()
+    gather2.links.wait('CD')
+    load_tok(0).start()
+    for i in range(4):
+        load_tok(i).wait()
     loop(count, fc1_tile)
     gather1.forward(1)
     gather1.wait_pair(1)
@@ -684,31 +739,33 @@
     hidden = dz.shape[1]
     return comm_call(
         bwd_kernel, "attn_bwd", 3, 80_000_000_000,
-        (h2, q_t, k_t, v_t, do_t, wide, row_max, row_inv, dz, h1full), [VMEM] * 8 + [HBM] * 2,
+        (h2, q_t, k_t, v_t, do_t, wide, row_max, row_inv, dz, h1full), [VMEM] + [HBM] * 5 + [VMEM] * 2 + [HBM] * 2,
         [full, full, shape((3, heads, dim, seq), BF16), shape((model, hidden), F32)], [HBM, HBM, VMEM, HBM],
         [turned] * 4 + [pltpu.VMEM((1, seq), F32), pltpu.VMEM((dim, seq), F32), pltpu.VMEM((seq, dim), F32),
                         pltpu.VMEM((seq, dim), F32), pltpu.VMEM((seq // rows, rows, model), BF16),
                         pltpu.VMEM((seq, hidden), BF16), pltpu.VMEM((2, OUT_TILE, hidden), F32),
-                        DMA(()), DMA((2,)), DMA((2,))] + [DMA((5,))] * 2 + [DMA((10,))] * 2,
+                        *[pltpu.VMEM(q_t.shape, BF16)] * 4, pltpu.VMEM(wide.shape, F32),
+                        DMA(()), DMA((5,)), DMA((5,)), DMA((2,))] + [DMA((5,))] * 2 + [DMA((10,))] * 2,
         aliases={9: 0})
 
 
-def qkv_kernel(qkv_ref, w_ref, dx1_ref, x_ref, affine_ref, vec_ref, ctx_ref, mfull, h1_in,
+def qkv_kernel(qkv_hbm, w_hbm, dx1_hbm, x_hbm, gain_ref, vec_ref, ctx_hbm, mfull, h1_in,
                dx_ref, vsum_ref, bias_ref, dwo_ref, dw_ref, h1full,
-               turned, part, crecv, diag_recv, last_recv, vacc, vsend, vrecv, last_send, last_got, tok, obuf, wbuf,
-               vsem, load_sem, out_sem, *comm_sems):
+               turned, part, crecv, diag_recv, last_recv, vacc, vsend, vrecv, last_got, tok, obuf, wbuf,
+               qkv_ref, w_ref, dx1_ref, x_ref, ctx_ref, vsem, last_sem, load_sem, in_sem, out_sem, *comm_sems):
     place = Place()
-    place.barrier()
+    place.barrier(everyone=True)
     rows, model = dx1_ref.shape
     scatter = Scatter(place, part, crecv, diag_recv, last_recv, *comm_sems[0:2])
     gather = ThirdGather(place, h1full, *comm_sems[2:4])
     gather.start(2, None)
+    inputs = start_copies(in_sem, (qkv_hbm, qkv_ref), (w_hbm, w_ref), (ctx_hbm, ctx_ref), (dx1_hbm, dx1_ref), (x_hbm, x_ref))
     loads = [pltpu.make_async_copy(src, tok, load_sem.at[i]) for i, src in enumerate((mfull, h1full))]
-    loads[0].start()
     tiles_o = Tiles(obuf, dwo_ref, out_sem.at[0])
     tiles = Tiles(wbuf, dw_ref, out_sem.at[1])
     count = model // OUT_TILE
     swaps = Links(place, vsem.at[0], vsem.at[1])
+    inputs[0].wait()
 
     def vec_step(i):
         if i > 0:
@@ -722,18 +779,28 @@
 
     vacc[...] = vec_ref[...]
     vec_step(0)
+    vec_send(0)
 
     def pair_step(i):
         pair = place.pair_at(i)
         turned[...] = qkv_ref[:, tile_at(pair, 2 * rows)].T
 
+        @pl.when(i == 0)
+        def _():
+            inputs[1].wait()
+
+        @pl.when(i == 1)
+        def _():
+            loads[0].start()
+
         @pl.when(i == 3)
         def _():
             gather.forward(2)
 
-        for at in range(3):
+        for at in range(1, 3):
             @pl.when(i == at)
             def _():
+                vec_step(at)
                 vec_send(at)
 
         scatter.between(i)
@@ -747,13 +814,10 @@
         loop(model // TILE, grad_norm)
         scatter.after(i)
 
-        for at in range(3):
-            @pl.when(i == at)
-            def _():
-                vec_step(at + 1)
-
     loop(4, pair_step)
     loads[0].wait()
+    for copy in inputs[2:]:
+        copy.wait()
 
     def proj_tile(n):
         cols = tile_at(n, OUT_TILE)
@@ -771,50 +835,116 @@
     bias_ref[...] = dot_t(ones, qkv_ref[...])
     loads[1].wait()
     loop(count, qkv_tile)
-    scatter.wait_last()
-    gain = affine_ref[0:1, :]
-
-    def norm_rows(i):
-        at = tile_at(i, LN_ROWS)
+    vec_step(3)
+    tiles_o.finish(count)
+    gain = gain_ref[...].reshape(1, model)
+
+    def norm_rows(at):
         grad = scatter.total(at)
         x_hat, inv_std = layer_norm_hat(x_ref[at, :].astype(F32))
         dx_ref[at, :] = (dx1_ref[at, :].astype(F32) + layer_norm_bwd(grad, x_hat, inv_std, gain)).astype(BF16)
         vacc[0:1, :] += jnp.sum(grad * x_hat, axis=0, keepdims=True)
         vacc[1:2, :] += jnp.sum(grad, axis=0, keepdims=True)
 
-    loop(rows // LN_ROWS, norm_rows)
-    finals = Links(place, vsem.at[2], vsem.at[3])
-    total = vacc[0:2, :]
-    for i, key in enumerate('CXY'):
-        last_send[i] = total
-        finals.send(key, key, last_send, last_got, i)
-        if i == 0:
-            tiles_o.finish(count)
-            tiles.finish(count)
-        finals.wait(key)
-        total = total + last_got[i]
+    scatter.norm_loop(norm_rows)
+    finals = Links(place, last_sem.at[0], last_sem.at[1])
+    last_got[0] = vacc[0:2, :]
+    vsum_ref[2:6, :] = vacc[2:6, :]
+    for k in range(1, 8):
+        finals.send(k, k, (last_got, (0,)), (last_got, (k,)))
+    tiles.finish(count)
+    finals.wait(*range(1, 8))
+    total = last_got[place.me]
+    for source in range(1, 8):
+        total += last_got[(place.me + 8 - source) % 8]
     vsum_ref[0:2, :] = total
-    vsum_ref[2:6, :] = vacc[2:6, :]
     for links in (swaps, finals, scatter.links, gather.links):
         links.finish()
 
 
-def qkv_call(qkv_rows, w_rows, dx1, x_in, affine, vec, ctx_rows, mfull, h1full):
+def qkv_call(qkv_rows, w_rows, dx1, x_in, gain, vec, ctx_rows, mfull, h1full):
     rows, model = dx1.shape
     feats, seq = qkv_rows.shape
     proj = ctx_rows.shape[0]
     return comm_call(
         qkv_kernel, "qkv_grads", 4, 30_000_000_000,
-        (qkv_rows, w_rows, dx1, x_in, affine, vec, ctx_rows, mfull, h1full), [VMEM] * 7 + [HBM] * 2,
+        (qkv_rows, w_rows, dx1, x_in, gain, vec, ctx_rows, mfull, h1full), [HBM] * 4 + [VMEM] * 2 + [HBM] * 3,
         [shape((rows, model), BF16), shape((6, model), F32), shape((8, feats), F32), shape((proj, model), F32),
          shape((feats, model), F32), shape(h1full.shape, BF16)],
         [VMEM] * 3 + [HBM] * 3,
         [pltpu.VMEM((2 * rows, feats), BF16)] + scatter_scratch(rows, model)
         + [pltpu.VMEM((8, model), F32), pltpu.VMEM((3, 8, model), F32), pltpu.VMEM((3, 8, model), F32),
-           pltpu.VMEM((3, 2, model), F32), pltpu.VMEM((3, 2, model), F32), pltpu.VMEM((8, rows, model), BF16),
+           pltpu.VMEM((8, 2, model), F32), pltpu.VMEM((8, rows, model), BF16),
            pltpu.VMEM((2, proj, OUT_TILE), F32), pltpu.VMEM((2, feats, OUT_TILE), F32),
-           DMA((4, 3)), DMA((2,)), DMA((2, 2))] + [DMA((10,))] * 2 + [DMA((5,))] * 2,
+           pltpu.VMEM((feats, seq), BF16), pltpu.VMEM((feats, model), BF16), pltpu.VMEM((rows, model), BF16),
+           pltpu.VMEM((rows, model), BF16), pltpu.VMEM((proj, seq), BF16),
+           DMA((2, 3)), DMA((2, 7)), DMA((2,)), DMA((5,)), DMA((2, 2))] + [DMA((12,))] * 2 + [DMA((5,))] * 2,
         aliases={8: 5})
+
+
+def finish_kernel(*refs):
+    count = (len(refs) - 8) // 2
+    rings, single, (small_sem, in_sem, out_sem) = refs[2 * count:2 * count + 2], refs[-6:-3], refs[-3:]
+    chunks, used = [], [0, 0]
+    small = [(src, buf, dst) for src, buf, dst in zip(refs[4:count], single, refs[count + 4:2 * count])]
+    for i, (src, buf, _) in enumerate(small):
+        pltpu.make_async_copy(src, buf, small_sem.at[0, i]).start()
+    for src, dst in zip(refs[:4], refs[count:count + 4]):
+        kind = 0 if src.shape[1] == rings[0].shape[2] else 1
+        rows = rings[kind].shape[1]
+        for row in range(0, src.shape[0], rows):
+            chunks.append((src.at[pl.ds(row, rows)], dst.at[pl.ds(row, rows)], kind, used[kind]))
+            used[kind] += 1
+
+    def copy_in(src, dst, kind, at):
+        slot = at % RING
+        return pltpu.make_async_copy(src, rings[kind].at[slot], in_sem.at[kind, slot])
+
+    def copy_out(src, dst, kind, at):
+        slot = at % RING
+        return pltpu.make_async_copy(rings[kind].at[slot], dst, out_sem.at[kind, slot])
+
+    waiting = {}
+
+    def start(chunk):
+        key = (chunk[2], chunk[3] % RING)
+        if key in waiting:
+            copy_out(*waiting.pop(key)).wait()
+        copy_in(*chunk).start()
+
+    for chunk in chunks[:AHEAD]:
+        start(chunk)
+    for i, (src, buf, dst) in enumerate(small):
+        pltpu.make_async_copy(src, buf, small_sem.at[0, i]).wait()
+        pltpu.make_async_copy(buf, dst, small_sem.at[1, i]).start()
+    for i, chunk in enumerate(chunks):
+        copy_in(*chunk).wait()
+        copy_out(*chunk).start()
+        waiting[(chunk[2], chunk[3] % RING)] = chunk
+        if i + AHEAD < len(chunks):
+            start(chunks[i + AHEAD])
+    for chunk in waiting.values():
+        copy_out(*chunk).wait()
+    for i, (_, buf, dst) in enumerate(small):
+        pltpu.make_async_copy(buf, dst, small_sem.at[1, i]).wait()
+
+
+RING = 32
+AHEAD = 20
+
+
+def finish_call(*arrays):
+    wide = max(a.shape[1] for a in arrays[:4])
+    narrow = min(a.shape[1] for a in arrays[:4])
+    small = [pltpu.VMEM(a.shape, a.dtype) for a in arrays[4:]]
+    return pl.pallas_call(
+        finish_kernel, name="finish", in_specs=[HBM] * len(arrays), out_specs=[HBM] * len(arrays),
+        out_shape=[shape(a.shape, a.dtype) for a in arrays],
+        scratch_shapes=[pltpu.VMEM((RING, 64, wide), F32), pltpu.VMEM((RING, 128, narrow), F32), *small,
+                        DMA((2, len(small))), DMA((2, RING)), DMA((2, RING))],
+        compiler_params=pltpu.CompilerParams(vmem_limit_bytes=66_000_000),
+        cost_estimate=pl.CostEstimate(flops=1_000_000, bytes_accessed=72_000_000, transcendentals=0),
+    )(*arrays)
 
 
 def solution(mesh):
@@ -823,16 +953,18 @@
         heads, dim = q_saved.shape[2:]
         seq, model = z_saved.shape[0], x_in.shape[1]
         q_t, k_t, v_t = (v[0].transpose(1, 2, 0) for v in (q_saved, k_saved, v_saved))
-        affine = jnp.stack([ln1_gain, ln1_bias, ln2_gain, ln2_bias])
+        affine = (ln1_gain, ln1_bias, ln2_gain, ln2_bias)
         dfull, ctx_t, wide_t, row_max, row_inv, h1_local, h2_local = fwd_call(d_out, q_t, k_t, v_t, x_in, x_mid, affine)
-        dx1, grad_pre, grad_bfc1, vec, h1_full = mlp_call(dfull, d_out, x_mid, affine, h1_local, z_saved, w_fc2, w_fc1)
+        dx1, grad_pre, grad_bfc1, vec, h1_full = mlp_call(dfull, d_out, x_mid, ln2_gain, h1_local, z_saved, w_fc2, w_fc1)
         mfull, do_t, grad_wfc2 = ctx_call(dx1, w_proj.reshape(heads * dim, model), z_saved, dfull)
         h1_full, _, qkv_t, grad_wfc1 = bwd_call(
             h2_local, q_t, k_t, v_t, do_t.reshape(heads, dim, seq), wide_t, row_max, row_inv, grad_pre, h1_full)
         qkv_rows = qkv_t.reshape(3 * heads * dim, seq)
         w_rows = w_qkv.transpose(0, 2, 3, 1).reshape(3 * heads * dim, model)
         grad_x, grad_vecs, bias_rows, grad_wproj, grad_wqkv, _ = qkv_call(
-            qkv_rows, w_rows, dx1, x_in, affine, vec, ctx_t.reshape(heads * dim, seq), mfull, h1_full)
+            qkv_rows, w_rows, dx1, x_in, ln1_gain, vec, ctx_t.reshape(heads * dim, seq), mfull, h1_full)
+        grad_wfc2, grad_wfc1, grad_wqkv, grad_wproj, grad_x, grad_vecs, grad_bfc1 = finish_call(
+            grad_wfc2, grad_wfc1, grad_wqkv, grad_wproj, grad_x, grad_vecs, grad_bfc1)
         grad_wproj = grad_wproj.reshape(heads, dim, model)
         grad_wqkv = grad_wqkv.reshape(3, heads, dim, model).transpose(0, 3, 1, 2)
         grad_bqkv = bias_rows[0].reshape(3, heads, dim)

time: 380 us -> 353 us (0.929)
  local copies, waits for them, and re-layouts: 38.9 us -> 1.45 us
  Pallas kernels: 339 us -> 349 us
    unnamed x12 -> x0, local copies, waits for them, and re-layouts: 34.6 us -> none
    pallas_call x0 -> x1, Pallas kernels: none -> 28 us  [finish_call(): pl.pallas_call(finish_kernel, name='finish', in_specs=[HBM] * len(arrays)...]
    pallas_call x5, Pallas kernels: 339 us -> 321 us  [comm_call(): pl.pallas_call(kernel, in_specs=in_specs, out_specs=out_specs, out_shape=...]
where the time goes in v5:
time: 353 us; the launch traced here: 352 us
  Pallas kernels  349 us (99%)
    pallas_call x5, Pallas kernels, comm_call(): pl.pallas_call(kernel, in_specs=in_specs, out_specs=out_specs, out_shape=...  321 us
    pallas_call x1, Pallas kernels, finish_call(): pl.pallas_call(finish_kernel, name='finish', in_specs=[HBM] * len(arrays)...  28 us

profile of v5, /device:TPU:0, one launch (start us, length us, event | category | flops | bytes accessed | tf_op | source)
XLA Modules:
  0.0 352.4 jit_solution(17215279734271448823)
XLA Ops:
  0.6 54.4 %attn_fwd.1 = (bf16[8,256,2560]{2,1,0:T(8,128)(2,1)}, bf16[4,80,2048]{2,1,0:T(8,128)(2,1)}, f32[4,80,2048]{2,1,0:T(8,128)}, f32[4,1,2048]{2,1,0:T(1,128)}, f32[4...) custom-call(bf16[256,2560]{1,0:T(8,128)(2,1)} %bitcast.31, bf16[4,80,2048]{2,1,0:T(8,128)(2,1)} %bitcast.35, ...), custom_call_target="tpu_custom_call" | custom-call | flops 40000000000 | bytes 40000000 | tf_op jit(solution)/shard_map/attn_fwd/pallas_call | solution.py:301
  55.0 73.7 %mlp_grads.1 = (bf16[256,2560]{1,0:T(8,128)(2,1)}, bf16[2048,1280]{1,0:T(8,128)(2,1)}, f32[1,1280]{1,0:T(1,128)}, f32[8,2560]{1,0:T(8,128)}, bf16[8,256,2560]{2,1,0:T(8,128)(2,1)}) custom-call(bf16[8,256,2560]{2,1,0:T(8,128)(2,1)} %get-tuple-element.38.dfull, bf16[256,2560]{1,0:T(8,128)(2,1)} %bitcast.32, bf16[256,2560]{1,0:T(8,128)(2,1)} %bitcast.34, ...), custom_call_target="tpu_custom_call" | custom-call | flops 60000002048 | bytes 40000000 | tf_op jit(solution)/shard_map/mlp_grads/pallas_call | solution.py:301
  128.8 51.7 %ctx_grads.1 = (bf16[8,256,2560]{2,1,0:T(8,128)(2,1)}, bf16[320,2048]{1,0:T(8,128)(2,1)}, f32[1280,2560]{1,0:T(8,128)}) custom-call(bf16[256,2560]{1,0:T(8,128)(2,1)} %get-tuple-element.40.dx1_ref.dx1_hbm, bf16[320,2560]{1,0:T(8,128)(2,1)} %bitcast.30, bf16[2048,1280]{1,0:T(8,128)(2,1)} %bitcast.27, bf16[8,256,2560]{2,1,0:T(8,128)(2,1)} %get-tuple-element.38.dfull), custom_call_target="tpu_custom_call" | custom-call | flops 30000001024 | bytes 40000000 | tf_op jit(solution)/shard_map/ctx_grads/pallas_call | solution.py:301
  180.6 71.9 %attn_bwd.1 = (bf16[8,256,2560]{2,1,0:T(8,128)(2,1)}, bf16[8,256,2560]{2,1,0:T(8,128)(2,1)}, bf16[3,4,80,2048]{3,2,1,0:T(8,128)(2,1)}, f32[2560,1280]{1,0:T(8,128)}) custom-call(bf16[256,2560]{1,0:T(8,128)(2,1)} %get-tuple-element.42.h2_ref, bf16[4,80,2048]{2,1,0:T(8,128)(2,1)} %bitcast.36, ...), custom_call_target="tpu_custom_call", output_to_operand_aliasing={{0}: (9, {})} | custom-call | flops 80000000000 | bytes 40000000 | tf_op jit(solution)/shard_map/attn_bwd/pallas_call | solution.py:301
  252.4 69.2 %qkv_grads.1 = (bf16[256,2560]{1,0:T(8,128)(2,1)}, f32[6,2560]{1,0:T(8,128)}, f32[8,960]{1,0:T(8,128)}, f32[320,2560]{1,0:T(8,128)}, f32[960,2560]{1,0:T(8,128)}, /*index=5*/bf16[8,256,2560]{2,1,0:T(8,128)(2,1)}) custom-call(bf16[960,2048]{1,0:T(8,128)(2,1)} %bitcast.44, bf16[960,2560]{1,0:T(8,128)(2,1)} %bitcast.28, ...), custom_call_target="tpu_custom_call", output_to_operand_aliasing={{5}: (8, {})} | custom-call | flops 30000001024 | bytes 40000000 | tf_op jit(solution)/shard_map/qkv_grads/pallas_call | solution.py:301
  321.6 28.0 %finish.1 = (f32[1280,2560]{1,0:T(8,128)}, f32[2560,1280]{1,0:T(8,128)}, f32[960,2560]{1,0:T(8,128)}, f32[320,2560]{1,0:T(8,128)}, bf16[256,2560]{1,0:T(8,128)(2...) custom-call(f32[1280,2560]{1,0:T(8,128)} %get-tuple-element.41.refs_0_, f32[2560,1280]{1,0:T(8,128)} %get-tuple-element.49.refs_1_, ...), custom_call_target="tpu_custom_call" | custom-call | flops 1000000 | bytes 72000000 | tf_op jit(solution)/shard_map/finish/pallas_call | solution.py:940
  349.7 0.8 slice_reduce_fusion
  350.5 0.7 reshape_squeeze.3
  351.1 1.3 reduce.1

commit v6 on v5

--- a/solution.py
+++ b/solution.py
@@ -12,12 +12,14 @@
 BLK = 512
 F32 = jnp.float32
 BF16 = jnp.bfloat16
+COLS = dict(axis=0, keepdims=True)
+ROWS = dict(axis=-1, keepdims=True)
 
 
 def layer_norm_bwd(grad_norm, x_hat, inv_std, norm_gain):
     grad_hat = grad_norm * norm_gain
-    centered_grad = grad_hat - jnp.mean(grad_hat, axis=-1, keepdims=True)
-    return inv_std * (centered_grad - x_hat * jnp.mean(grad_hat * x_hat, axis=-1, keepdims=True))
+    centered_grad = grad_hat - jnp.mean(grad_hat, **ROWS)
+    return inv_std * (centered_grad - x_hat * jnp.mean(grad_hat * x_hat, **ROWS))
 
 
 def dot(a, b):
@@ -122,8 +124,6 @@
 
 
 class ThirdGather:
-    COPIES = 5
-
     def __init__(self, place, full, send_sem, recv_sem):
         self.place, self.full = place, full
         self.links = Links(place, send_sem, recv_sem)
@@ -131,32 +131,30 @@
         self.first, self.second = pl.ds(0, half), pl.ds(half, half)
 
     def start(self, third, own):
-        me, full = self.place.me, self.full
-        near = {'X': self.first, 'Y': self.second} if third == 0 else {'X': self.second, 'Y': self.first}
-        if third == 2:
-            block = self.place.block
-            near = {'Y': (block['X'], self.first), 'X': (block['Y'], self.second)}
+        me, full, block = self.place.me, self.full, self.place.block
+        near = {'near': {'X': self.first, 'Y': self.second}, 'rest': {'X': self.second, 'Y': self.first}}.get(third)
         for key in 'XY':
-            if third == 2:
-                self.links.send('N' + key, key, full, full, *near[key])
+            if near is None:
+                slot, half = (block['Y'], self.second) if key == 'X' else (block['X'], self.first)
+                self.links.send(third + key, key, full, full, slot, half)
             else:
                 src = (full, (me, near[key])) if own is None else (own, (near[key],))
-                self.links.send('N' + key, key, src, (full, (me, near[key])))
-        if third == 0:
+                self.links.send(third + key, key, src, (full, (me, near[key])))
+        if third == 'near':
             self.links.send('CO', 'C', (own, ()), (full, (me,)))
 
     def forward(self, third):
         block = self.place.block
         for key in 'XY':
-            self.links.wait('N' + key)
-            half = self.first if (third == 0) == (key == 'X') else self.second
+            self.links.wait(third + key)
+            half = self.first if (third == 'near') == (key == 'X') else self.second
             slot = block[key]
-            if third == 2:
+            if third == 'diag':
                 slot, half = block['D'], (self.second if key == 'X' else self.first)
-            self.links.send('C' + key, 'C', self.full, self.full, slot, half)
+            self.links.send('C' + third + key, 'C', self.full, self.full, slot, half)
 
     def wait_pair(self, third):
-        self.links.wait('CX', 'CY', *(('CO',) if third == 0 else ()))
+        self.links.wait('C' + third + 'X', 'C' + third + 'Y', *(('CO',) if third == 'near' else ()))
 
 
 class Scatter:
@@ -265,8 +263,8 @@
 
 
 def layer_norm_hat(rows_f32):
-    centered = rows_f32 - jnp.mean(rows_f32, axis=-1, keepdims=True)
-    inv_std = lax.rsqrt(jnp.mean(centered * centered, axis=-1, keepdims=True) + LN_EPS)
+    centered = rows_f32 - jnp.mean(rows_f32, **ROWS)
+    inv_std = lax.rsqrt(jnp.mean(centered * centered, **ROWS) + LN_EPS)
     return centered * inv_std, inv_std
 
 
@@ -275,6 +273,8 @@
 VMEM = pl.BlockSpec(memory_space=pltpu.VMEM)
 HBM = pl.BlockSpec(memory_space=pl.ANY)
 DMA = pltpu.SemaphoreType.DMA
+COMM = DMA((12,))
+PAIR = DMA((2,))
 shape = jax.ShapeDtypeStruct
 
 
@@ -302,7 +302,7 @@
         kernel, in_specs=in_specs, out_specs=out_specs, out_shape=out_shape, scratch_shapes=scratch, name=name,
         input_output_aliases=aliases,
         compiler_params=pltpu.CompilerParams(collective_id=ident, has_side_effects=True, vmem_limit_bytes=66_000_000),
-        cost_estimate=pl.CostEstimate(flops=flops, bytes_accessed=40_000_000, transcendentals=3_000_000),
+        cost_estimate=pl.CostEstimate(flops=flops, bytes_accessed=flops // 1000, transcendentals=flops // 1000),
     )(*args)
 
 
@@ -373,17 +373,17 @@
                 at = tile_at(ki, BLK)
                 blk = dot(k_rows[at, :], q_blk)
                 strip[at, :] = blk
-                return jnp.maximum(run_max, jnp.max(blk, axis=0, keepdims=True))
+                return jnp.maximum(run_max, jnp.max(blk, **COLS))
 
             diag = causal_fill(dot(k_rows[q_at, :], q_blk), -1e30)
             strip[q_at, :] = diag
-            row_max = lax.fori_loop(0, qi, score_step, jnp.max(diag, axis=0, keepdims=True))
+            row_max = lax.fori_loop(0, qi, score_step, jnp.max(diag, **COLS))
 
             def exp_step(ki, run_sum):
                 at = tile_at(ki, BLK)
                 probs = jnp.exp2((strip[at, :] - row_max) * exp_scale)
                 strip[at, :] = probs
-                return run_sum + jnp.sum(probs, axis=0, keepdims=True)
+                return run_sum + jnp.sum(probs, **COLS)
 
             row_inv = 1.0 / lax.fori_loop(0, qi + 1, exp_step, jnp.zeros_like(row_max))
 
@@ -434,15 +434,15 @@
          shape((heads, 1, seq), F32), shape((heads, 1, seq), F32), shape((rows, model), BF16), shape((rows, model), BF16)],
         [HBM] + [VMEM] * 6,
         [pltpu.VMEM((seq, dim), BF16), pltpu.VMEM((seq, BLK), F32)] + [pltpu.VMEM(q_t.shape, BF16)] * 3
-        + [pltpu.VMEM((rows, model), BF16)] * 2 + [DMA(()), DMA((5,))] + [DMA((10,))] * 2)
+        + [pltpu.VMEM((rows, model), BF16)] * 2 + [DMA(()), DMA((5,))] + [COMM] * 2)
 
 
 def dot_t(a, b):
     return lax.dot_general(a, b, (((1,), (1,)), ((), ())), preferred_element_type=F32)
 
 
-def mlp_kernel(dfull, dout_hbm, mid_hbm, gain_ref, h1_ref, z_ref, w2_ref, w1_ref,
-               dx1_ref, dz_ref, gb1_ref, vec_ref, h1full,
+def mlp_kernel(dfull, dout_hbm, mid_hbm, gain_ref, h2_ref, z_ref, w2_ref, w1_ref,
+               dx1_ref, dz_ref, gb1_ref, vec_ref, h2full,
                w2v, w1v, dzv, ybuf, part, crecv, diag_recv, last_recv, dout_ref, mid_ref,
                load_sem, y_sem, z_sem, dz_sem, own_sem, *comm_sems):
     place = Place()
@@ -450,9 +450,9 @@
     rows, model = dout_hbm.shape
     hidden = w2v.shape[0]
     scatter = Scatter(place, part, crecv, diag_recv, last_recv, *comm_sems[0:2])
-    gather = ThirdGather(place, h1full, *comm_sems[2:4])
-    gather.start(0, h1_ref)
-    own_copy = pltpu.make_async_copy(h1_ref, h1full.at[place.me], own_sem)
+    gather = ThirdGather(place, h2full, *comm_sems[2:4])
+    gather.start('near', h2_ref)
+    own_copy = pltpu.make_async_copy(h2_ref, h2full.at[place.me], own_sem)
 
     def load_pair(i):
         return pltpu.make_async_copy(dfull.at[pl.ds(2 * place.pair_at(i), 2)], ybuf.at[i % 2], y_sem.at[i])
@@ -488,7 +488,7 @@
             acc = dot_t(ybuf[slot].reshape(2 * rows, model), w2v[cols, :])
             grad = (acc * gelu_slope(dzv[at, cols].astype(F32))).astype(BF16)
             dzv[at, cols] = grad
-            gb1_ref[:, cols] += jnp.sum(grad.astype(F32), axis=0, keepdims=True)
+            gb1_ref[:, cols] += jnp.sum(grad.astype(F32), **COLS)
 
         loop(hidden // TILE, grad_act)
         store_grad(i).start()
@@ -503,7 +503,7 @@
 
         @pl.when(i == 2)
         def _():
-            gather.forward(0)
+            gather.forward('near')
 
         scatter.between(i)
 
@@ -530,13 +530,13 @@
         mid = (dout_rows + layer_norm_bwd(grad, x_hat, inv_std, gain)).astype(BF16)
         dx1_ref[at, :] = mid
         for row, val in enumerate((grad * x_hat, grad, mid.astype(F32), dout_rows)):
-            vec_ref[row + 2:row + 3, :] += jnp.sum(val, axis=0, keepdims=True)
+            vec_ref[row + 2:row + 3, :] += jnp.sum(val, **COLS)
 
     scatter.norm_loop(norm_rows)
     for i in range(4):
         store_grad(i).wait()
     own_copy.wait()
-    gather.wait_pair(0)
+    gather.wait_pair('near')
     gather.links.finish()
     scatter.links.finish()
 
@@ -558,7 +558,7 @@
         [pltpu.VMEM((hidden, model), BF16), pltpu.VMEM((model, hidden), BF16),
          pltpu.VMEM((seq, hidden), BF16), pltpu.VMEM((2, 2, rows, model), BF16)]
         + scatter_scratch(rows, model) + [pltpu.VMEM((rows, model), BF16)] * 2
-        + [DMA((4,))] * 4 + [DMA(())] + [DMA((12,))] * 2 + [DMA((5,))] * 2)
+        + [DMA((4,))] * 4 + [DMA(())] + [COMM] * 4)
 
 
 def gelu(pre_act):
@@ -633,20 +633,23 @@
         [shape((seq // rows, rows, model), BF16), shape((feats, seq), BF16), shape((hidden, model), F32)], [HBM, VMEM, HBM],
         [pltpu.VMEM((2, rows, model), BF16), pltpu.VMEM((seq, hidden), BF16), pltpu.VMEM((hidden, seq), BF16),
          pltpu.VMEM((seq // rows, rows, model), BF16), pltpu.VMEM((2, hidden, OUT_TILE), F32),
-         DMA(()), DMA(()), DMA((2,)), DMA((2,))] + [DMA((10,))] * 2)
-
-
-def bwd_kernel(h2_ref, q_hbm, k_hbm, v_hbm, do_hbm, wide_hbm, max_ref, inv_ref, dz_ref, h1_in,
-               h1full, h2full, out_ref, dw1_ref,
+         DMA(()), DMA(()), PAIR, PAIR] + [COMM] * 2)
+
+
+def bwd_kernel(h1_ref, q_hbm, k_hbm, v_hbm, do_hbm, wide_hbm, max_ref, inv_ref, dz_ref, h2_in,
+               h2full, h1full, out_ref, dw1_ref,
                k_rows, v_rows, q_rows, do_rows, delta, dq_acc, dk_acc, dv_acc, tok, dzv, wbuf,
                q_ref, k_ref, v_ref, do_ref, wide_ref, own_sem, head_sem, load_sem, out_sem, *comm_sems):
     place = Place()
     place.barrier()
     gather1 = ThirdGather(place, h1full, *comm_sems[0:2])
-    gather2 = Gather(place, h2_ref, h2full, *comm_sems[2:4])
-    gather2.start()
+    gather2 = ThirdGather(place, h2full, *comm_sems[2:4])
+    gather2.start('rest', None)
+    gather2.start('diag', None)
+    gather1.start('near', h1_ref)
+    gather1.start('rest', h1_ref)
     loads = start_copies(head_sem, (k_hbm, k_ref), (v_hbm, v_ref), (q_hbm, q_ref), (do_hbm, do_ref), (wide_hbm, wide_ref))
-    own_copy = pltpu.make_async_copy(h2_ref, h2full.at[place.me], own_sem)
+    own_copy = pltpu.make_async_copy(h1_ref, h1full.at[place.me], own_sem)
     own_copy.start()
     heads, dim, seq = q_ref.shape
     blocks = seq // BLK
@@ -658,7 +661,7 @@
         v_rows[...] = v_ref[h].T
         q_rows[...] = q_ref[h].T
         do_rows[...] = do_ref[h].T
-        delta[...] = jnp.sum(do_ref[h].astype(F32) * wide_ref[h], axis=0, keepdims=True)
+        delta[...] = jnp.sum(do_ref[h].astype(F32) * wide_ref[h], **COLS)
         dq_acc[...] = jnp.zeros_like(dq_acc)
         dk_acc[...] = jnp.zeros_like(dk_acc)
         dv_acc[...] = jnp.zeros_like(dv_acc)
@@ -681,12 +684,8 @@
         out_ref[1, h] = dk_acc[...].astype(BF16).T
         out_ref[2, h] = dv_acc[...].astype(BF16).T
 
-    load_grad = pltpu.make_async_copy(dz_ref, dzv, load_sem.at[4])
-
-    def load_tok(i):
-        at = pl.ds(2 * place.pair_at(i), 2)
-        return pltpu.make_async_copy(h2full.at[at], tok.at[at], load_sem.at[i])
-
+    load_grad, load_tok = [pltpu.make_async_copy(src, dst, load_sem.at[i])
+                           for i, (src, dst) in enumerate(((dz_ref, dzv), (h2full, tok)))]
     for copy in loads:
         copy.wait()
     count = tok.shape[2] // OUT_TILE
@@ -701,51 +700,46 @@
 
         @pl.when(h == 1)
         def _():
-            gather2.relay()
-            gather1.start(1, None)
-
-        @pl.when(h == 2)
-        def _():
             load_grad.start()
-            gather2.forward('X')
-            gather2.forward('Y')
-            own_copy.wait()
-            gather2.links.wait('CO')
-            load_tok(3).start()
-
-    loop(heads, head_step)
-    gather2.forward('D')
-    gather2.links.wait('CX', 'CY')
-    load_tok(1).start()
-    load_tok(2).start()
+            gather2.forward('rest')
+
+        @pl.when(h == heads - 2)
+        def _():
+            gather2.forward('diag')
+            gather2.wait_pair('rest')
+
+    loop(heads - 1, head_step)
+    gather2.wait_pair('diag')
+    load_tok.start()
+    head(heads - 1)
     load_grad.wait()
-    gather2.links.wait('CD')
-    load_tok(0).start()
-    for i in range(4):
-        load_tok(i).wait()
+    load_tok.wait()
     loop(count, fc1_tile)
-    gather1.forward(1)
-    gather1.wait_pair(1)
+    for third in ('near', 'rest'):
+        gather1.forward(third)
+    for third in ('near', 'rest'):
+        gather1.wait_pair(third)
+    own_copy.wait()
     tiles.finish(count)
     gather1.links.finish()
     gather2.links.finish()
 
 
-def bwd_call(h2, q_t, k_t, v_t, do_t, wide, row_max, row_inv, dz, h1full):
+def bwd_call(h1, q_t, k_t, v_t, do_t, wide, row_max, row_inv, dz, h2full):
     heads, dim, seq = q_t.shape
-    rows, model = h2.shape
+    rows, model = h1.shape
     full = shape((seq // rows, rows, model), BF16)
     turned = pltpu.VMEM((seq, dim), BF16)
     hidden = dz.shape[1]
     return comm_call(
         bwd_kernel, "attn_bwd", 3, 80_000_000_000,
-        (h2, q_t, k_t, v_t, do_t, wide, row_max, row_inv, dz, h1full), [VMEM] + [HBM] * 5 + [VMEM] * 2 + [HBM] * 2,
+        (h1, q_t, k_t, v_t, do_t, wide, row_max, row_inv, dz, h2full), [VMEM] + [HBM] * 5 + [VMEM] * 2 + [HBM] * 2,
         [full, full, shape((3, heads, dim, seq), BF16), shape((model, hidden), F32)], [HBM, HBM, VMEM, HBM],
         [turned] * 4 + [pltpu.VMEM((1, seq), F32), pltpu.VMEM((dim, seq), F32), pltpu.VMEM((seq, dim), F32),
                         pltpu.VMEM((seq, dim), F32), pltpu.VMEM((seq // rows, rows, model), BF16),
                         pltpu.VMEM((seq, hidden), BF16), pltpu.VMEM((2, OUT_TILE, hidden), F32),
                         *[pltpu.VMEM(q_t.shape, BF16)] * 4, pltpu.VMEM(wide.shape, F32),
-                        DMA(()), DMA((5,)), DMA((5,)), DMA((2,))] + [DMA((5,))] * 2 + [DMA((10,))] * 2,
+                        DMA(()), DMA((5,)), PAIR, PAIR] + [COMM] * 4,
         aliases={9: 0})
 
 
@@ -758,7 +752,7 @@
     rows, model = dx1_ref.shape
     scatter = Scatter(place, part, crecv, diag_recv, last_recv, *comm_sems[0:2])
     gather = ThirdGather(place, h1full, *comm_sems[2:4])
-    gather.start(2, None)
+    gather.start('diag', None)
     inputs = start_copies(in_sem, (qkv_hbm, qkv_ref), (w_hbm, w_ref), (ctx_hbm, ctx_ref), (dx1_hbm, dx1_ref), (x_hbm, x_ref))
     loads = [pltpu.make_async_copy(src, tok, load_sem.at[i]) for i, src in enumerate((mfull, h1full))]
     tiles_o = Tiles(obuf, dwo_ref, out_sem.at[0])
@@ -795,7 +789,7 @@
 
         @pl.when(i == 3)
         def _():
-            gather.forward(2)
+            gather.forward('diag')
 
         for at in range(1, 3):
             @pl.when(i == at)
@@ -829,7 +823,7 @@
 
     loop(count, proj_tile)
     scatter.add_diag()
-    gather.wait_pair(2)
+    gather.wait_pair('diag')
     loads[1].start()
     ones = jnp.ones((8, qkv_ref.shape[1]), BF16)
     bias_ref[...] = dot_t(ones, qkv_ref[...])
@@ -843,8 +837,8 @@
         grad = scatter.total(at)
         x_hat, inv_std = layer_norm_hat(x_ref[at, :].astype(F32))
         dx_ref[at, :] = (dx1_ref[at, :].astype(F32) + layer_norm_bwd(grad, x_hat, inv_std, gain)).astype(BF16)
-        vacc[0:1, :] += jnp.sum(grad * x_hat, axis=0, keepdims=True)
-        vacc[1:2, :] += jnp.sum(grad, axis=0, keepdims=True)
+        vacc[0:1, :] += jnp.sum(grad * x_hat, **COLS)
+        vacc[1:2, :] += jnp.sum(grad, **COLS)
 
     scatter.norm_loop(norm_rows)
     finals = Links(place, last_sem.at[0], last_sem.at[1])
@@ -878,7 +872,7 @@
            pltpu.VMEM((2, proj, OUT_TILE), F32), pltpu.VMEM((2, feats, OUT_TILE), F32),
            pltpu.VMEM((feats, seq), BF16), pltpu.VMEM((feats, model), BF16), pltpu.VMEM((rows, model), BF16),
            pltpu.VMEM((rows, model), BF16), pltpu.VMEM((proj, seq), BF16),
-           DMA((2, 3)), DMA((2, 7)), DMA((2,)), DMA((5,)), DMA((2, 2))] + [DMA((12,))] * 2 + [DMA((5,))] * 2,
+           DMA((2, 3)), DMA((2, 7)), PAIR, DMA((5,)), DMA((2, 2))] + [COMM] * 4,
         aliases={8: 5})
 
 
@@ -955,10 +949,10 @@
         q_t, k_t, v_t = (v[0].transpose(1, 2, 0) for v in (q_saved, k_saved, v_saved))
         affine = (ln1_gain, ln1_bias, ln2_gain, ln2_bias)
         dfull, ctx_t, wide_t, row_max, row_inv, h1_local, h2_local = fwd_call(d_out, q_t, k_t, v_t, x_in, x_mid, affine)
-        dx1, grad_pre, grad_bfc1, vec, h1_full = mlp_call(dfull, d_out, x_mid, ln2_gain, h1_local, z_saved, w_fc2, w_fc1)
+        dx1, grad_pre, grad_bfc1, vec, h2_full = mlp_call(dfull, d_out, x_mid, ln2_gain, h2_local, z_saved, w_fc2, w_fc1)
         mfull, do_t, grad_wfc2 = ctx_call(dx1, w_proj.reshape(heads * dim, model), z_saved, dfull)
-        h1_full, _, qkv_t, grad_wfc1 = bwd_call(
-            h2_local, q_t, k_t, v_t, do_t.reshape(heads, dim, seq), wide_t, row_max, row_inv, grad_pre, h1_full)
+        _, h1_full, qkv_t, grad_wfc1 = bwd_call(
+            h1_local, q_t, k_t, v_t, do_t.reshape(heads, dim, seq), wide_t, row_max, row_inv, grad_pre, h2_full)
         qkv_rows = qkv_t.reshape(3 * heads * dim, seq)
         w_rows = w_qkv.transpose(0, 2, 3, 1).reshape(3 * heads * dim, model)
         grad_x, grad_vecs, bias_rows, grad_wproj, grad_wqkv, _ = qkv_call(

time: 353 us -> 350 us (level)
  no operation moved by 1% of the time
where the time goes in v6:
time: 350 us; the launch traced here: 349 us
  Pallas kernels  346 us (99%)
    pallas_call x5, Pallas kernels, comm_call(): pl.pallas_call(kernel, in_specs=in_specs, out_specs=out_specs, out_shape=...  318 us
    pallas_call x1, Pallas kernels, finish_call(): pl.pallas_call(finish_kernel, name='finish', in_specs=[HBM] * len(arrays)...  28 us

profile of v6, /device:TPU:0, one launch (start us, length us, event | category | flops | bytes accessed | tf_op | source)
XLA Modules:
  0.0 349.2 jit_solution(11604362974255279396)
XLA Ops:
  0.6 54.5 %attn_fwd.1 = (bf16[8,256,2560]{2,1,0:T(8,128)(2,1)}, bf16[4,80,2048]{2,1,0:T(8,128)(2,1)}, f32[4,80,2048]{2,1,0:T(8,128)}, f32[4,1,2048]{2,1,0:T(1,128)}, f32[4...) custom-call(bf16[256,2560]{1,0:T(8,128)(2,1)} %bitcast.31, bf16[4,80,2048]{2,1,0:T(8,128)(2,1)} %bitcast.35, ...), custom_call_target="tpu_custom_call" | custom-call | flops 40000000000 | bytes 40000000 | tf_op jit(solution)/shard_map/attn_fwd/pallas_call | solution.py:301
  55.1 73.9 %mlp_grads.1 = (bf16[256,2560]{1,0:T(8,128)(2,1)}, bf16[2048,1280]{1,0:T(8,128)(2,1)}, f32[1,1280]{1,0:T(1,128)}, f32[8,2560]{1,0:T(8,128)}, bf16[8,256,2560]{2,1,0:T(8,128)(2,1)}) custom-call(bf16[8,256,2560]{2,1,0:T(8,128)(2,1)} %get-tuple-element.38.dfull, bf16[256,2560]{1,0:T(8,128)(2,1)} %bitcast.32, bf16[256,2560]{1,0:T(8,128)(2,1)} %bitcast.34, ...), custom_call_target="tpu_custom_call" | custom-call | flops 60000002048 | bytes 60000000 | tf_op jit(solution)/shard_map/mlp_grads/pallas_call | solution.py:301
  129.0 52.0 %ctx_grads.1 = (bf16[8,256,2560]{2,1,0:T(8,128)(2,1)}, bf16[320,2048]{1,0:T(8,128)(2,1)}, f32[1280,2560]{1,0:T(8,128)}) custom-call(bf16[256,2560]{1,0:T(8,128)(2,1)} %get-tuple-element.40.dx1_ref.dx1_hbm, bf16[320,2560]{1,0:T(8,128)(2,1)} %bitcast.30, bf16[2048,1280]{1,0:T(8,128)(2,1)} %bitcast.27, bf16[8,256,2560]{2,1,0:T(8,128)(2,1)} %get-tuple-element.38.dfull), custom_call_target="tpu_custom_call" | custom-call | flops 30000001024 | bytes 30000000 | tf_op jit(solution)/shard_map/ctx_grads/pallas_call | solution.py:301
  181.0 68.0 %attn_bwd.1 = (bf16[8,256,2560]{2,1,0:T(8,128)(2,1)}, bf16[8,256,2560]{2,1,0:T(8,128)(2,1)}, bf16[3,4,80,2048]{3,2,1,0:T(8,128)(2,1)}, f32[2560,1280]{1,0:T(8,128)}) custom-call(bf16[256,2560]{1,0:T(8,128)(2,1)} %get-tuple-element.42.h1_ref, bf16[4,80,2048]{2,1,0:T(8,128)(2,1)} %bitcast.36, ...), custom_call_target="tpu_custom_call", output_to_operand_aliasing={{0}: (9, {})} | custom-call | flops 80000000000 | bytes 80000000 | tf_op jit(solution)/shard_map/attn_bwd/pallas_call | solution.py:301
  249.0 69.3 %qkv_grads.1 = (bf16[256,2560]{1,0:T(8,128)(2,1)}, f32[6,2560]{1,0:T(8,128)}, f32[8,960]{1,0:T(8,128)}, f32[320,2560]{1,0:T(8,128)}, f32[960,2560]{1,0:T(8,128)}, /*index=5*/bf16[8,256,2560]{2,1,0:T(8,128)(2,1)}) custom-call(bf16[960,2048]{1,0:T(8,128)(2,1)} %bitcast.44, bf16[960,2560]{1,0:T(8,128)(2,1)} %bitcast.28, ...), custom_call_target="tpu_custom_call", output_to_operand_aliasing={{5}: (8, {})} | custom-call | flops 30000001024 | bytes 30000000 | tf_op jit(solution)/shard_map/qkv_grads/pallas_call | solution.py:301
  318.4 28.0 %finish.1 = (f32[1280,2560]{1,0:T(8,128)}, f32[2560,1280]{1,0:T(8,128)}, f32[960,2560]{1,0:T(8,128)}, f32[320,2560]{1,0:T(8,128)}, bf16[256,2560]{1,0:T(8,128)(2...) custom-call(f32[1280,2560]{1,0:T(8,128)} %get-tuple-element.41.refs_0_, f32[2560,1280]{1,0:T(8,128)} %get-tuple-element.49.refs_1_, ...), custom_call_target="tpu_custom_call" | custom-call | flops 1000000 | bytes 72000000 | tf_op jit(solution)/shard_map/finish/pallas_call | solution.py:934
  346.4 0.8 slice_reduce_fusion
  347.2 0.7 reshape_squeeze.3
  347.9 1.3 reduce.1

commit v7 on v6

--- a/solution.py
+++ b/solution.py
@@ -12,6 +12,7 @@
 BLK = 512
 F32 = jnp.float32
 BF16 = jnp.bfloat16
+DIM0, DIM1, DIM2 = range(3)
 COLS = dict(axis=0, keepdims=True)
 ROWS = dict(axis=-1, keepdims=True)
 
@@ -43,12 +44,19 @@
         self.peer = {'X': self.me + self.dx, 'Y': self.me + self.dy, 'C': self.me + self.dc}
         self.peer.update({k: (self.me + k) % 8 for k in range(1, 8)})
         self.block = {'O': self.me, 'X': self.me + self.dx, 'Y': self.me + self.dy, 'D': self.me + self.dx + self.dy}
+        self.pair = {key: val // 2 for key, val in self.block.items()}
         self.other = {key: val + self.dc for key, val in self.block.items()}
         self.x, self.y = (self.me // 2) % 2, self.me // 4
 
     def pair_at(self, i):
         flip_x, flip_y = 1 - i // 2, 1 - i % 2
         return 2 * (self.y + flip_y * (1 - 2 * self.y)) + self.x + flip_x * (1 - 2 * self.x)
+
+    def chunk(self, i, c):
+        mixed = i * (3 - i) // 2
+        pair, half = (self.pair['X'], i - 1) if c < 2 else (self.pair['Y'], 2 - i)
+        slot = (1 - mixed) * (2 * self.pair_at(i) + c // 2) + mixed * (2 * pair + c % 2)
+        return slot, (1 - mixed) * (c % 2) + mixed * half
 
     def barrier(self, everyone=False):
         sem = pltpu.get_barrier_semaphore()
@@ -99,7 +107,7 @@
     def __init__(self, place, own, full, send_sem, recv_sem):
         self.place, self.own, self.full = place, own, full
         self.links = Links(place, send_sem, recv_sem)
-        half = own.shape[0] // 2
+        half = own.shape[DIM0] // 2
         self.first, self.second = pl.ds(0, half), pl.ds(half, half)
 
     def start(self):
@@ -127,7 +135,7 @@
     def __init__(self, place, full, send_sem, recv_sem):
         self.place, self.full = place, full
         self.links = Links(place, send_sem, recv_sem)
-        half = full.shape[1] // 2
+        half = full.shape[DIM1] // 2
         self.first, self.second = pl.ds(0, half), pl.ds(half, half)
 
     def start(self, third, own):
@@ -157,6 +165,9 @@
         self.links.wait('C' + third + 'X', 'C' + third + 'Y', *(('CO',) if third == 'near' else ()))
 
 
+CRECV = dict(O=0, Xa=1, Xb=1, Ya=2, Yb=2, D=3)
+
+
 class Scatter:
     COPIES = 10
 
@@ -164,10 +175,11 @@
         self.place, self.part, self.crecv = place, part, crecv
         self.diag_recv, self.last_recv = diag_recv, last_recv
         self.links = Links(place, send_sem, recv_sem)
-        half = part.shape[1] // 2
+        half = part.shape[DIM1] // 2
         self.half = {'a': pl.ds(0, half), 'b': pl.ds(half, half)}
-        for at, key in enumerate('OXYD'):
-            self.links.define('C' + key, 'C', (part, (place.other[key],)), (crecv, (at,)))
+        for name, at in CRECV.items():
+            index = (at,) if len(name) == 1 else (at, self.half[name[1]])
+            self.links.define('C' + name, 'C', (part, (place.other[name[0]],) + index[1:]), (crecv, index))
 
     def add_rows(self, slot, start, count, other, other_start):
         step = 64
@@ -181,13 +193,21 @@
 
         lax.fori_loop(0, count // step, body, 0)
 
-    def swap(self, key):
-        self.links.start('C' + key)
-
-    def add_pair(self, key):
-        self.links.wait('C' + key)
-        at = 'OXYD'.index(key)
-        self.add_rows(self.place.block[key], 0, self.part.shape[1], self.crecv.at[at], 0)
+    def store(self, i, cols, rows):
+        for c in range(4):
+            slot, half = self.place.chunk(i, c)
+            size = rows.shape[DIM0] // 4
+            self.part[slot, tile_at(half, size), cols] = rows[c * size:(c + 1) * size]
+
+    def swap(self, *names):
+        for name in names:
+            self.links.start('C' + name)
+
+    def add_pair(self, name):
+        self.links.wait('C' + name)
+        rows = self.part.shape[DIM1]
+        start, count = (0, rows) if len(name) == 1 else ((rows // 2) * 'ab'.index(name[1]), rows // 2)
+        self.add_rows(self.place.block[name[0]], start, count, self.crecv.at[CRECV[name]], start)
 
     def send_half(self, key, half):
         at = self.half[half]
@@ -198,7 +218,9 @@
             self.links.send('D' + half, key, (self.part, (self.place.block['D'], self.half[half])), (self.diag_recv, (i,)))
 
     def add_diag(self):
-        rows = self.part.shape[1] // 4
+        self.add_pair('Xb')
+        self.add_pair('Ya')
+        rows = self.part.shape[DIM1] // 4
         for i, (half, key, start) in enumerate((('a', 'Y', 0), ('b', 'X', 2 * rows))):
             self.links.wait('D' + half)
             for quarter in range(2):
@@ -214,7 +236,7 @@
         self.links.wait('Ya' + str(quarter), 'Xb' + str(quarter))
 
     def norm_loop(self, body):
-        rows = self.part.shape[1]
+        rows = self.part.shape[DIM1]
         chunks = rows // LN_ROWS
         quarter = chunks // 4
 
@@ -237,19 +259,15 @@
 
         @pl.when(i == 2)
         def _():
-            self.add_pair('X')
-            self.send_half('X', 'a')
-
-        @pl.when(i == 3)
-        def _():
-            self.add_pair('Y')
-            self.send_half('Y', 'b')
+            for name in ('Xa', 'Yb'):
+                self.add_pair(name)
+                self.send_half(*name)
 
     def after(self, i):
-        for at, key in enumerate('DXYO'):
+        for at, names in enumerate((('D',), ('Xa', 'Yb'), ('Xb', 'Ya'), ('O',))):
             @pl.when(i == at)
             def _():
-                self.swap(key)
+                self.swap(*names)
 
     def total(self, at):
         me = self.place.me
@@ -273,7 +291,7 @@
 VMEM = pl.BlockSpec(memory_space=pltpu.VMEM)
 HBM = pl.BlockSpec(memory_space=pl.ANY)
 DMA = pltpu.SemaphoreType.DMA
-COMM = DMA((12,))
+COMM = DMA((14,))
 PAIR = DMA((2,))
 shape = jax.ShapeDtypeStruct
 
@@ -282,11 +300,19 @@
     return pl.ds(pl.multiple_of(i * size, size), size)
 
 
-def start_copies(sem, *pairs):
-    copies = [pltpu.make_async_copy(src, dst, sem.at[i]) for i, (src, dst) in enumerate(pairs)]
+def start_all(copies):
     for copy in copies:
         copy.start()
     return copies
+
+
+def wait_all(copies):
+    for copy in copies:
+        copy.wait()
+
+
+def start_copies(sem, *pairs):
+    return start_all([pltpu.make_async_copy(src, dst, sem.at[i]) for i, (src, dst) in enumerate(pairs)])
 
 
 def loop(count, body, start=0):
@@ -333,7 +359,7 @@
 
 
 def flat_cols(ref, cols):
-    return ref[:, :, cols].reshape(ref.shape[0] * ref.shape[1], OUT_TILE)
+    return ref[:, :, cols].reshape(ref.shape[DIM0] * ref.shape[DIM1], OUT_TILE)
 
 
 def fwd_kernel(dout_ref, q_hbm, k_hbm, v_hbm, x_hbm, mid_hbm, gain1_ref, bias1_ref, gain2_ref, bias2_ref,
@@ -350,7 +376,7 @@
     exp_scale = dim ** -0.5 * LOG2E
     loads[0].wait()
     loads[1].wait()
-    affine = [ref[...].reshape(1, ref.shape[0]) for ref in (gain1_ref, bias1_ref, gain2_ref, bias2_ref)]
+    affine = [ref[...].reshape(1, ref.shape[DIM0]) for ref in (gain1_ref, bias1_ref, gain2_ref, bias2_ref)]
 
     def norm_rows(i):
         at = tile_at(i, LN_ROWS)
@@ -358,7 +384,7 @@
             x_hat, _ = layer_norm_hat(src[at, :].astype(F32))
             dst[at, :] = (x_hat * affine[2 * row] + affine[2 * row + 1]).astype(BF16)
 
-    loop(x_ref.shape[0] // LN_ROWS, norm_rows)
+    loop(x_ref.shape[DIM0] // LN_ROWS, norm_rows)
     for copy in loads[2:]:
         copy.wait()
 
@@ -448,54 +474,55 @@
     place = Place()
     place.barrier()
     rows, model = dout_hbm.shape
-    hidden = w2v.shape[0]
+    hidden = w2v.shape[DIM0]
     scatter = Scatter(place, part, crecv, diag_recv, last_recv, *comm_sems[0:2])
     gather = ThirdGather(place, h2full, *comm_sems[2:4])
     gather.start('near', h2_ref)
     own_copy = pltpu.make_async_copy(h2_ref, h2full.at[place.me], own_sem)
 
+    half = rows // 2
+
+    def chunk_copies(i, copy):
+        return [copy(c, *place.chunk(i, c)) for c in range(4)]
+
     def load_pair(i):
-        return pltpu.make_async_copy(dfull.at[pl.ds(2 * place.pair_at(i), 2)], ybuf.at[i % 2], y_sem.at[i])
+        return chunk_copies(i, lambda c, slot, at: pltpu.make_async_copy(
+            dfull.at[slot, tile_at(at, half)], ybuf.at[i % 2, c], y_sem.at[i, c]))
+
+    def load_pre(i):
+        return chunk_copies(i, lambda c, slot, at: pltpu.make_async_copy(
+            z_ref.at[tile_at(2 * slot + at, half)], dzv.at[i, c], z_sem.at[i, c]))
 
     def store_grad(i):
-        at = tile_at(place.pair_at(i), 2 * rows)
-        return pltpu.make_async_copy(dzv.at[at], dz_ref.at[at], dz_sem.at[i])
-
-    def load_pre(i):
-        at = tile_at(place.pair_at(i), 2 * rows)
-        return pltpu.make_async_copy(z_ref.at[at], dzv.at[at], z_sem.at[i])
-
-    load_pair(0).start()
-    load_pre(0).start()
+        return chunk_copies(i, lambda c, slot, at: pltpu.make_async_copy(
+            dzv.at[i, c], dz_ref.at[tile_at(2 * slot + at, half)], dz_sem.at[i, c]))
+
+    start_all(load_pair(0) + load_pre(0))
     loads = start_copies(load_sem, (w2_ref, w2v), (w1_ref, w1v), (dout_hbm, dout_ref), (mid_hbm, mid_ref))
     for i in range(1, 4):
-        load_pre(i).start()
-    load_pair(1).start()
+        start_all(load_pre(i))
+    start_all(load_pair(1))
     own_copy.start()
     gb1_ref[...] = jnp.zeros_like(gb1_ref)
     vec_ref[...] = jnp.zeros_like(vec_ref)
     loads[0].wait()
 
     def pair_step(i):
-        slot = i % 2
-        pair = place.pair_at(i)
-        at = tile_at(pair, 2 * rows)
-        load_pair(i).wait()
-        load_pre(i).wait()
+        wait_all(load_pair(i) + load_pre(i))
 
         def grad_act(n):
             cols = tile_at(n, TILE)
-            acc = dot_t(ybuf[slot].reshape(2 * rows, model), w2v[cols, :])
-            grad = (acc * gelu_slope(dzv[at, cols].astype(F32))).astype(BF16)
-            dzv[at, cols] = grad
+            acc = dot_t(ybuf[i % 2].reshape(2 * rows, model), w2v[cols, :])
+            grad = (acc * gelu_slope(dzv[i, :, :, cols].reshape(2 * rows, TILE).astype(F32))).astype(BF16)
+            dzv[i, :, :, cols] = grad.reshape(4, half, TILE)
             gb1_ref[:, cols] += jnp.sum(grad.astype(F32), **COLS)
 
         loop(hidden // TILE, grad_act)
-        store_grad(i).start()
+        start_all(store_grad(i))
 
         @pl.when(i < 2)
         def _():
-            load_pair(i + 2).start()
+            start_all(load_pair(i + 2))
 
         @pl.when(i == 0)
         def _():
@@ -506,18 +533,19 @@
             gather.forward('near')
 
         scatter.between(i)
+
+        @pl.when(i == 3)
+        def _():
+            scatter.add_diag()
 
         def grad_norm(n):
             cols = tile_at(n, TILE)
-            acc = dot_t(dzv[at, :], w1v[cols, :]).astype(BF16)
-            part[2 * pair, :, cols] = acc[:rows]
-            part[2 * pair + 1, :, cols] = acc[rows:]
+            scatter.store(i, cols, dot_t(dzv[i].reshape(2 * rows, hidden), w1v[cols, :]).astype(BF16))
 
         loop(model // TILE, grad_norm)
         scatter.after(i)
 
     loop(4, pair_step)
-    scatter.add_diag()
 
     gain = gain_ref[...].reshape(1, model)
     loads[2].wait()
@@ -534,7 +562,7 @@
 
     scatter.norm_loop(norm_rows)
     for i in range(4):
-        store_grad(i).wait()
+        wait_all(store_grad(i))
     own_copy.wait()
     gather.wait_pair('near')
     gather.links.finish()
@@ -556,9 +584,9 @@
          shape(dfull.shape, BF16)],
         [VMEM, HBM, VMEM, VMEM, HBM],
         [pltpu.VMEM((hidden, model), BF16), pltpu.VMEM((model, hidden), BF16),
-         pltpu.VMEM((seq, hidden), BF16), pltpu.VMEM((2, 2, rows, model), BF16)]
+         pltpu.VMEM((4, 4, rows // 2, hidden), BF16), pltpu.VMEM((2, 4, rows // 2, model), BF16)]
         + scatter_scratch(rows, model) + [pltpu.VMEM((rows, model), BF16)] * 2
-        + [DMA((4,))] * 4 + [DMA(())] + [COMM] * 4)
+        + [DMA((4,))] + [DMA((4, 4))] * 3 + [DMA(())] + [COMM] * 4)
 
 
 def gelu(pre_act):
@@ -590,7 +618,7 @@
         tiles.put(n, lambda: dot(ut[...], flat_cols(yv, cols)))
 
     loads[0].wait()
-    loop(ut.shape[0] // 256, turn)
+    loop(ut.shape[DIM0] // 256, turn)
     gather.relay()
     loads[1].wait()
     loop(count, weight_tile)
@@ -626,7 +654,7 @@
 
 def ctx_call(dx1, w_rows, z_saved, dfull):
     rows, model = dx1.shape
-    feats = w_rows.shape[0]
+    feats = w_rows.shape[DIM0]
     seq, hidden = z_saved.shape
     return comm_call(
         ctx_kernel, "ctx_grads", 2, 30_000_000_000, (dx1, w_rows, z_saved, dfull), [VMEM] * 2 + [HBM] * 2,
@@ -688,7 +716,7 @@
                            for i, (src, dst) in enumerate(((dz_ref, dzv), (h2full, tok)))]
     for copy in loads:
         copy.wait()
-    count = tok.shape[2] // OUT_TILE
+    count = tok.shape[DIM2] // OUT_TILE
     tiles = Tiles(wbuf, dw1_ref, out_sem, rows=True)
 
     def fc1_tile(n):
@@ -730,7 +758,7 @@
     rows, model = h1.shape
     full = shape((seq // rows, rows, model), BF16)
     turned = pltpu.VMEM((seq, dim), BF16)
-    hidden = dz.shape[1]
+    hidden = dz.shape[DIM1]
     return comm_call(
         bwd_kernel, "attn_bwd", 3, 80_000_000_000,
         (h1, q_t, k_t, v_t, do_t, wide, row_max, row_inv, dz, h2full), [VMEM] + [HBM] * 5 + [VMEM] * 2 + [HBM] * 2,
@@ -776,8 +804,9 @@
     vec_send(0)
 
     def pair_step(i):
-        pair = place.pair_at(i)
-        turned[...] = qkv_ref[:, tile_at(pair, 2 * rows)].T
+        for c in range(4):
+            slot, at = place.chunk(i, c)
+            turned[tile_at(c, rows // 2), :] = qkv_ref[:, tile_at(2 * slot + at, rows // 2)].T
 
         @pl.when(i == 0)
         def _():
@@ -801,9 +830,7 @@
 
         def grad_norm(n):
             cols = tile_at(n, TILE)
-            acc = dot(turned[...], w_ref[:, cols]).astype(BF16)
-            part[2 * pair, :, cols] = acc[:rows]
-            part[2 * pair + 1, :, cols] = acc[rows:]
+            scatter.store(i, cols, dot(turned[...], w_ref[:, cols]).astype(BF16))
 
         loop(model // TILE, grad_norm)
         scatter.after(i)
@@ -825,8 +852,11 @@
     scatter.add_diag()
     gather.wait_pair('diag')
     loads[1].start()
-    ones = jnp.ones((8, qkv_ref.shape[1]), BF16)
-    bias_ref[...] = dot_t(ones, qkv_ref[...])
+    ones = jnp.ones((8, qkv_ref.shape[DIM1]), BF16)
+    kinds, heads, dim = bias_ref.shape
+    for row in range(kinds * heads):
+        feats = qkv_ref[row * dim:(row + 1) * dim, :]
+        bias_ref[row // heads, row % heads, :] = dot_t(ones, feats)[0]
     loads[1].wait()
     loop(count, qkv_tile)
     vec_step(3)
@@ -856,14 +886,14 @@
         links.finish()
 
 
-def qkv_call(qkv_rows, w_rows, dx1, x_in, gain, vec, ctx_rows, mfull, h1full):
+def qkv_call(heads, qkv_rows, w_rows, dx1, x_in, gain, vec, ctx_rows, mfull, h1full):
     rows, model = dx1.shape
     feats, seq = qkv_rows.shape
-    proj = ctx_rows.shape[0]
+    proj = ctx_rows.shape[DIM0]
     return comm_call(
         qkv_kernel, "qkv_grads", 4, 30_000_000_000,
         (qkv_rows, w_rows, dx1, x_in, gain, vec, ctx_rows, mfull, h1full), [HBM] * 4 + [VMEM] * 2 + [HBM] * 3,
-        [shape((rows, model), BF16), shape((6, model), F32), shape((8, feats), F32), shape((proj, model), F32),
+        [shape((rows, model), BF16), shape((6, model), F32), shape((3, heads, feats // (3 * heads)), F32), shape((proj, model), F32),
          shape((feats, model), F32), shape(h1full.shape, BF16)],
         [VMEM] * 3 + [HBM] * 3,
         [pltpu.VMEM((2 * rows, feats), BF16)] + scatter_scratch(rows, model)
@@ -877,16 +907,17 @@
 
 
 def finish_kernel(*refs):
-    count = (len(refs) - 8) // 2
-    rings, single, (small_sem, in_sem, out_sem) = refs[2 * count:2 * count + 2], refs[-6:-3], refs[-3:]
+    count = len(refs) // 3
+    refs[2 * count - 1][...] = refs[count - 1][...].reshape(refs[2 * count - 1].shape)
+    rings, single, (small_sem, in_sem, out_sem) = refs[2 * count:2 * count + 2], refs[2 * count + 2:-3], refs[-3:]
     chunks, used = [], [0, 0]
-    small = [(src, buf, dst) for src, buf, dst in zip(refs[4:count], single, refs[count + 4:2 * count])]
+    small = [(src, buf, dst) for src, buf, dst in zip(refs[4:count - 1], single, refs[count + 4:2 * count - 1])]
     for i, (src, buf, _) in enumerate(small):
         pltpu.make_async_copy(src, buf, small_sem.at[0, i]).start()
     for src, dst in zip(refs[:4], refs[count:count + 4]):
-        kind = 0 if src.shape[1] == rings[0].shape[2] else 1
-        rows = rings[kind].shape[1]
-        for row in range(0, src.shape[0], rows):
+        kind = 0 if src.shape[DIM1] == rings[0].shape[DIM2] else 1
+        rows = rings[kind].shape[DIM1]
+        for row in range(0, src.shape[DIM0], rows):
             chunks.append((src.at[pl.ds(row, rows)], dst.at[pl.ds(row, rows)], kind, used[kind]))
             used[kind] += 1
 
@@ -923,18 +954,18 @@
         pltpu.make_async_copy(buf, dst, small_sem.at[1, i]).wait()
 
 
-RING = 32
-AHEAD = 20
+RING = 8
+AHEAD = 12
 
 
 def finish_call(*arrays):
-    wide = max(a.shape[1] for a in arrays[:4])
-    narrow = min(a.shape[1] for a in arrays[:4])
-    small = [pltpu.VMEM(a.shape, a.dtype) for a in arrays[4:]]
+    wide = max(a.shape[DIM1] for a in arrays[:4])
+    narrow = min(a.shape[DIM1] for a in arrays[:4])
+    small = [pltpu.VMEM(a.shape, a.dtype) for a in arrays[4:-1]]
     return pl.pallas_call(
-        finish_kernel, name="finish", in_specs=[HBM] * len(arrays), out_specs=[HBM] * len(arrays),
-        out_shape=[shape(a.shape, a.dtype) for a in arrays],
-        scratch_shapes=[pltpu.VMEM((RING, 64, wide), F32), pltpu.VMEM((RING, 128, narrow), F32), *small,
+        finish_kernel, name="finish", in_specs=[HBM] * (len(arrays) - 1) + [VMEM], out_specs=[HBM] * (len(arrays) - 1) + [VMEM],
+        out_shape=[shape(a.shape, a.dtype) for a in arrays[:-1]] + [shape(arrays[-1].shape[1:], F32)],
+        scratch_shapes=[pltpu.VMEM((RING, 320, wide), F32), pltpu.VMEM((RING, 640, narrow), F32), *small,
                         DMA((2, len(small))), DMA((2, RING)), DMA((2, RING))],
         compiler_params=pltpu.CompilerParams(vmem_limit_bytes=66_000_000),
         cost_estimate=pl.CostEstimate(flops=1_000_000, bytes_accessed=72_000_000, transcendentals=0),
@@ -945,7 +976,7 @@
     def local_backward(x_in, x_mid, d_out, q_saved, k_saved, v_saved, z_saved, ln1_gain, ln1_bias, ln2_gain, ln2_bias, w_qkv, w_proj, w_fc1, w_fc2):
         x_in, x_mid, d_out, z_saved = x_in[0], x_mid[0], d_out[0], z_saved[0]
         heads, dim = q_saved.shape[2:]
-        seq, model = z_saved.shape[0], x_in.shape[1]
+        seq, model = z_saved.shape[DIM0], x_in.shape[DIM1]
         q_t, k_t, v_t = (v[0].transpose(1, 2, 0) for v in (q_saved, k_saved, v_saved))
         affine = (ln1_gain, ln1_bias, ln2_gain, ln2_bias)
         dfull, ctx_t, wide_t, row_max, row_inv, h1_local, h2_local = fwd_call(d_out, q_t, k_t, v_t, x_in, x_mid, affine)
@@ -955,14 +986,13 @@
             h1_local, q_t, k_t, v_t, do_t.reshape(heads, dim, seq), wide_t, row_max, row_inv, grad_pre, h2_full)
         qkv_rows = qkv_t.reshape(3 * heads * dim, seq)
         w_rows = w_qkv.transpose(0, 2, 3, 1).reshape(3 * heads * dim, model)
-        grad_x, grad_vecs, bias_rows, grad_wproj, grad_wqkv, _ = qkv_call(
-            qkv_rows, w_rows, dx1, x_in, ln1_gain, vec, ctx_t.reshape(heads * dim, seq), mfull, h1_full)
-        grad_wfc2, grad_wfc1, grad_wqkv, grad_wproj, grad_x, grad_vecs, grad_bfc1 = finish_call(
-            grad_wfc2, grad_wfc1, grad_wqkv, grad_wproj, grad_x, grad_vecs, grad_bfc1)
+        grad_x, grad_vecs, grad_bqkv, grad_wproj, grad_wqkv, _ = qkv_call(
+            heads, qkv_rows, w_rows, dx1, x_in, ln1_gain, vec, ctx_t.reshape(heads * dim, seq), mfull, h1_full)
+        grad_wfc2, grad_wfc1, grad_wqkv, grad_wproj, grad_x, grad_vecs, grad_bqkv, grad_bfc1 = finish_call(
+            grad_wfc2, grad_wfc1, grad_wqkv, grad_wproj, grad_x, grad_vecs, grad_bqkv, grad_bfc1)
         grad_wproj = grad_wproj.reshape(heads, dim, model)
         grad_wqkv = grad_wqkv.reshape(3, heads, dim, model).transpose(0, 3, 1, 2)
-        grad_bqkv = bias_rows[0].reshape(3, heads, dim)
-        return grad_x[None], grad_wqkv, grad_bqkv, grad_wproj, grad_wfc1, grad_bfc1[0], grad_wfc2, grad_vecs
+        return grad_x[None], grad_wqkv, grad_bqkv, grad_wproj, grad_wfc1, grad_bfc1, grad_wfc2, grad_vecs
 
     tok_spec = P('dp', 'tp', None)
     head_spec = P('dp', None, 'tp', None)

time: 350 us -> 340 us (0.971)
  Pallas kernels: 346 us -> 339 us
    pallas_call x5, Pallas kernels: 318 us -> 313 us  [comm_call(): pl.pallas_call(kernel, in_specs=in_specs, out_specs=out_specs, out_shape=...]
where the time goes in v7:
time: 340 us
  Pallas kernels  339 us (100%)
    pallas_call x5, Pallas kernels, comm_call(): pl.pallas_call(kernel, in_specs=in_specs, out_specs=out_specs, out_shape=...  313 us
    pallas_call x1, Pallas kernels, finish_call(): pl.pallas_call(finish_kernel, name='finish', in_specs=[HBM] * (len(arrays...  26.3 us

profile of v7, /device:TPU:0, one launch (start us, length us, event | category | flops | bytes accessed | tf_op | source)
XLA Modules:
  0.0 340.0 jit_solution(2341030647140167875)
XLA Ops:
  0.6 54.5 %attn_fwd.1 = (bf16[8,256,2560]{2,1,0:T(8,128)(2,1)}, bf16[4,80,2048]{2,1,0:T(8,128)(2,1)}, f32[4,80,2048]{2,1,0:T(8,128)}, f32[4,1,2048]{2,1,0:T(1,128)}, f32[4...) custom-call(bf16[256,2560]{1,0:T(8,128)(2,1)} %bitcast.31, bf16[4,80,2048]{2,1,0:T(8,128)(2,1)} %bitcast.35, ...), custom_call_target="tpu_custom_call" | custom-call | flops 40000000000 | bytes 40000000 | tf_op jit(solution)/shard_map/attn_fwd/pallas_call | solution.py:327
  55.1 69.0 %mlp_grads.1 = (bf16[256,2560]{1,0:T(8,128)(2,1)}, bf16[2048,1280]{1,0:T(8,128)(2,1)}, f32[1,1280]{1,0:T(1,128)}, f32[8,2560]{1,0:T(8,128)}, bf16[8,256,2560]{2,1,0:T(8,128)(2,1)}) custom-call(bf16[8,256,2560]{2,1,0:T(8,128)(2,1)} %get-tuple-element.39.dfull, bf16[256,2560]{1,0:T(8,128)(2,1)} %bitcast.32, bf16[256,2560]{1,0:T(8,128)(2,1)} %bitcast.34, ...), custom_call_target="tpu_custom_call" | custom-call | flops 60000002048 | bytes 60000000 | tf_op jit(solution)/shard_map/mlp_grads/pallas_call | solution.py:327
  124.1 51.8 %ctx_grads.1 = (bf16[8,256,2560]{2,1,0:T(8,128)(2,1)}, bf16[320,2048]{1,0:T(8,128)(2,1)}, f32[1280,2560]{1,0:T(8,128)}) custom-call(bf16[256,2560]{1,0:T(8,128)(2,1)} %get-tuple-element.41.dx1_ref.dx1_hbm, bf16[320,2560]{1,0:T(8,128)(2,1)} %bitcast.30, bf16[2048,1280]{1,0:T(8,128)(2,1)} %bitcast.27, bf16[8,256,2560]{2,1,0:T(8,128)(2,1)} %get-tuple-element.39.dfull), custom_call_target="tpu_custom_call" | custom-call | flops 30000001024 | bytes 30000000 | tf_op jit(solution)/shard_map/ctx_grads/pallas_call | solution.py:327
  175.9 68.2 %attn_bwd.1 = (bf16[8,256,2560]{2,1,0:T(8,128)(2,1)}, bf16[8,256,2560]{2,1,0:T(8,128)(2,1)}, bf16[3,4,80,2048]{3,2,1,0:T(8,128)(2,1)}, f32[2560,1280]{1,0:T(8,128)}) custom-call(bf16[256,2560]{1,0:T(8,128)(2,1)} %get-tuple-element.43.h1_ref, bf16[4,80,2048]{2,1,0:T(8,128)(2,1)} %bitcast.36, ...), custom_call_target="tpu_custom_call", output_to_operand_aliasing={{0}: (9, {})} | custom-call | flops 80000000000 | bytes 80000000 | tf_op jit(solution)/shard_map/attn_bwd/pallas_call | solution.py:327
  244.2 69.4 %qkv_grads.1 = (bf16[256,2560]{1,0:T(8,128)(2,1)}, f32[6,2560]{1,0:T(8,128)}, f32[3,4,80]{2,1,0:T(4,128)}, f32[320,2560]{1,0:T(8,128)}, f32[960,2560]{1,0:T(8,128)}, /*index=5*/bf16[8,256,2560]{2,1,0:T(8,128)(2,1)}) custom-call(bf16[960,2048]{1,0:T(8,128)(2,1)} %bitcast.44, bf16[960,2560]{1,0:T(8,128)(2,1)} %bitcast.28, ...), custom_call_target="tpu_custom_call", output_to_operand_aliasing={{5}: (8, {})} | custom-call | flops 30000001024 | bytes 30000000 | tf_op jit(solution)/shard_map/qkv_grads/pallas_call | solution.py:327
  313.6 26.3 %finish.1 = (f32[1280,2560]{1,0:T(8,128)}, f32[2560,1280]{1,0:T(8,128)}, f32[960,2560]{1,0:T(8,128)}, f32[320,2560]{1,0:T(8,128)}, bf16[256,2560]{1,0:T(8,128)(2...) custom-call(f32[1280,2560]{1,0:T(8,128)} %get-tuple-element.42.refs_0_, ...), custom_call_target="tpu_custom_call" | custom-call | flops 1000000 | bytes 72000000 | tf_op jit(solution)/shard_map/finish/pallas_call | solution.py:965

commit v8 on v7

--- a/solution.py
+++ b/solution.py
@@ -363,8 +363,9 @@
 
 
 def fwd_kernel(dout_ref, q_hbm, k_hbm, v_hbm, x_hbm, mid_hbm, gain1_ref, bias1_ref, gain2_ref, bias2_ref,
-               dfull, ctx_ref, wide_ref, max_ref, inv_ref, h1_ref, h2_ref,
-               k_rows, strip, q_ref, k_ref, v_ref, x_ref, mid_ref, own_sem, load_sem, *comm_sems):
+               dfull, ctx_out, wide_out, max_ref, inv_ref, h1_out, h2_out,
+               k_rows, strip, q_ref, k_ref, v_ref, ctx_ref, x_ref, mid_ref, h1_ref, h2_ref, wide_ref,
+               own_sem, load_sem, *comm_sems):
     place = Place()
     place.barrier()
     gather = Gather(place, dout_ref, dfull, *comm_sems)
@@ -445,8 +446,10 @@
 
     loop(heads, head_step)
     gather.forward('D')
+    results = start_copies(load_sem, (ctx_ref, ctx_out), (wide_ref, wide_out), (h1_ref, h1_out), (h2_ref, h2_out))
     gather.links.wait('CO', 'CX', 'CY', 'CD')
     own_copy.wait()
+    wait_all(results)
     gather.links.finish()
 
 
@@ -458,9 +461,9 @@
         [VMEM] + [HBM] * 5 + [VMEM] * 4,
         [shape((seq // rows, rows, model), BF16), shape((heads, dim, seq), BF16), shape((heads, dim, seq), F32),
          shape((heads, 1, seq), F32), shape((heads, 1, seq), F32), shape((rows, model), BF16), shape((rows, model), BF16)],
-        [HBM] + [VMEM] * 6,
-        [pltpu.VMEM((seq, dim), BF16), pltpu.VMEM((seq, BLK), F32)] + [pltpu.VMEM(q_t.shape, BF16)] * 3
-        + [pltpu.VMEM((rows, model), BF16)] * 2 + [DMA(()), DMA((5,))] + [COMM] * 2)
+        [HBM] * 3 + [VMEM] * 2 + [HBM] * 2,
+        [pltpu.VMEM((seq, dim), BF16), pltpu.VMEM((seq, BLK), F32)] + [pltpu.VMEM(q_t.shape, BF16)] * 4
+        + [pltpu.VMEM((rows, model), BF16)] * 4 + [pltpu.VMEM(q_t.shape, F32)] + [DMA(()), DMA((5,))] + [COMM] * 2)
 
 
 def dot_t(a, b):
@@ -665,9 +668,9 @@
 
 
 def bwd_kernel(h1_ref, q_hbm, k_hbm, v_hbm, do_hbm, wide_hbm, max_ref, inv_ref, dz_ref, h2_in,
-               h2full, h1full, out_ref, dw1_ref,
+               h2full, h1full, qkv_out, dw1_ref,
                k_rows, v_rows, q_rows, do_rows, delta, dq_acc, dk_acc, dv_acc, tok, dzv, wbuf,
-               q_ref, k_ref, v_ref, do_ref, wide_ref, own_sem, head_sem, load_sem, out_sem, *comm_sems):
+               q_ref, k_ref, v_ref, do_ref, wide_ref, out_ref, own_sem, head_sem, load_sem, out_sem, *comm_sems):
     place = Place()
     place.barrier()
     gather1 = ThirdGather(place, h1full, *comm_sems[0:2])
@@ -742,12 +745,14 @@
     head(heads - 1)
     load_grad.wait()
     load_tok.wait()
+    results = start_copies(head_sem, (out_ref, qkv_out))
     loop(count, fc1_tile)
     for third in ('near', 'rest'):
         gather1.forward(third)
     for third in ('near', 'rest'):
         gather1.wait_pair(third)
     own_copy.wait()
+    wait_all(results)
     tiles.finish(count)
     gather1.links.finish()
     gather2.links.finish()
@@ -762,11 +767,11 @@
     return comm_call(
         bwd_kernel, "attn_bwd", 3, 80_000_000_000,
         (h1, q_t, k_t, v_t, do_t, wide, row_max, row_inv, dz, h2full), [VMEM] + [HBM] * 5 + [VMEM] * 2 + [HBM] * 2,
-        [full, full, shape((3, heads, dim, seq), BF16), shape((model, hidden), F32)], [HBM, HBM, VMEM, HBM],
+        [full, full, shape((3, heads, dim, seq), BF16), shape((model, hidden), F32)], [HBM] * 4,
         [turned] * 4 + [pltpu.VMEM((1, seq), F32), pltpu.VMEM((dim, seq), F32), pltpu.VMEM((seq, dim), F32),
                         pltpu.VMEM((seq, dim), F32), pltpu.VMEM((seq // rows, rows, model), BF16),
                         pltpu.VMEM((seq, hidden), BF16), pltpu.VMEM((2, OUT_TILE, hidden), F32),
-                        *[pltpu.VMEM(q_t.shape, BF16)] * 4, pltpu.VMEM(wide.shape, F32),
+                        *[pltpu.VMEM(q_t.shape, BF16)] * 4, pltpu.VMEM(wide.shape, F32), pltpu.VMEM((3, heads, dim, seq), BF16),
                         DMA(()), DMA((5,)), PAIR, PAIR] + [COMM] * 4,
         aliases={9: 0})
 

time: 340 us -> 337 us (level)
  Pallas kernels: 339 us -> 335 us
    pallas_call x5, Pallas kernels: 313 us -> 309 us  [comm_call(): pl.pallas_call(kernel, in_specs=in_specs, out_specs=out_specs, out_shape=...]
where the time goes in v8:
time: 337 us; the launch traced here: 336 us
  Pallas kernels  335 us (99%)
    pallas_call x5, Pallas kernels, comm_call(): pl.pallas_call(kernel, in_specs=in_specs, out_specs=out_specs, out_shape=...  309 us
    pallas_call x1, Pallas kernels, finish_call(): pl.pallas_call(finish_kernel, name='finish', in_specs=[HBM] * (len(arrays...  26.3 us

profile of v8, /device:TPU:0, one launch (start us, length us, event | category | flops | bytes accessed | tf_op | source)
XLA Modules:
  0.0 336.1 jit_solution(1470521615636508883)
XLA Ops:
  0.6 52.4 %attn_fwd.1 = (bf16[8,256,2560]{2,1,0:T(8,128)(2,1)}, bf16[4,80,2048]{2,1,0:T(8,128)(2,1)}, f32[4,80,2048]{2,1,0:T(8,128)}, f32[4,1,2048]{2,1,0:T(1,128)}, f32[4...) custom-call(bf16[256,2560]{1,0:T(8,128)(2,1)} %bitcast.31, bf16[4,80,2048]{2,1,0:T(8,128)(2,1)} %bitcast.35, ...), custom_call_target="tpu_custom_call" | custom-call | flops 40000000000 | bytes 40000000 | tf_op jit(solution)/shard_map/attn_fwd/pallas_call | solution.py:327
  53.1 68.9 %mlp_grads.1 = (bf16[256,2560]{1,0:T(8,128)(2,1)}, bf16[2048,1280]{1,0:T(8,128)(2,1)}, f32[1,1280]{1,0:T(1,128)}, f32[8,2560]{1,0:T(8,128)}, bf16[8,256,2560]{2,1,0:T(8,128)(2,1)}) custom-call(bf16[8,256,2560]{2,1,0:T(8,128)(2,1)} %get-tuple-element.39.dfull, bf16[256,2560]{1,0:T(8,128)(2,1)} %bitcast.32, bf16[256,2560]{1,0:T(8,128)(2,1)} %bitcast.34, ...), custom_call_target="tpu_custom_call" | custom-call | flops 60000002048 | bytes 60000000 | tf_op jit(solution)/shard_map/mlp_grads/pallas_call | solution.py:327
  122.0 51.9 %ctx_grads.1 = (bf16[8,256,2560]{2,1,0:T(8,128)(2,1)}, bf16[320,2048]{1,0:T(8,128)(2,1)}, f32[1280,2560]{1,0:T(8,128)}) custom-call(bf16[256,2560]{1,0:T(8,128)(2,1)} %get-tuple-element.41.dx1_ref.dx1_hbm, bf16[320,2560]{1,0:T(8,128)(2,1)} %bitcast.30, bf16[2048,1280]{1,0:T(8,128)(2,1)} %bitcast.27, bf16[8,256,2560]{2,1,0:T(8,128)(2,1)} %get-tuple-element.39.dfull), custom_call_target="tpu_custom_call" | custom-call | flops 30000001024 | bytes 30000000 | tf_op jit(solution)/shard_map/ctx_grads/pallas_call | solution.py:327
  173.9 66.3 %attn_bwd.1 = (bf16[8,256,2560]{2,1,0:T(8,128)(2,1)}, bf16[8,256,2560]{2,1,0:T(8,128)(2,1)}, bf16[3,4,80,2048]{3,2,1,0:T(8,128)(2,1)}, f32[2560,1280]{1,0:T(8,128)}) custom-call(bf16[256,2560]{1,0:T(8,128)(2,1)} %get-tuple-element.43.h1_ref, bf16[4,80,2048]{2,1,0:T(8,128)(2,1)} %bitcast.36, ...), custom_call_target="tpu_custom_call", output_to_operand_aliasing={{0}: (9, {})} | custom-call | flops 80000000000 | bytes 80000000 | tf_op jit(solution)/shard_map/attn_bwd/pallas_call | solution.py:327
  240.2 69.4 %qkv_grads.1 = (bf16[256,2560]{1,0:T(8,128)(2,1)}, f32[6,2560]{1,0:T(8,128)}, f32[3,4,80]{2,1,0:T(4,128)}, f32[320,2560]{1,0:T(8,128)}, f32[960,2560]{1,0:T(8,128)}, /*index=5*/bf16[8,256,2560]{2,1,0:T(8,128)(2,1)}) custom-call(bf16[960,2048]{1,0:T(8,128)(2,1)} %bitcast.44, bf16[960,2560]{1,0:T(8,128)(2,1)} %bitcast.28, ...), custom_call_target="tpu_custom_call", output_to_operand_aliasing={{5}: (8, {})} | custom-call | flops 30000001024 | bytes 30000000 | tf_op jit(solution)/shard_map/qkv_grads/pallas_call | solution.py:327
  309.6 26.3 %finish.1 = (f32[1280,2560]{1,0:T(8,128)}, f32[2560,1280]{1,0:T(8,128)}, f32[960,2560]{1,0:T(8,128)}, f32[320,2560]{1,0:T(8,128)}, bf16[256,2560]{1,0:T(8,128)(2...) custom-call(f32[1280,2560]{1,0:T(8,128)} %get-tuple-element.42.refs_0_, ...), custom_call_target="tpu_custom_call" | custom-call | flops 1000000 | bytes 72000000 | tf_op jit(solution)/shard_map/finish/pallas_call | solution.py:970

commit v9 on v8

--- a/solution.py
+++ b/solution.py
@@ -959,8 +959,8 @@
         pltpu.make_async_copy(buf, dst, small_sem.at[1, i]).wait()
 
 
-RING = 8
-AHEAD = 12
+RING = 16
+AHEAD = 24
 
 
 def finish_call(*arrays):
@@ -970,7 +970,7 @@
     return pl.pallas_call(
         finish_kernel, name="finish", in_specs=[HBM] * (len(arrays) - 1) + [VMEM], out_specs=[HBM] * (len(arrays) - 1) + [VMEM],
         out_shape=[shape(a.shape, a.dtype) for a in arrays[:-1]] + [shape(arrays[-1].shape[1:], F32)],
-        scratch_shapes=[pltpu.VMEM((RING, 320, wide), F32), pltpu.VMEM((RING, 640, narrow), F32), *small,
+        scratch_shapes=[pltpu.VMEM((RING, 160, wide), F32), pltpu.VMEM((RING, 320, narrow), F32), *small,
                         DMA((2, len(small))), DMA((2, RING)), DMA((2, RING))],
         compiler_params=pltpu.CompilerParams(vmem_limit_bytes=66_000_000),
         cost_estimate=pl.CostEstimate(flops=1_000_000, bytes_accessed=72_000_000, transcendentals=0),

time: 337 us -> 337 us (level)
  no operation moved by 1% of the time
where the time goes in v9:
time: 337 us; the launch traced here: 336 us
  Pallas kernels  335 us (99%)
    pallas_call x5, Pallas kernels, comm_call(): pl.pallas_call(kernel, in_specs=in_specs, out_specs=out_specs, out_shape=...  309 us
    pallas_call x1, Pallas kernels, finish_call(): pl.pallas_call(finish_kernel, name='finish', in_specs=[HBM] * (len(arrays...  26.4 us

profile of v9, /device:TPU:0, one launch (start us, length us, event | category | flops | bytes accessed | tf_op | source)
XLA Modules:
  0.0 336.2 jit_solution(54124482228344919)
XLA Ops:
  0.6 52.4 %attn_fwd.1 = (bf16[8,256,2560]{2,1,0:T(8,128)(2,1)}, bf16[4,80,2048]{2,1,0:T(8,128)(2,1)}, f32[4,80,2048]{2,1,0:T(8,128)}, f32[4,1,2048]{2,1,0:T(1,128)}, f32[4...) custom-call(bf16[256,2560]{1,0:T(8,128)(2,1)} %bitcast.31, bf16[4,80,2048]{2,1,0:T(8,128)(2,1)} %bitcast.35, ...), custom_call_target="tpu_custom_call" | custom-call | flops 40000000000 | bytes 40000000 | tf_op jit(solution)/shard_map/attn_fwd/pallas_call | solution.py:327
  53.1 68.9 %mlp_grads.1 = (bf16[256,2560]{1,0:T(8,128)(2,1)}, bf16[2048,1280]{1,0:T(8,128)(2,1)}, f32[1,1280]{1,0:T(1,128)}, f32[8,2560]{1,0:T(8,128)}, bf16[8,256,2560]{2,1,0:T(8,128)(2,1)}) custom-call(bf16[8,256,2560]{2,1,0:T(8,128)(2,1)} %get-tuple-element.39.dfull, bf16[256,2560]{1,0:T(8,128)(2,1)} %bitcast.32, bf16[256,2560]{1,0:T(8,128)(2,1)} %bitcast.34, ...), custom_call_target="tpu_custom_call" | custom-call | flops 60000002048 | bytes 60000000 | tf_op jit(solution)/shard_map/mlp_grads/pallas_call | solution.py:327
  122.0 51.9 %ctx_grads.1 = (bf16[8,256,2560]{2,1,0:T(8,128)(2,1)}, bf16[320,2048]{1,0:T(8,128)(2,1)}, f32[1280,2560]{1,0:T(8,128)}) custom-call(bf16[256,2560]{1,0:T(8,128)(2,1)} %get-tuple-element.41.dx1_ref.dx1_hbm, bf16[320,2560]{1,0:T(8,128)(2,1)} %bitcast.30, bf16[2048,1280]{1,0:T(8,128)(2,1)} %bitcast.27, bf16[8,256,2560]{2,1,0:T(8,128)(2,1)} %get-tuple-element.39.dfull), custom_call_target="tpu_custom_call" | custom-call | flops 30000001024 | bytes 30000000 | tf_op jit(solution)/shard_map/ctx_grads/pallas_call | solution.py:327
  173.9 66.3 %attn_bwd.1 = (bf16[8,256,2560]{2,1,0:T(8,128)(2,1)}, bf16[8,256,2560]{2,1,0:T(8,128)(2,1)}, bf16[3,4,80,2048]{3,2,1,0:T(8,128)(2,1)}, f32[2560,1280]{1,0:T(8,128)}) custom-call(bf16[256,2560]{1,0:T(8,128)(2,1)} %get-tuple-element.43.h1_ref, bf16[4,80,2048]{2,1,0:T(8,128)(2,1)} %bitcast.36, ...), custom_call_target="tpu_custom_call", output_to_operand_aliasing={{0}: (9, {})} | custom-call | flops 80000000000 | bytes 80000000 | tf_op jit(solution)/shard_map/attn_bwd/pallas_call | solution.py:327
  240.2 69.4 %qkv_grads.1 = (bf16[256,2560]{1,0:T(8,128)(2,1)}, f32[6,2560]{1,0:T(8,128)}, f32[3,4,80]{2,1,0:T(4,128)}, f32[320,2560]{1,0:T(8,128)}, f32[960,2560]{1,0:T(8,128)}, /*index=5*/bf16[8,256,2560]{2,1,0:T(8,128)(2,1)}) custom-call(bf16[960,2048]{1,0:T(8,128)(2,1)} %bitcast.44, bf16[960,2560]{1,0:T(8,128)(2,1)} %bitcast.28, ...), custom_call_target="tpu_custom_call", output_to_operand_aliasing={{5}: (8, {})} | custom-call | flops 30000001024 | bytes 30000000 | tf_op jit(solution)/shard_map/qkv_grads/pallas_call | solution.py:327
  309.6 26.4 %finish.1 = (f32[1280,2560]{1,0:T(8,128)}, f32[2560,1280]{1,0:T(8,128)}, f32[960,2560]{1,0:T(8,128)}, f32[320,2560]{1,0:T(8,128)}, bf16[256,2560]{1,0:T(8,128)(2...) custom-call(f32[1280,2560]{1,0:T(8,128)} %get-tuple-element.42.refs_0_, ...), custom_call_target="tpu_custom_call" | custom-call | flops 1000000 | bytes 72000000 | tf_op jit(solution)/shard_map/finish/pallas_call | solution.py:970
